TPU v7x, 256 devices: a whole 4x4x8 slice. The times are simulated.
256 devices in a mesh: tile: 128 (over y, x, z), rhs: 2 (over core).
Axes of the slice: x: 4, y: 4, z: 8, core: 2. Of those that a mesh axis runs over, the one named last changes fastest.
Arguments:
- sensitivity: bfloat16 [131072, 5120], P('tile', 'rhs'), may hold values from -0.0625 to 0.0625
- precision: float32 [5120], P('rhs'), may hold values from 3 to 60
- reaction: float32 [1024, 128], P('tile'), may hold values from 0.25 to 2
- load: float32 [64, 131072], P(None, 'tile'), may hold values from -24 to 24
Outputs:
- solution: float32 [64, 131072], P(None, 'tile')
- residual: float32 [64, 131072], P(None, 'tile')
All inputs are finite; a program needn't handle non-finite values.
Results may differ from a plain program's by a relative error of at most 0.0042.
Values may be sent and summed in bfloat16 or wider, within the bound.
No kernel may reach another device: no remote copies, remote signals or barrier semaphores. Data moves between devices by JAX's collectives and lax.ppermute only.
A program may use at most 64 MiB of HBM per device.

v0:
```python
import jax
import jax.numpy as jnp
from jax import lax
from jax.sharding import Mesh
from jax.sharding import PartitionSpec as P

ITERS = 2
TILE = ("tile_0", "tile_1", "tile_2")


def sent_to_all(array, axis):
    peers = lax.axis_size(axis)
    return lax.all_to_all(
        jnp.broadcast_to(array[None], (peers, *array.shape)), axis, 0, 0, tiled=True
    )


def over_copies(array, axis):
    return sent_to_all(array, axis).sum(axis=0)


def one_axis_at_a_time(array, axes):
    far, near = axes
    return over_copies(over_copies(array, near), far)


def packed_total(arrays, axis):
    vector, at, finished = (jnp.concatenate([a.reshape(-1) for a in arrays]), 0, [])
    running = one_axis_at_a_time(vector, axis)
    for a in arrays:
        finished.append(running[at : at + a.size].reshape(a.shape))
        at += a.size
    return tuple(finished)


def with_halo(block, sides, width):
    for axis, dim in sides:
        count = lax.axis_size(axis)
        forward = [(i, i + 1) for i in range(count - 1)]
        backward = [(target, source) for source, target in forward]
        low = lax.ppermute(
            lax.slice_in_dim(block, block.shape[dim] - width, None, axis=dim), axis, forward
        )
        high = lax.ppermute(lax.slice_in_dim(block, 0, width, axis=dim), axis, backward)
        block = jnp.concatenate([low, block, high], axis=dim)
    return block


def filled_up(lines, peers):
    spare = -len(lines) % peers
    return jnp.pad(lines, [(0, spare)] + [(0, 0)] * (lines.ndim - 1))


def joined_along(tiles, dim):
    shape = list(tiles.shape[1:])
    shape[dim] *= tiles.shape[0]
    return jnp.moveaxis(tiles, 0, dim).reshape(shape)


def whole_of(array, axes, dim):
    far, near = axes
    tiles = sent_to_all(sent_to_all(array, far), near)
    return joined_along(tiles.swapaxes(0, 1).reshape(-1, *array.shape), dim)


def split_up(array, dim, peers):
    before, after = (array.shape[:dim], array.shape[dim + 1 :])
    return jnp.moveaxis(array.reshape(*before, peers, -1, *after), dim, 0)


def sent_and_summed(array, axis, dim):
    peers = lax.axis_size(axis)
    tiles = lax.all_to_all(split_up(array, dim, peers), axis, 0, 0, tiled=True)
    return jnp.sum(tiles, axis=0)


def sum_by_axis(array, axes, dim):
    far, near = axes
    own = sent_and_summed(split_up(array, dim, lax.axis_size(far)), near, dim + 1)
    return jnp.sum(lax.all_to_all(own, far, 0, 0, tiled=True), axis=0)


def nested_sum(array, axes):
    lines = array.reshape(-1)
    padded = filled_up(lines, lax.axis_size(axes[0]) * lax.axis_size(axes[1]))
    whole = whole_of(sum_by_axis(padded, axes, 0), axes, 0)
    return lax.slice_in_dim(whole, 0, len(lines)).reshape(array.shape)


def stencil_rows(padded_field, reaction):
    sided = jnp.pad(padded_field, ((0, 0), (0, 0), (1, 1)))
    center = padded_field[:, 1:-1, :]
    neighbours = (
        padded_field[:, 2:, :] + padded_field[:, :-2, :] + sided[:, 1:-1, 2:] + sided[:, 1:-1, :-2]
    )
    return (reaction + 4.0) * center - neighbours


def joint_products(direction, residual, image):
    return packed_total(
        (
            jnp.sum(residual * residual, axis=1),
            jnp.sum(direction * image, axis=1),
            jnp.sum(residual * image, axis=1),
            jnp.sum(image * image, axis=1),
        ),
        ("tile_0", ("tile_1", "tile_2")),
    )


def per_device(sensitivity, precision, reaction, load):
    count_rhs = load.shape[0]
    strip_rows = reaction.shape[0]
    columns = reaction.shape[1]
    strip_index = lax.axis_index(TILE)
    strip_count = lax.axis_size(TILE)
    reaction_deep = with_halo(reaction, ((TILE, 0),), 1)
    positions = jnp.arange(strip_rows + 2)
    inside = jnp.logical_and(
        jnp.logical_or(positions > 0, strip_index > 0),
        jnp.logical_or(positions < strip_rows + 1, strip_index < strip_count - 1),
    )
    inside_mask = inside.astype(jnp.float32)[None, :, None]
    solution = jnp.zeros_like(load)
    residual = load
    direction = load
    current = None
    for iteration in range(ITERS):
        grid = direction.reshape(count_rhs, strip_rows, columns)
        widened = with_halo(grid, ((TILE, 1),), 2)
        once = stencil_rows(widened, reaction_deep) * inside_mask
        twice = stencil_rows(once, reaction)
        lowered = direction.astype(jnp.bfloat16)
        partial_obs = jnp.dot(lowered, sensitivity, preferred_element_type=jnp.float32)
        whole = nested_sum(partial_obs, ("tile_0", ("tile_1", "tile_2")))
        weighted = (precision[None, :] * whole).astype(jnp.bfloat16)
        back_half = lax.dot_general(
            weighted, sensitivity, (((1,), (1,)), ((), ())), preferred_element_type=jnp.float32
        )
        image = over_copies(back_half, "rhs") + twice.reshape(direction.shape)
        squared, curved, cross, image_sq = joint_products(direction, residual, image)
        if iteration == 0:
            current = squared
        alpha = current / curved
        solution = solution + alpha[:, None] * direction
        residual = residual - alpha[:, None] * image
        if iteration + 1 < ITERS:
            fresh = current - 2.0 * alpha * cross + alpha * alpha * image_sq
            direction = residual + (fresh / current)[:, None] * direction
            current = fresh
    return (solution, residual)


def solution(mesh):
    torus = Mesh(
        mesh.devices.reshape(4, 4, 8, mesh.shape["rhs"]), ("tile_0", "tile_1", "tile_2", "rhs")
    )
    placed = (P(TILE, "rhs"), P("rhs"), P(TILE, None), P(None, TILE))
    return jax.shard_map(
        per_device,
        mesh=torus,
        in_specs=placed,
        out_specs=(P(None, TILE), P(None, TILE)),
        check_vma=False,
    )
```

profile of v0, /device:TPU:1, one launch (start us, length us, event | category | flops | bytes accessed | tf_op | source)
XLA Modules:
  0.0 213.5 jit_solution(1272202076202806200)
XLA Ops:
  0.6 3.6 %fusion.24 = f32[64,2560]{1,0:T(8,128)S(1)} fusion(bf16[1024,2560]{1,0:T(8,128)(2,1)} %param.4, f32[64,1024]{1,0:T(8,128)} %param.7), kind=kOutput, calls=%fused_computation.59 | convolution fusion | flops 335609856 | bytes 6160384 | tf_op jit(solution)/shard_map/dot_general | solution.py:134
  4.8 28.7 %all_to_all.84 = f32[32,4,1280]{2,1,0:T(4,128)S(1)} all-to-all(f32[32,4,1280]{2,1,0:T(4,128)S(1)} %bitcast.65), channel_id=1, replica_groups=mesh['tile_0'=4,'tile_1'=4,'tile_2'=8,'rhs'=2] {'tile_1','tile_2'}, dimensions={0} | all-to-all | bytes 1310720 | tf_op jit(solution)/shard_map/all_to_all | solution.py:73
  33.7 8.2 %all_to_all.85 = f32[4,1,1280]{2,1,0:T(1,128)S(1)} all-to-all(f32[4,1,1280]{2,1,0:T(1,128)S(1)} %all_to_all.55), channel_id=1, replica_groups=mesh['tile_0'=4,'tile_1'=4,'tile_2'=8,'rhs'=2] {'tile_0'}, dimensions={0} | all-to-all | bytes 40960 | tf_op jit(solution)/shard_map/all_to_all | solution.py:80
  42.0 6.6 %all_to_all.86 = f32[4,1,1280]{2,1,0:T(1,128)S(1)} all-to-all(f32[4,1,1280]{2,1,0:T(1,128)S(1)} %broadcast_in_dim.24), channel_id=1, replica_groups=mesh['tile_0'=4,'tile_1'=4,'tile_2'=8,'rhs'=2] {'tile_0'}, dimensions={0} | all-to-all | bytes 40960 | tf_op jit(solution)/shard_map/all_to_all | solution.py:13
  49.5 7.7 %all-to-all-start.3 = ((f32[32,4,1280]{2,1,0:T(4,128)}), f32[32,4,1280]{2,1,0:T(4,128)S(1)}, u32[]{:S(2)}, u32[]{:S(2)}) async-start(f32[32,4,1280]{2,1,0:T(4,128)} %broadcast_in_dim.26), calls=%async_computation.3 | async-start | bytes 1310720 | tf_op jit(solution)/shard_map/all_to_all | solution.py:13
  57.2 3.1 %collective-permute-start = (f32[1,128]{1,0:T(1,128)S(1)}, f32[1,128]{1,0:T(1,128)S(1)}, u32[]{:S(2)}, u32[]{:S(2)}) collective-permute-start(f32[1,128]{1,0:T(1,128)S(1)} %get-tuple-element.20), channel_id=1, source_target_pairs={{0,2},{2,4},{4,6},{6,8},{8,10},{10,12},{12,14},{14,16},{16,18},{18... | collective-permute-start | bytes 1544 | tf_op jit(solution)/shard_map/ppermute | solution.py:41
  61.8 4.0 %collective-permute-start.2 = (f32[64,2,128]{2,1,0:T(2,128)S(1)}, f32[64,2,128]{2,1,0:T(2,128)S(1)}, u32[]{:S(2)}, u32[]{:S(2)}) collective-permute-start(f32[64,2,128]{2,1,0:T(2,128)S(1)} %get-tuple-element.18), channel_id=1, source_target_pairs={{0,2},{2,4},{4,6},{6,8},{8,10},{10,12},{12,14},{14,16},{16,18},{18... | collective-permute-start | bytes 196616 | tf_op jit(solution)/shard_map/ppermute | solution.py:41
  68.7 3.9 %collective-permute-done.3 = f32[64,2,128]{2,1,0:T(2,128)S(1)} collective-permute-done((f32[64,2,128]{2,1,0:T(2,128)S(1)}, f32[64,2,128]{2,1,0:T(2,128)S(1)}, u32[]{:S(2)}, u32[]{:S(2)}) %collective-permute-start.3) | collective-permute-done | bytes 65568 | tf_op jit(solution)/shard_map/ppermute | solution.py:44
  73.5 4.2 %fusion.8 = f32[64,1024]{1,0:T(8,128)S(1)} fusion(bf16[1024,2560]{1,0:T(8,128)(2,1)} %param.4, f32[64,2560]{1,0:T(8,128)S(1)} %reshape_reshape_reshape.6, f32[2560]{0:T(1024)S(1)} %copy-done.1), kind=kOutput, calls=%fused_computation.26 | convolution fusion | flops 335872000 | bytes 6170624 | tf_op jit(solution)/shard_map/dot_general | solution.py:137
  77.7 8.7 %all_to_all.87 = f32[2,64,1024]{2,1,0:T(8,128)S(1)} all-to-all(f32[2,64,1024]{2,1,0:T(8,128)S(1)} %broadcast_in_dim.27), channel_id=1, replica_groups=mesh['tile_0'=4,'tile_1'=4,'tile_2'=8,'rhs'=2] {'rhs'}, dimensions={0} | all-to-all | bytes 1048576 | tf_op jit(solution)/shard_map/all_to_all | solution.py:13
  87.8 21.5 %all_to_all.88 = f32[32,1,256]{2,1,0:T(1,128)S(1)} all-to-all(f32[32,1,256]{2,1,0:T(1,128)S(1)} %broadcast_in_dim.28), channel_id=1, replica_groups=mesh['tile_0'=4,'tile_1'=4,'tile_2'=8,'rhs'=2] {'tile_1','tile_2'}, dimensions={0} | all-to-all | bytes 65536 | tf_op jit(solution)/shard_map/all_to_all | solution.py:13
  109.3 7.0 %all_to_all.89 = f32[4,1,256]{2,1,0:T(1,128)S(1)} all-to-all(f32[4,1,256]{2,1,0:T(1,128)S(1)} %broadcast_in_dim.29), channel_id=1, replica_groups=mesh['tile_0'=4,'tile_1'=4,'tile_2'=8,'rhs'=2] {'tile_0'}, dimensions={0} | all-to-all | bytes 8192 | tf_op jit(solution)/shard_map/all_to_all | solution.py:13
  116.6 3.5 %fusion.22 = f32[64,2560]{1,0:T(8,128)S(1)} fusion(bf16[1024,2560]{1,0:T(8,128)(2,1)} %param.4, f32[64,1024]{1,0:T(8,128)S(1)} %get-tuple-element.9), kind=kOutput, calls=%fused_computation.57 | convolution fusion | flops 335609856 | bytes 6160384 | tf_op jit(solution)/shard_map/dot_general | solution.py:134
  120.6 17.5 %all_to_all.90 = f32[32,4,1280]{2,1,0:T(4,128)S(1)} all-to-all(f32[32,4,1280]{2,1,0:T(4,128)S(1)} %bitcast.66), channel_id=1, replica_groups=mesh['tile_0'=4,'tile_1'=4,'tile_2'=8,'rhs'=2] {'tile_1','tile_2'}, dimensions={0} | all-to-all | bytes 1310720 | tf_op jit(solution)/shard_map/all_to_all | solution.py:73
  138.2 6.6 %all_to_all.91 = f32[4,1,1280]{2,1,0:T(1,128)S(1)} all-to-all(f32[4,1,1280]{2,1,0:T(1,128)S(1)} %all_to_all.63), channel_id=1, replica_groups=mesh['tile_0'=4,'tile_1'=4,'tile_2'=8,'rhs'=2] {'tile_0'}, dimensions={0} | all-to-all | bytes 40960 | tf_op jit(solution)/shard_map/all_to_all | solution.py:80
  144.9 6.6 %all_to_all.92 = f32[4,1,1280]{2,1,0:T(1,128)S(1)} all-to-all(f32[4,1,1280]{2,1,0:T(1,128)S(1)} %broadcast_in_dim.30), channel_id=1, replica_groups=mesh['tile_0'=4,'tile_1'=4,'tile_2'=8,'rhs'=2] {'tile_0'}, dimensions={0} | all-to-all | bytes 40960 | tf_op jit(solution)/shard_map/all_to_all | solution.py:13
  152.4 8.0 %all-to-all-start.10 = ((f32[32,4,1280]{2,1,0:T(4,128)}), f32[32,4,1280]{2,1,0:T(4,128)S(1)}, u32[]{:S(2)}, u32[]{:S(2)}) async-start(f32[32,4,1280]{2,1,0:T(4,128)} %broadcast_in_dim.32), calls=%async_computation.10 | async-start | bytes 1310720 | tf_op jit(solution)/shard_map/all_to_all | solution.py:13
  160.5 3.1 %collective-permute-start.4 = (f32[64,2,128]{2,1,0:T(2,128)S(1)}, f32[64,2,128]{2,1,0:T(2,128)S(1)}, u32[]{:S(2)}, u32[]{:S(2)}) collective-permute-start(f32[64,2,128]{2,1,0:T(2,128)S(1)} %get-tuple-element.16), channel_id=1, source_target_pairs={{0,2},{2,4},{4,6},{6,8},{8,10},{10,12},{12,14},{14,16},{16,18},{18... | collective-permute-start | bytes 196616 | tf_op jit(solution)/shard_map/ppermute | solution.py:41
  164.9 3.5 %collective-permute-done.4 = f32[64,2,128]{2,1,0:T(2,128)S(1)} collective-permute-done((f32[64,2,128]{2,1,0:T(2,128)S(1)}, f32[64,2,128]{2,1,0:T(2,128)S(1)}, u32[]{:S(2)}, u32[]{:S(2)}) %collective-permute-start.4) | collective-permute-done | bytes 65568 | tf_op jit(solution)/shard_map/ppermute | solution.py:41
  168.4 4.5 %collective-permute-done.5 = f32[64,2,128]{2,1,0:T(2,128)S(1)} collective-permute-done((f32[64,2,128]{2,1,0:T(2,128)S(1)}, f32[64,2,128]{2,1,0:T(2,128)S(1)}, u32[]{:S(2)}, u32[]{:S(2)}) %collective-permute-start.5) | collective-permute-done | bytes 65568 | tf_op jit(solution)/shard_map/ppermute | solution.py:44
  174.1 4.2 %fusion.9 = f32[64,1024]{1,0:T(8,128)S(1)} fusion(bf16[1024,2560]{1,0:T(8,128)(2,1)} %param.4, f32[64,2560]{1,0:T(8,128)S(1)} %reshape_reshape_reshape.7, f32[2560]{0:T(1024)S(1)} %copy-done.1), kind=kOutput, calls=%fused_computation.27 | convolution fusion | flops 335872000 | bytes 6170624 | tf_op jit(solution)/shard_map/dot_general | solution.py:137
  178.3 12.0 %all_to_all.93 = f32[2,64,1024]{2,1,0:T(8,128)S(1)} all-to-all(f32[2,64,1024]{2,1,0:T(8,128)S(1)} %broadcast_in_dim.33), channel_id=1, replica_groups=mesh['tile_0'=4,'tile_1'=4,'tile_2'=8,'rhs'=2] {'rhs'}, dimensions={0} | all-to-all | bytes 1048576 | tf_op jit(solution)/shard_map/all_to_all | solution.py:13
  191.8 14.1 %all_to_all.94 = f32[32,1,256]{2,1,0:T(1,128)S(1)} all-to-all(f32[32,1,256]{2,1,0:T(1,128)S(1)} %broadcast_in_dim.34), channel_id=1, replica_groups=mesh['tile_0'=4,'tile_1'=4,'tile_2'=8,'rhs'=2] {'tile_1','tile_2'}, dimensions={0} | all-to-all | bytes 65536 | tf_op jit(solution)/shard_map/all_to_all | solution.py:13
  206.0 6.5 %all_to_all.95 = f32[4,1,256]{2,1,0:T(1,128)S(1)} all-to-all(f32[4,1,256]{2,1,0:T(1,128)S(1)} %broadcast_in_dim.35), channel_id=1, replica_groups=mesh['tile_0'=4,'tile_1'=4,'tile_2'=8,'rhs'=2] {'tile_0'}, dimensions={0} | all-to-all | bytes 8192 | tf_op jit(solution)/shard_map/all_to_all | solution.py:13
  (70 shorter events, 15.2 us)
Async XLA Ops:
  0.6 61.0 %copy-start = (f32[64,1024]{1,0:T(8,128)S(1)}, f32[64,1024]{1,0:T(8,128)}, u32[]{:S(2)}) copy-start(f32[64,1024]{1,0:T(8,128)} %param.7) | copy-start | bytes 786436
  0.6 56.6 %copy-start.2 = (f32[8,128]{1,0:T(8,128)S(1)}, f32[8,128]{1,0:T(8,128)}, u32[]{:S(2)}) copy-start(f32[8,128]{1,0:T(8,128)} %param.6) | copy-start | bytes 12292
  4.8 68.6 %copy-start.1 = (f32[2560]{0:T(1024)S(1)}, f32[2560]{0:T(1024)}, u32[]{:S(2)}) copy-start(f32[2560]{0:T(1024)} %param.5) | copy-start | bytes 30724
  49.5 23.6 %all-to-all-start.3 = ((f32[32,4,1280]{2,1,0:T(4,128)}), f32[32,4,1280]{2,1,0:T(4,128)S(1)}, u32[]{:S(2)}, u32[]{:S(2)}) async-start(f32[32,4,1280]{2,1,0:T(4,128)} %broadcast_in_dim.26), calls=%async_computation.3 | async-start | bytes 1310720 | tf_op jit(solution)/shard_map/all_to_all | solution.py:13
  57.2 9.9 %collective-permute-start = (f32[1,128]{1,0:T(1,128)S(1)}, f32[1,128]{1,0:T(1,128)S(1)}, u32[]{:S(2)}, u32[]{:S(2)}) collective-permute-start(f32[1,128]{1,0:T(1,128)S(1)} %get-tuple-element.20), channel_id=1, source_target_pairs={{0,2},{2,4},{4,6},{6,8},{8,10},{10,12},{12,14},{14,16},{16,18},{18... | collective-permute-start | bytes 1544 | tf_op jit(solution)/shard_map/ppermute | solution.py:41
  60.4 8.3 %collective-permute-start.1 = (f32[1,128]{1,0:T(1,128)S(1)}, f32[1,128]{1,0:T(1,128)S(1)}, u32[]{:S(2)}, u32[]{:S(2)}) collective-permute-start(f32[1,128]{1,0:T(1,128)S(1)} %get-tuple-element.21), channel_id=1, source_target_pairs={{2,0},{4,2},{6,4},{8,6},{10,8},{12,10},{14,12},{16,14},{18,16},{20... | collective-permute-start | bytes 1544 | tf_op jit(solution)/shard_map/ppermute | solution.py:44
  61.8 6.9 %collective-permute-start.2 = (f32[64,2,128]{2,1,0:T(2,128)S(1)}, f32[64,2,128]{2,1,0:T(2,128)S(1)}, u32[]{:S(2)}, u32[]{:S(2)}) collective-permute-start(f32[64,2,128]{2,1,0:T(2,128)S(1)} %get-tuple-element.18), channel_id=1, source_target_pairs={{0,2},{2,4},{4,6},{6,8},{8,10},{10,12},{12,14},{14,16},{16,18},{18... | collective-permute-start | bytes 196616 | tf_op jit(solution)/shard_map/ppermute | solution.py:41
  65.8 6.9 %collective-permute-start.3 = (f32[64,2,128]{2,1,0:T(2,128)S(1)}, f32[64,2,128]{2,1,0:T(2,128)S(1)}, u32[]{:S(2)}, u32[]{:S(2)}) collective-permute-start(f32[64,2,128]{2,1,0:T(2,128)S(1)} %get-tuple-element.19), channel_id=1, source_target_pairs={{2,0},{4,2},{6,4},{8,6},{10,8},{12,10},{14,12},{16,14},{18,16},{20... | collective-permute-start | bytes 196616 | tf_op jit(solution)/shard_map/ppermute | solution.py:44
  152.4 21.4 %all-to-all-start.10 = ((f32[32,4,1280]{2,1,0:T(4,128)}), f32[32,4,1280]{2,1,0:T(4,128)S(1)}, u32[]{:S(2)}, u32[]{:S(2)}) async-start(f32[32,4,1280]{2,1,0:T(4,128)} %broadcast_in_dim.32), calls=%async_computation.10 | async-start | bytes 1310720 | tf_op jit(solution)/shard_map/all_to_all | solution.py:13
  160.5 7.9 %collective-permute-start.4 = (f32[64,2,128]{2,1,0:T(2,128)S(1)}, f32[64,2,128]{2,1,0:T(2,128)S(1)}, u32[]{:S(2)}, u32[]{:S(2)}) collective-permute-start(f32[64,2,128]{2,1,0:T(2,128)S(1)} %get-tuple-element.16), channel_id=1, source_target_pairs={{0,2},{2,4},{4,6},{6,8},{8,10},{10,12},{12,14},{14,16},{16,18},{18... | collective-permute-start | bytes 196616 | tf_op jit(solution)/shard_map/ppermute | solution.py:41
  163.6 9.2 %collective-permute-start.5 = (f32[64,2,128]{2,1,0:T(2,128)S(1)}, f32[64,2,128]{2,1,0:T(2,128)S(1)}, u32[]{:S(2)}, u32[]{:S(2)}) collective-permute-start(f32[64,2,128]{2,1,0:T(2,128)S(1)} %get-tuple-element.17), channel_id=1, source_target_pairs={{2,0},{4,2},{6,4},{8,6},{10,8},{12,10},{14,12},{16,14},{18,16},{20... | collective-permute-start | bytes 196616 | tf_op jit(solution)/shard_map/ppermute | solution.py:44
where the time goes:
time: 215 us; the launch traced here: 213 us
  blocking collectives  144 us (67%)
  starting transfers between devices  29.8 us (14%)
  matrix products  15.5 us (7%)
  waiting for transfers between devices  13.9 us (6%)
  other arithmetic  5.22 us (2%)
  local copies, waits for them, and re-layouts  4.04 us (2%)
    all_to_all x8, blocking collectives, sent_to_all(): lax.all_to_all(jnp.broadcast_to(array[None], (peers, *array.shape)), axis...  83 us
    all_to_all x2, blocking collectives, sent_and_summed(): tiles = lax.all_to_all(split_up(array, dim, peers), axis, 0, 0, tiled=True)  46.2 us
    all_to_all x2, starting transfers between devices, sent_to_all(): lax.all_to_all(jnp.broadcast_to(array[None], (peers, *array.shape)), axis...  15.7 us
    all_to_all x2, blocking collectives, sum_by_axis(): return jnp.sum(lax.all_to_all(own, far, 0, 0, tiled=True), axis=0)  14.8 us
    ppermute x3, starting transfers between devices, with_halo(): lax.ppermute(lax.slice_in_dim(block, block.shape[dim] - width, None, axis...  10.3 us
    ppermute x3, waiting for transfers between devices, with_halo(): lax.ppermute(lax.slice_in_dim(block, 0, width, axis=dim), axis, backward)  9.99 us
    dot_general x2, matrix products, per_device(): lax.dot_general(weighted, sensitivity, (((1,), (1,)), ((), ())), preferre...  8.34 us
    dot_general x2, matrix products, per_device(): jnp.dot(lowered, sensitivity, preferred_element_type=jnp.float32)  7.13 us
  transfers between devices with their start and end apart: 8, of which 5 were waited for; matrix products, arithmetic and copies ran while one was open for 1% of the time, Pallas kernels for 0%

commit v1 on v0

v1 whole, which is shorter than its diff:
```python
import jax
import jax.numpy as jnp
from jax import lax
from jax.sharding import Mesh
from jax.sharding import PartitionSpec as P

TILE = ("tile_0", "tile_1", "tile_2")
SWAP = [(0, 1), (1, 0)]
F32, BF16 = jnp.float32, jnp.bfloat16


def split3(x):
    hi = lax.reduce_precision(x, 8, 7)
    mid = lax.reduce_precision(x - hi, 8, 7)
    low = x - hi - mid
    return jnp.stack([hi, mid, low], axis=-1).astype(BF16)


def with_halo(block, dim, width):
    count = lax.axis_size(TILE)
    forward = [(i, i + 1) for i in range(count - 1)]
    backward = [(i + 1, i) for i in range(count - 1)]
    size = block.shape[dim]
    low = lax.ppermute(lax.slice_in_dim(block, size - width, size, axis=dim), TILE, forward)
    high = lax.ppermute(lax.slice_in_dim(block, 0, width, axis=dim), TILE, backward)
    return jnp.concatenate([low, block, high], axis=dim)


def stencil_rows(padded_field, reaction):
    sided = jnp.pad(padded_field, ((0, 0), (0, 0), (1, 1)))
    center = padded_field[:, 1:-1, :]
    neighbours = (
        padded_field[:, 2:, :] + padded_field[:, :-2, :] + sided[:, 1:-1, 2:] + sided[:, 1:-1, :-2]
    )
    return (reaction + 4.0) * center - neighbours


def per_device(sensitivity, precision, reaction, load):
    rows, params = load.shape
    strip_rows, columns = reaction.shape
    obs = sensitivity.shape[1]
    strip = lax.axis_index(TILE)
    strips = lax.axis_size(TILE)
    halves = strips // rows
    piece = obs // halves
    lanes = piece // 2
    reaction_deep = with_halo(reaction, 0, 1)
    positions = jnp.arange(strip_rows + 2)
    inside = jnp.logical_and(
        jnp.logical_or(positions > 0, strip > 0),
        jnp.logical_or(positions < strip_rows + 1, strip < strips - 1),
    )
    inside_mask = inside.astype(F32)[None, :, None]
    own_precision = lax.dynamic_index_in_dim(
        precision.reshape(halves, 2, lanes), strip % halves, 0, keepdims=False
    )

    def smoothed(field):
        grid = field.reshape(rows, strip_rows, columns)
        once = stencil_rows(with_halo(grid, 1, 2), reaction_deep) * inside_mask
        return once, stencil_rows(once, reaction).reshape(field.shape)

    def exchanged(tiles):
        return lax.all_to_all(tiles, TILE, 0, 0, tiled=True)

    def observed(field):
        partial = jnp.dot(field.astype(BF16), sensitivity, preferred_element_type=F32)
        return partial.astype(BF16).reshape(strips, 2, lanes)

    def projected(weighted):
        half = lax.dot_general(
            weighted.reshape(rows, obs), sensitivity, (((1,), (1,)), ((), ())), preferred_element_type=F32
        )
        return half + lax.ppermute(half, "rhs", SWAP)

    def to_all(tile):
        return exchanged(jnp.broadcast_to(tile[None], (strips, *tile.shape)))

    _, prior = smoothed(load)
    predicted = exchanged(observed(load)).astype(F32).sum(axis=0)
    weighted = (own_precision * predicted).astype(BF16)
    image = projected(to_all(weighted)) + prior

    once, prior = smoothed(image)
    own_once = once[:, 1:-1, :]
    bent = jnp.sum(own_once * own_once, axis=(1, 2))
    sums = jnp.stack(
        [jnp.sum(load * load, axis=1), jnp.sum(load * image, axis=1), jnp.sum(image * image, axis=1)], axis=-1
    )
    terms = split3(sums).reshape(rows, 9)
    terms = jnp.pad(terms, ((0, 0), (0, 119)))
    terms = jnp.broadcast_to(terms[:, None, None, :], (rows, halves, 2, 128)).reshape(strips, 2, 128)
    arrived = exchanged(jnp.concatenate([observed(image), terms], axis=2)).astype(F32).sum(axis=0)
    predicted = arrived[:, :lanes]
    raised = own_precision * predicted
    own_sums = arrived[0, lanes : lanes + 9].reshape(3, 3).sum(axis=1)
    own_data = jnp.sum(raised * predicted)
    own_terms = split3(jnp.concatenate([own_sums, own_data[None]])).reshape(12)
    bent_terms = split3(bent)[:, :2].reshape(2 * rows)
    message = jnp.concatenate(
        [raised.astype(BF16), jnp.stack([jnp.pad(own_terms, (0, 116)), bent_terms])], axis=1
    )
    received = to_all(message)
    scalars = received[:, :, lanes:].astype(F32)
    bent_sum = jnp.sum(scalars[:, 1, :], axis=0).reshape(rows, 2).sum(axis=1)
    terms = scalars[:, 0, :12].reshape(rows, halves, 4, 3).sum(axis=3)
    bb, bq, qq = terms[:, 0, 0], terms[:, 0, 1], terms[:, 0, 2]
    data = terms[:, :, 3].sum(axis=1)
    qw = data + lax.ppermute(data, "rhs", SWAP) + bent_sum

    alpha = bb / bq
    fresh = bb - 2.0 * alpha * bq + alpha * alpha * qq
    beta = fresh / bb
    grown = 1.0 + beta
    curved = grown * grown * bq - 2.0 * alpha * grown * qq + alpha * alpha * qw
    second = fresh / curved
    near = (alpha + second * grown)[:, None]
    far = (alpha * second)[:, None]

    twice = projected(received[:, :, :lanes]) + prior
    solution = near * load - far * image
    residual = load - near * image + far * twice
    return (solution, residual)


def solution(mesh):
    torus = Mesh(
        mesh.devices.reshape(4, 4, 8, mesh.shape["rhs"]), ("tile_0", "tile_1", "tile_2", "rhs")
    )
    placed = (P(TILE, "rhs"), P("rhs"), P(TILE, None), P(None, TILE))
    return jax.shard_map(
        per_device,
        mesh=torus,
        in_specs=placed,
        out_specs=(P(None, TILE), P(None, TILE)),
        check_vma=False,
    )
```

time: 215 us -> 142 us (0.66)
  blocking collectives: 144 us -> 21.6 us
  starting transfers between devices: 29.8 us -> 57.7 us
  waiting for transfers between devices: 13.9 us -> 34.5 us
  other arithmetic: 5.22 us -> 7.69 us
  matrix products: 15.5 us -> 13.1 us
    all_to_all x12 -> x1, blocking collectives: 144 us -> 21.6 us  [exchanged(): return lax.all_to_all(tiles, TILE, 0, 0, tiled=True)]
    all_to_all x2 -> x3, waiting for transfers between devices: 0.46 us -> 32.6 us  [exchanged(): return lax.all_to_all(tiles, TILE, 0, 0, tiled=True)]
    all_to_all x2 -> x3, starting transfers between devices: 15.7 us -> 34.7 us  [exchanged(): return lax.all_to_all(tiles, TILE, 0, 0, tiled=True)]
    ppermute x6 -> x9, waiting for transfers between devices: 13.5 us -> 1.92 us  [the longest x3 0.67 us: with_halo(): lax.ppermute(lax.slice_in_dim(block, size - width, size, axis=dim), TILE,...]
    ppermute x6 -> x9, starting transfers between devices: 14.1 us -> 23 us  [the longest x3 12 us: with_halo(): lax.ppermute(lax.slice_in_dim(block, size - width, size, axis=dim), TILE,...]
    dot_general x4, matrix products: 15.5 us -> 13.1 us  [the longest x2 8.48 us: projected(): lax.dot_general(weighted.reshape(rows, obs), sensitivity, (((1,), (1,)),...]
    slice x3 -> x7, local copies, waits for them, and re-layouts: 0.09 us -> 2.36 us  [the longest x1 1.84 us: per_device(): bb, bq, qq = (terms[:, 0, 0], terms[:, 0, 1], terms[:, 0, 2])]
  transfers between devices with their start and end apart: 8 -> 12, of which waited for: 5 -> 6; matrix products, arithmetic and copies ran while one was open for 1% -> 4% of each run, Pallas kernels for 0% -> 0%
where the time goes in v1:
time: 142 us
  starting transfers between devices  57.7 us (41%)
  waiting for transfers between devices  34.5 us (24%)
  blocking collectives  21.6 us (15%)
  matrix products  13.1 us (9%)
  other arithmetic  7.69 us (5%)
  local copies, waits for them, and re-layouts  5.92 us (4%)
    all_to_all x3, starting transfers between devices, exchanged(): return lax.all_to_all(tiles, TILE, 0, 0, tiled=True)  34.7 us
    all_to_all x3, waiting for transfers between devices, exchanged(): return lax.all_to_all(tiles, TILE, 0, 0, tiled=True)  32.6 us
    all_to_all x1, blocking collectives, exchanged(): return lax.all_to_all(tiles, TILE, 0, 0, tiled=True)  21.6 us
    ppermute x3, starting transfers between devices, with_halo(): lax.ppermute(lax.slice_in_dim(block, size - width, size, axis=dim), TILE,...  12 us
    dot_general x2, matrix products, projected(): lax.dot_general(weighted.reshape(rows, obs), sensitivity, (((1,), (1,)),...  8.48 us
    ppermute x2, starting transfers between devices, projected(): return half + lax.ppermute(half, 'rhs', SWAP)  7.04 us
    dot_general x2, matrix products, observed(): jnp.dot(field.astype(BF16), sensitivity, preferred_element_type=F32)  4.64 us
    ppermute x3, starting transfers between devices, with_halo(): lax.ppermute(lax.slice_in_dim(block, 0, width, axis=dim), TILE, backward)  3.88 us
  transfers between devices with their start and end apart: 12, of which 6 were waited for; matrix products, arithmetic and copies ran while one was open for 4% of the time, Pallas kernels for 0%

profile of v1, /device:TPU:1, one launch (start us, length us, event | category | flops | bytes accessed | tf_op | source)
XLA Modules:
  0.0 141.6 jit_solution(15514597990441685819)
XLA Ops:
  0.7 3.6 %convolution_convert_fusion.1 = bf16[64,2560]{1,0:T(8,128)(2,1)S(1)} fusion(bf16[1024,2560]{1,0:T(8,128)(2,1)} %param.4, f32[64,1024]{1,0:T(8,128)} %param.7), kind=kOutput, calls=%fused_computation.1 | convolution fusion | flops 335773696 | bytes 5832704 | tf_op jit(solution)/shard_map/dot_general | solution.py:67
  5.1 16.3 %all-to-all-start = ((bf16[128,2,640]{2,1,0:T(2,128)(2,1)}), bf16[128,2,640]{2,1,0:T(2,128)(2,1)S(1)}, u32[]{:S(2)}, u32[]{:S(2)}) async-start(bf16[128,2,640]{2,1,0:T(2,128)(2,1)} %reshape.357), calls=%async_computation | async-start | bytes 655360 | tf_op jit(solution)/shard_map/all_to_all | solution.py:64
  21.5 1.3 collective-permute-start.4
  22.8 4.0 %collective-permute-start.3 = (f32[64,2,128]{2,1,0:T(2,128)S(1)}, f32[64,2,128]{2,1,0:T(2,128)S(1)}, u32[]{:S(2)}, u32[]{:S(2)}) collective-permute-start(f32[64,2,128]{2,1,0:T(2,128)S(1)} %get-tuple-element.23), channel_id=1, source_target_pairs={{0,2},{2,4},{4,6},{6,8},{8,10},{10,12},{12,14},{14,16},{16,18},{18... | collective-permute-start | bytes 196616 | tf_op jit(solution)/shard_map/ppermute | solution.py:24
  26.9 9.7 %all-to-all-done = bf16[128,2,640]{2,1,0:T(2,128)(2,1)S(1)} async-done(((bf16[128,2,640]{2,1,0:T(2,128)(2,1)}), bf16[128,2,640]{2,1,0:T(2,128)(2,1)S(1)}, u32[]{:S(2)}, u32[]{:S(2)}) %all-to-all-start) | async-done | bytes 327712 | tf_op jit(solution)/shard_map/all_to_all | solution.py:64
  37.0 0.9 broadcast_in_dim.13
  37.8 6.5 %all-to-all-start.1 = ((bf16[128,2,640]{2,1,0:T(2,128)(2,1)}), bf16[128,2,640]{2,1,0:T(2,128)(2,1)S(1)}, u32[]{:S(2)}, u32[]{:S(2)}) async-start(bf16[128,2,640]{2,1,0:T(2,128)(2,1)} %broadcast_in_dim.13), calls=%async_computation.1 | async-start | bytes 655360 | tf_op jit(solution)/shard_map/all_to_all | solution.py:64
  44.4 1.3 collective-permute-start.2
  45.7 4.0 %collective-permute-start.1 = (f32[1,128]{1,0:T(1,128)S(1)}, f32[1,128]{1,0:T(1,128)S(1)}, u32[]{:S(2)}, u32[]{:S(2)}) collective-permute-start(f32[1,128]{1,0:T(1,128)S(1)} %get-tuple-element.27), channel_id=1, source_target_pairs={{0,2},{2,4},{4,6},{6,8},{8,10},{10,12},{12,14},{14,16},{16,18},{18... | collective-permute-start | bytes 1544 | tf_op jit(solution)/shard_map/ppermute | solution.py:24
  50.5 7.8 %all-to-all-done.1 = bf16[128,2,640]{2,1,0:T(2,128)(2,1)S(1)} async-done(((bf16[128,2,640]{2,1,0:T(2,128)(2,1)}), bf16[128,2,640]{2,1,0:T(2,128)(2,1)S(1)}, u32[]{:S(2)}, u32[]{:S(2)}) %all-to-all-start.1) | async-done | bytes 327712 | tf_op jit(solution)/shard_map/all_to_all | solution.py:64
  58.5 4.3 %fusion.28 = f32[64,1024]{1,0:T(8,128)S(1)} fusion(bf16[64,2560]{1,0:T(8,128)(2,1)S(1)} %reshape.358, bf16[1024,2560]{1,0:T(8,128)(2,1)} %param.4), kind=kOutput, calls=%fused_computation.92 | convolution fusion | flops 335544320 | bytes 5832704 | tf_op jit(solution)/shard_map/dot_general | solution.py:71
  62.8 3.6 %collective-permute-start = (f32[64,1024]{1,0:T(8,128)S(1)}, f32[64,1024]{1,0:T(8,128)S(1)}, u32[]{:S(2)}, u32[]{:S(2)}) collective-permute-start(f32[64,1024]{1,0:T(8,128)S(1)} %fusion.28), channel_id=1, source_target_pairs={{0,1},{1,0},{2,3},{3,2},{4,5},{5,4},{6,7},{7,6},{8,9},{9,8},{10,11... | collective-permute-start | bytes 786440 | tf_op jit(solution)/shard_map/ppermute | solution.py:74
  67.8 1.0 convolution_convert_fusion
  68.9 1.3 collective-permute-start.6
  70.2 4.0 %collective-permute-start.5 = (f32[64,2,128]{2,1,0:T(2,128)S(1)}, f32[64,2,128]{2,1,0:T(2,128)S(1)}, u32[]{:S(2)}, u32[]{:S(2)}) collective-permute-start(f32[64,2,128]{2,1,0:T(2,128)S(1)} %get-tuple-element.21), channel_id=1, source_target_pairs={{0,2},{2,4},{4,6},{6,8},{8,10},{10,12},{12,14},{14,16},{16,18},{18... | collective-permute-start | bytes 196616 | tf_op jit(solution)/shard_map/ppermute | solution.py:24
  74.6 1.1 pad_maximum_fusion.2
  75.7 11.9 %all-to-all-start.2 = ((bf16[128,2,768]{2,1,0:T(2,128)(2,1)}), bf16[128,2,768]{2,1,0:T(2,128)(2,1)S(1)}, u32[]{:S(2)}, u32[]{:S(2)}) async-start(bf16[128,2,768]{2,1,0:T(2,128)(2,1)} %pad_maximum_fusion.2), calls=%async_computation.2 | async-start | bytes 786432 | tf_op jit(solution)/shard_map/all_to_all | solution.py:64
  88.9 15.1 %all-to-all-done.2 = bf16[128,2,768]{2,1,0:T(2,128)(2,1)S(1)} async-done(((bf16[128,2,768]{2,1,0:T(2,128)(2,1)}), bf16[128,2,768]{2,1,0:T(2,128)(2,1)S(1)}, u32[]{:S(2)}, u32[]{:S(2)}) %all-to-all-start.2) | async-done | bytes 393248 | tf_op jit(solution)/shard_map/all_to_all | solution.py:64
  106.4 21.6 %all_to_all.20 = bf16[128,2,768]{2,1,0:T(2,128)(2,1)S(1)} all-to-all(bf16[128,2,768]{2,1,0:T(2,128)(2,1)S(1)} %broadcast_in_dim.17), channel_id=1, replica_groups=mesh['tile_0'=4,'tile_1'=4,'tile_2'=8,'rhs'=2] {'tile_0','tile_1','tile_2'}, dimensions={0} | all-to-all | bytes 786432 | tf_op jit(solution)/shard_map/all_to_all | solution.py:64
  128.6 1.8 %slice_reduce_fusion.3 = (f32[64]{0:T(128)S(1)}, f32[64]{0:T(128)S(1)}, f32[64]{0:T(128)S(1)}) fusion(f32[64,2,4]{2,1,0:T(2,128)S(1)} %reduce_sum.122), kind=kLoop, calls=%fused_computation.51 | loop fusion | bytes 1536 | tf_op jit(solution)/shard_map/slice | solution.py:107
  130.5 0.9 slice_reduce_fusion.1
  131.9 4.2 %fusion.29 = f32[64,1024]{1,0:T(8,128)S(1)} fusion(bf16[64,2560]{1,0:T(8,128)(2,1)S(1)} %reshape.364, bf16[1024,2560]{1,0:T(8,128)(2,1)} %param.4), kind=kOutput, calls=%fused_computation.93 | convolution fusion | flops 335544320 | bytes 5832704 | tf_op jit(solution)/shard_map/dot_general | solution.py:71
  136.0 3.4 %collective-permute-start.8 = (f32[64,1024]{1,0:T(8,128)S(1)}, f32[64,1024]{1,0:T(8,128)S(1)}, u32[]{:S(2)}, u32[]{:S(2)}) collective-permute-start(f32[64,1024]{1,0:T(8,128)S(1)} %fusion.29), channel_id=1, source_target_pairs={{0,1},{1,0},{2,3},{3,2},{4,5},{5,4},{6,7},{7,6},{8,9},{9,8},{10,11... | collective-permute-start | bytes 786440 | tf_op jit(solution)/shard_map/ppermute | solution.py:74
  140.7 1.0 fusion.15
  (79 shorter events, 9.9 us)
Async XLA Ops:
  0.6 20.8 %copy-start = (f32[64,1024]{1,0:T(8,128)S(1)}, f32[64,1024]{1,0:T(8,128)}, u32[]{:S(2)}) copy-start(f32[64,1024]{1,0:T(8,128)} %param.7) | copy-start | bytes 786436
  0.6 26.2 %copy-start.2 = (f32[2560]{0:T(1024)S(1)}, f32[2560]{0:T(1024)}, u32[]{:S(2)}) copy-start(f32[2560]{0:T(1024)} %param.5) | copy-start | bytes 30724
  0.7 43.7 %copy-start.1 = (f32[8,128]{1,0:T(8,128)S(1)}, f32[8,128]{1,0:T(8,128)}, u32[]{:S(2)}) copy-start(f32[8,128]{1,0:T(8,128)} %param.6) | copy-start | bytes 12292
  5.1 31.5 %all-to-all-start = ((bf16[128,2,640]{2,1,0:T(2,128)(2,1)}), bf16[128,2,640]{2,1,0:T(2,128)(2,1)S(1)}, u32[]{:S(2)}, u32[]{:S(2)}) async-start(bf16[128,2,640]{2,1,0:T(2,128)(2,1)} %reshape.357), calls=%async_computation | async-start | bytes 655360 | tf_op jit(solution)/shard_map/all_to_all | solution.py:64
  21.5 28.8 %collective-permute-start.4 = (f32[64,2,128]{2,1,0:T(2,128)S(1)}, f32[64,2,128]{2,1,0:T(2,128)S(1)}, u32[]{:S(2)}, u32[]{:S(2)}) collective-permute-start(f32[64,2,128]{2,1,0:T(2,128)S(1)} %get-tuple-element.24), channel_id=1, source_target_pairs={{2,0},{4,2},{6,4},{8,6},{10,8},{12,10},{14,12},{16,14},{18,16},{20... | collective-permute-start | bytes 196616 | tf_op jit(solution)/shard_map/ppermute | solution.py:25
  22.8 27.6 %collective-permute-start.3 = (f32[64,2,128]{2,1,0:T(2,128)S(1)}, f32[64,2,128]{2,1,0:T(2,128)S(1)}, u32[]{:S(2)}, u32[]{:S(2)}) collective-permute-start(f32[64,2,128]{2,1,0:T(2,128)S(1)} %get-tuple-element.23), channel_id=1, source_target_pairs={{0,2},{2,4},{4,6},{6,8},{8,10},{10,12},{12,14},{14,16},{16,18},{18... | collective-permute-start | bytes 196616 | tf_op jit(solution)/shard_map/ppermute | solution.py:24
  37.8 20.4 %all-to-all-start.1 = ((bf16[128,2,640]{2,1,0:T(2,128)(2,1)}), bf16[128,2,640]{2,1,0:T(2,128)(2,1)S(1)}, u32[]{:S(2)}, u32[]{:S(2)}) async-start(bf16[128,2,640]{2,1,0:T(2,128)(2,1)} %broadcast_in_dim.13), calls=%async_computation.1 | async-start | bytes 655360 | tf_op jit(solution)/shard_map/all_to_all | solution.py:64
  44.4 5.3 %collective-permute-start.2 = (f32[1,128]{1,0:T(1,128)S(1)}, f32[1,128]{1,0:T(1,128)S(1)}, u32[]{:S(2)}, u32[]{:S(2)}) collective-permute-start(f32[1,128]{1,0:T(1,128)S(1)} %get-tuple-element.28), channel_id=1, source_target_pairs={{2,0},{4,2},{6,4},{8,6},{10,8},{12,10},{14,12},{16,14},{18,16},{20... | collective-permute-start | bytes 1544 | tf_op jit(solution)/shard_map/ppermute | solution.py:25
  45.7 4.7 %collective-permute-start.1 = (f32[1,128]{1,0:T(1,128)S(1)}, f32[1,128]{1,0:T(1,128)S(1)}, u32[]{:S(2)}, u32[]{:S(2)}) collective-permute-start(f32[1,128]{1,0:T(1,128)S(1)} %get-tuple-element.27), channel_id=1, source_target_pairs={{0,2},{2,4},{4,6},{6,8},{8,10},{10,12},{12,14},{14,16},{16,18},{18... | collective-permute-start | bytes 1544 | tf_op jit(solution)/shard_map/ppermute | solution.py:24
  58.3 9.5 %slice-start = ((s8[5242880]{0:T(1024)(128)(4,1)}), s8[1048576]{0:T(1024)(128)(4,1)S(1)}, s32[]{:S(2)}) async-start(s8[5242880]{0:T(1024)(128)(4,1)} %bitcast.48), calls=%async_computation.4 | async-start | bytes 2097152
  58.5 9.3 %slice-start.1 = ((s8[5242880]{0:T(1024)(128)(4,1)}), s8[4194304]{0:T(1024)(128)(4,1)S(1)}, s32[]{:S(2)}) async-start(s8[5242880]{0:T(1024)(128)(4,1)} %bitcast.48), calls=%async_computation.5 | async-start | bytes 8388608
  62.8 4.8 %collective-permute-start = (f32[64,1024]{1,0:T(8,128)S(1)}, f32[64,1024]{1,0:T(8,128)S(1)}, u32[]{:S(2)}, u32[]{:S(2)}) collective-permute-start(f32[64,1024]{1,0:T(8,128)S(1)} %fusion.28), channel_id=1, source_target_pairs={{0,1},{1,0},{2,3},{3,2},{4,5},{5,4},{6,7},{7,6},{8,9},{9,8},{10,11... | collective-permute-start | bytes 786440 | tf_op jit(solution)/shard_map/ppermute | solution.py:74
  68.9 18.6 %collective-permute-start.6 = (f32[64,2,128]{2,1,0:T(2,128)S(1)}, f32[64,2,128]{2,1,0:T(2,128)S(1)}, u32[]{:S(2)}, u32[]{:S(2)}) collective-permute-start(f32[64,2,128]{2,1,0:T(2,128)S(1)} %get-tuple-element.22), channel_id=1, source_target_pairs={{2,0},{4,2},{6,4},{8,6},{10,8},{12,10},{14,12},{16,14},{18,16},{20... | collective-permute-start | bytes 196616 | tf_op jit(solution)/shard_map/ppermute | solution.py:25
  70.2 17.3 %collective-permute-start.5 = (f32[64,2,128]{2,1,0:T(2,128)S(1)}, f32[64,2,128]{2,1,0:T(2,128)S(1)}, u32[]{:S(2)}, u32[]{:S(2)}) collective-permute-start(f32[64,2,128]{2,1,0:T(2,128)S(1)} %get-tuple-element.21), channel_id=1, source_target_pairs={{0,2},{2,4},{4,6},{6,8},{8,10},{10,12},{12,14},{14,16},{16,18},{18... | collective-permute-start | bytes 196616 | tf_op jit(solution)/shard_map/ppermute | solution.py:24
  75.7 28.3 %all-to-all-start.2 = ((bf16[128,2,768]{2,1,0:T(2,128)(2,1)}), bf16[128,2,768]{2,1,0:T(2,128)(2,1)S(1)}, u32[]{:S(2)}, u32[]{:S(2)}) async-start(bf16[128,2,768]{2,1,0:T(2,128)(2,1)} %pad_maximum_fusion.2), calls=%async_computation.2 | async-start | bytes 786432 | tf_op jit(solution)/shard_map/all_to_all | solution.py:64
  136.0 4.6 %collective-permute-start.8 = (f32[64,1024]{1,0:T(8,128)S(1)}, f32[64,1024]{1,0:T(8,128)S(1)}, u32[]{:S(2)}, u32[]{:S(2)}) collective-permute-start(f32[64,1024]{1,0:T(8,128)S(1)} %fusion.29), channel_id=1, source_target_pairs={{0,1},{1,0},{2,3},{3,2},{4,5},{5,4},{6,7},{7,6},{8,9},{9,8},{10,11... | collective-permute-start | bytes 786440 | tf_op jit(solution)/shard_map/ppermute | solution.py:74
  139.5 1.2 collective-permute-start.7

commit v2 on v1

v2 whole, which is shorter than its diff:
```python
import jax
import jax.numpy as jnp
from jax import lax
from jax.sharding import Mesh
from jax.sharding import PartitionSpec as P

TILE = ("tile_0", "tile_1", "tile_2")
PLANE = ("tile_0", "tile_1")
LINE = "tile_2"
SWAP = [(0, 1), (1, 0)]
F32, BF16 = jnp.float32, jnp.bfloat16
BLOCK = 8


def packed(x):
    hi = lax.reduce_precision(x, 8, 7)
    mid = lax.reduce_precision(x - hi, 8, 7)
    return jnp.concatenate([hi, mid, x - hi - mid], axis=-1)


def unpacked(x):
    hi, mid, low = jnp.split(x, 3, axis=-1)
    return hi + mid + low


def neighbour_rows(block, dim, width):
    count = lax.axis_size(TILE)
    forward = [(i, i + 1) for i in range(count - 1)]
    backward = [(i + 1, i) for i in range(count - 1)]
    size = block.shape[dim]
    low = lax.ppermute(lax.slice_in_dim(block, size - width, size, axis=dim), TILE, forward)
    high = lax.ppermute(lax.slice_in_dim(block, 0, width, axis=dim), TILE, backward)
    return low, high


def stencil_rows(padded_field, reaction):
    sided = jnp.pad(padded_field, ((0, 0), (0, 0), (1, 1)))
    center = padded_field[:, 1:-1, :]
    neighbours = (
        padded_field[:, 2:, :] + padded_field[:, :-2, :] + sided[:, 1:-1, 2:] + sided[:, 1:-1, :-2]
    )
    return (reaction + 4.0) * center - neighbours


def per_device(sensitivity, precision, reaction, load):
    rows, params = load.shape
    strip_rows, columns = reaction.shape
    obs = sensitivity.shape[1]
    strip = lax.axis_index(TILE)
    strips = lax.axis_size(TILE)
    plane = lax.axis_size(PLANE)
    line = lax.axis_size(LINE)
    groups = rows // BLOCK
    halves = plane // groups
    piece = obs // halves
    positions = jnp.arange(strip_rows + 2)
    inside = jnp.logical_and(
        jnp.logical_or(positions > 0, strip > 0),
        jnp.logical_or(positions < strip_rows + 1, strip < strips - 1),
    )
    inside_mask = inside.astype(F32)[None, :, None]
    own_precision = lax.dynamic_index_in_dim(
        precision.reshape(halves, 1, piece), lax.axis_index(PLANE) % halves, 0, keepdims=False
    )

    def gridded(field):
        return field.reshape(rows, strip_rows, columns)

    def smoothed(field, low, high):
        widened = jnp.concatenate([low, gridded(field), high], axis=1)
        once = stencil_rows(widened, reaction_deep) * inside_mask
        return once, stencil_rows(once, reaction).reshape(field.shape)

    def exchanged(tiles, axis):
        return lax.all_to_all(tiles, axis, 0, 0, tiled=True)

    def summed(tiles, axis):
        return exchanged(tiles.astype(BF16), axis).astype(F32).sum(axis=0)

    def to_all(tile, axis):
        copies = jnp.broadcast_to(tile.astype(BF16)[None], (lax.axis_size(axis), *tile.shape))
        return exchanged(copies, axis)

    def total(tile, axis):
        return to_all(tile, axis).astype(F32).sum(axis=0)

    def observed(field):
        partial = jnp.dot(field.astype(BF16), sensitivity, preferred_element_type=F32)
        tiles = partial.reshape(groups, BLOCK, halves, piece).swapaxes(1, 2)
        return tiles.reshape(plane, BLOCK, piece)

    def projected(tiles):
        weighted = tiles.reshape(groups, halves, BLOCK, piece).swapaxes(1, 2).reshape(rows, obs)
        return lax.dot_general(
            weighted, sensitivity, (((1,), (1,)), ((), ())), preferred_element_type=F32
        )

    def lined(terms):
        return jnp.pad(terms, ((0, 0),) * (terms.ndim - 1) + ((0, 128 - terms.shape[-1]),))

    reaction_low, reaction_high = neighbour_rows(reaction, 0, 1)
    reaction_deep = jnp.concatenate([reaction_low, reaction, reaction_high], axis=0)
    low, high = neighbour_rows(gridded(load), 1, 2)
    tiles, low, high = lax.optimization_barrier((observed(load), low, high))
    _, prior = smoothed(load, low, high)
    predicted = total(summed(tiles, PLANE), LINE)
    half = projected(to_all(own_precision * predicted, PLANE))
    image = half + lax.ppermute(half, "rhs", SWAP) + prior

    low, high = neighbour_rows(gridded(image), 1, 2)
    sums = jnp.stack(
        [jnp.sum(load * load, axis=1), jnp.sum(load * image, axis=1), jnp.sum(image * image, axis=1)], axis=-1
    )
    terms = lined(packed(sums)).reshape(groups, 1, BLOCK, 128)
    terms = jnp.broadcast_to(terms, (groups, halves, BLOCK, 128)).reshape(plane, BLOCK, 128)
    arrived = summed(jnp.concatenate([observed(image), terms], axis=2), PLANE)
    arrived, low, high = lax.optimization_barrier((arrived, low, high))
    once, prior = smoothed(image, low, high)
    bent = jnp.sum(once[:, 1:-1, :] ** 2, axis=(1, 2)).reshape(groups, BLOCK)
    terms = jnp.concatenate([packed(unpacked(arrived[:, piece : piece + 9])), packed(bent)], axis=1)
    arrived = total(jnp.concatenate([arrived[:, :piece], lined(terms)], axis=1), LINE)
    predicted = arrived[:, :piece]
    raised = own_precision * predicted
    data = jnp.sum(raised * predicted, axis=1, keepdims=True)
    row_sums = unpacked(arrived[:, piece : piece + 9])
    bent = unpacked(arrived[:, piece + 9 : piece + 9 + 3 * BLOCK])
    terms = jnp.concatenate([packed(jnp.concatenate([row_sums, data], axis=1)), packed(bent)], axis=1)
    received = to_all(jnp.concatenate([raised, lined(terms)], axis=1), PLANE)
    scalars = received[:, :, piece:].astype(F32)
    bent = unpacked(jnp.sum(scalars[:, :, 12 : 12 + 3 * BLOCK], axis=0)).reshape(rows)
    terms = unpacked(scalars[:, :, :12]).reshape(groups, halves, BLOCK, 4)
    bb, bq, qq = (terms[:, 0, :, i].reshape(rows) for i in range(3))
    data = terms[:, :, :, 3].sum(axis=1).reshape(rows)
    qw = data + lax.ppermute(data, "rhs", SWAP) + bent

    alpha = bb / bq
    fresh = bb - 2.0 * alpha * bq + alpha * alpha * qq
    beta = fresh / bb
    grown = 1.0 + beta
    curved = grown * grown * bq - 2.0 * alpha * grown * qq + alpha * alpha * qw
    second = fresh / curved
    near = (alpha + second * grown)[:, None]
    far = (alpha * second)[:, None]

    half = projected(received[:, :, :piece])
    twice = half + lax.ppermute(half, "rhs", SWAP) + prior
    solution = near * load - far * image
    residual = load - near * image + far * twice
    return (solution, residual)


def solution(mesh):
    torus = Mesh(
        mesh.devices.reshape(4, 4, 8, mesh.shape["rhs"]), ("tile_0", "tile_1", "tile_2", "rhs")
    )
    placed = (P(TILE, "rhs"), P("rhs"), P(TILE, None), P(None, TILE))
    return jax.shard_map(
        per_device,
        mesh=torus,
        in_specs=placed,
        out_specs=(P(None, TILE), P(None, TILE)),
        check_vma=False,
    )
```

time: 142 us -> 127 us (0.89)
  blocking collectives: 21.6 us -> 48.1 us
  starting transfers between devices: 57.7 us -> 36.1 us
  waiting for transfers between devices: 34.5 us -> 19 us
  other arithmetic: 7.69 us -> 4.41 us
  local copies, waits for them, and re-layouts: 5.92 us -> 4.4 us
    all_to_all x1 -> x3, blocking collectives: 21.6 us -> 48.1 us  [exchanged(): return lax.all_to_all(tiles, axis, 0, 0, tiled=True)]
    all_to_all x3, starting transfers between devices: 34.7 us -> 12.3 us  [exchanged(): return lax.all_to_all(tiles, axis, 0, 0, tiled=True)]
    all_to_all x3, waiting for transfers between devices: 32.6 us -> 16.8 us  [exchanged(): return lax.all_to_all(tiles, axis, 0, 0, tiled=True)]
    reduce_sum x7 -> x6, other arithmetic: 2.28 us -> 0.22 us  [the longest x2 0.11 us: summed(): return exchanged(tiles.astype(BF16), axis).astype(F32).sum(axis=0)]
    slice x7 -> x8, local copies, waits for them, and re-layouts: 2.36 us -> 0.58 us  [the longest x2 0.43 us: per_device(): scalars = received[:, :, piece:].astype(F32)]
  transfers between devices with their start and end apart: 12 -> 12, of which waited for: 6 -> 6; matrix products, arithmetic and copies ran while one was open for 4% -> 8% of each run, Pallas kernels for 0% -> 0%
where the time goes in v2:
time: 127 us; the launch traced here: 126 us
  blocking collectives  48.1 us (38%)
  starting transfers between devices  36.1 us (28%)
  waiting for transfers between devices  19 us (15%)
  matrix products  13.1 us (10%)
  other arithmetic  4.41 us (3%)
  local copies, waits for them, and re-layouts  4.4 us (3%)
    all_to_all x3, blocking collectives, exchanged(): return lax.all_to_all(tiles, axis, 0, 0, tiled=True)  48.1 us
    all_to_all x3, waiting for transfers between devices, exchanged(): return lax.all_to_all(tiles, axis, 0, 0, tiled=True)  16.8 us
    all_to_all x3, starting transfers between devices, exchanged(): return lax.all_to_all(tiles, axis, 0, 0, tiled=True)  12.3 us
    ppermute x3, starting transfers between devices, neighbour_rows(): lax.ppermute(lax.slice_in_dim(block, size - width, size, axis=dim), TILE,...  9.91 us
    dot_general x2, matrix products, projected(): lax.dot_general(weighted, sensitivity, (((1,), (1,)), ((), ())), preferre...  8.48 us
    ppermute x1, starting transfers between devices, per_device(): image = half + lax.ppermute(half, 'rhs', SWAP) + prior  5.12 us
    ppermute x1, starting transfers between devices, per_device(): qw = data + lax.ppermute(data, 'rhs', SWAP) + bent  4.86 us
    dot_general x2, matrix products, observed(): jnp.dot(field.astype(BF16), sensitivity, preferred_element_type=F32)  4.62 us
  transfers between devices with their start and end apart: 12, of which 6 were waited for; matrix products, arithmetic and copies ran while one was open for 8% of the time, Pallas kernels for 0%

profile of v2, /device:TPU:1, one launch (start us, length us, event | category | flops | bytes accessed | tf_op | source)
XLA Modules:
  0.0 126.3 jit_solution(14848340006433851359)
XLA Ops:
  0.6 1.0 copy.35
  1.7 4.4 %collective-permute-start = (f32[64,2,128]{2,1,0:T(2,128)S(1)}, f32[64,2,128]{2,1,0:T(2,128)S(1)}, u32[]{:S(2)}, u32[]{:S(2)}) collective-permute-start(f32[64,2,128]{2,1,0:T(2,128)S(1)} %get-tuple-element.36), channel_id=1, source_target_pairs={{0,2},{2,4},{4,6},{6,8},{8,10},{10,12},{12,14},{14,16},{16,18},{18... | collective-permute-start | bytes 196616 | tf_op jit(solution)/shard_map/ppermute | solution.py:31
  6.1 1.3 %collective-permute-start.1 = (f32[64,2,128]{2,1,0:T(2,128)S(1)}, f32[64,2,128]{2,1,0:T(2,128)S(1)}, u32[]{:S(2)}, u32[]{:S(2)}) collective-permute-start(f32[64,2,128]{2,1,0:T(2,128)S(1)} %get-tuple-element.35), channel_id=1, source_target_pairs={{2,0},{4,2},{6,4},{8,6},{10,8},{12,10},{14,12},{16,14},{18,16},{20... | collective-permute-start | bytes 196616 | tf_op jit(solution)/shard_map/ppermute | solution.py:32
  7.4 3.6 %fusion.17 = bf16[64,2560]{1,0:T(8,128)(2,1)S(1)} fusion(bf16[1024,2560]{1,0:T(8,128)(2,1)} %param.4, f32[64,1024]{1,0:T(8,128)} %param.7), kind=kOutput, calls=%fused_computation.48 | convolution fusion | flops 335609856 | bytes 5832704 | tf_op jit(solution)/shard_map/dot_general | solution.py:88
  11.3 19.0 %all_to_all.30 = bf16[16,8,1280]{2,1,0:T(8,128)(2,1)S(1)} all-to-all(bf16[16,8,1280]{2,1,0:T(8,128)(2,1)S(1)} %bitcast.63), channel_id=1, replica_groups=mesh['tile_0'=4,'tile_1'=4,'tile_2'=8,'rhs'=2] {'tile_0','tile_1'}, dimensions={0} | all-to-all | bytes 655360 | tf_op jit(solution)/shard_map/all_to_all | solution.py:75
  31.0 5.2 %all-to-all-start.1 = ((bf16[8,8,1280]{2,1,0:T(8,128)(2,1)}), bf16[8,8,1280]{2,1,0:T(8,128)(2,1)S(1)}, u32[]{:S(2)}, u32[]{:S(2)}) async-start(bf16[8,8,1280]{2,1,0:T(8,128)(2,1)} %broadcast_in_dim.14), calls=%async_computation.1 | async-start | bytes 327680 | tf_op jit(solution)/shard_map/all_to_all | solution.py:75
  36.2 3.4 %collective-permute-start.3 = (f32[1,128]{1,0:T(1,128)S(1)}, f32[1,128]{1,0:T(1,128)S(1)}, u32[]{:S(2)}, u32[]{:S(2)}) collective-permute-start(f32[1,128]{1,0:T(1,128)S(1)} %get-tuple-element.49), channel_id=1, source_target_pairs={{0,2},{2,4},{4,6},{6,8},{8,10},{10,12},{12,14},{14,16},{16,18},{18... | collective-permute-start | bytes 1544 | tf_op jit(solution)/shard_map/ppermute | solution.py:31
  39.5 1.3 %collective-permute-start.4 = (f32[1,128]{1,0:T(1,128)S(1)}, f32[1,128]{1,0:T(1,128)S(1)}, u32[]{:S(2)}, u32[]{:S(2)}) collective-permute-start(f32[1,128]{1,0:T(1,128)S(1)} %get-tuple-element.50), channel_id=1, source_target_pairs={{2,0},{4,2},{6,4},{8,6},{10,8},{12,10},{14,12},{16,14},{18,16},{20... | collective-permute-start | bytes 1544 | tf_op jit(solution)/shard_map/ppermute | solution.py:32
  41.0 3.6 %all-to-all-done.1 = bf16[8,8,1280]{2,1,0:T(8,128)(2,1)S(1)} async-done(((bf16[8,8,1280]{2,1,0:T(8,128)(2,1)}), bf16[8,8,1280]{2,1,0:T(8,128)(2,1)S(1)}, u32[]{:S(2)}, u32[]{:S(2)}) %all-to-all-start.1) | async-done | bytes 163872 | tf_op jit(solution)/shard_map/all_to_all | solution.py:75
  45.3 3.5 %all-to-all-start.2 = ((bf16[16,8,1280]{2,1,0:T(8,128)(2,1)}), bf16[16,8,1280]{2,1,0:T(8,128)(2,1)S(1)}, u32[]{:S(2)}, u32[]{:S(2)}) async-start(bf16[16,8,1280]{2,1,0:T(8,128)(2,1)} %broadcast_in_dim.15), calls=%async_computation.2 | async-start | bytes 655360 | tf_op jit(solution)/shard_map/all_to_all | solution.py:75
  49.0 7.7 %all-to-all-done.2 = bf16[16,8,1280]{2,1,0:T(8,128)(2,1)S(1)} async-done(((bf16[16,8,1280]{2,1,0:T(8,128)(2,1)}), bf16[16,8,1280]{2,1,0:T(8,128)(2,1)S(1)}, u32[]{:S(2)}, u32[]{:S(2)}) %all-to-all-start.2) | async-done | bytes 327712 | tf_op jit(solution)/shard_map/all_to_all | solution.py:75
  56.7 4.3 %fusion.35 = f32[64,1024]{1,0:T(8,128)S(1)} fusion(bf16[64,2560]{1,0:T(8,128)(2,1)S(1)} %bitcast.61, bf16[1024,2560]{1,0:T(8,128)(2,1)} %param.4), kind=kOutput, calls=%fused_computation.113 | convolution fusion | flops 335544320 | bytes 5832704 | tf_op jit(solution)/shard_map/dot_general | solution.py:94
  61.0 5.1 %collective-permute-start.2 = (f32[64,1024]{1,0:T(8,128)S(1)}, f32[64,1024]{1,0:T(8,128)S(1)}, u32[]{:S(2)}, u32[]{:S(2)}) collective-permute-start(f32[64,1024]{1,0:T(8,128)S(1)} %fusion.35), channel_id=1, source_target_pairs={{0,1},{1,0},{2,3},{3,2},{4,5},{5,4},{6,7},{7,6},{8,9},{9,8},{10,11... | collective-permute-start | bytes 786440 | tf_op jit(solution)/shard_map/ppermute | solution.py:108
  67.5 1.0 convolution_convert_fusion
  69.5 3.5 %all-to-all-start.3 = ((bf16[16,8,1408]{2,1,0:T(8,128)(2,1)}), bf16[16,8,1408]{2,1,0:T(8,128)(2,1)S(1)}, u32[]{:S(2)}, u32[]{:S(2)}) async-start(bf16[16,8,1408]{2,1,0:T(8,128)(2,1)} %pad_maximum_fusion.2), calls=%async_computation.3 | async-start | bytes 720896 | tf_op jit(solution)/shard_map/all_to_all | solution.py:75
  73.2 2.2 %collective-permute-start.5 = (f32[64,2,128]{2,1,0:T(2,128)S(1)}, f32[64,2,128]{2,1,0:T(2,128)S(1)}, u32[]{:S(2)}, u32[]{:S(2)}) collective-permute-start(f32[64,2,128]{2,1,0:T(2,128)S(1)} %get-tuple-element.34), channel_id=1, source_target_pairs={{0,2},{2,4},{4,6},{6,8},{8,10},{10,12},{12,14},{14,16},{16,18},{18... | collective-permute-start | bytes 196616 | tf_op jit(solution)/shard_map/ppermute | solution.py:31
  75.4 1.3 %collective-permute-start.6 = (f32[64,2,128]{2,1,0:T(2,128)S(1)}, f32[64,2,128]{2,1,0:T(2,128)S(1)}, u32[]{:S(2)}, u32[]{:S(2)}) collective-permute-start(f32[64,2,128]{2,1,0:T(2,128)S(1)} %get-tuple-element.33), channel_id=1, source_target_pairs={{2,0},{4,2},{6,4},{8,6},{10,8},{12,10},{14,12},{16,14},{18,16},{20... | collective-permute-start | bytes 196616 | tf_op jit(solution)/shard_map/ppermute | solution.py:32
  76.7 5.6 %all-to-all-done.3 = bf16[16,8,1408]{2,1,0:T(8,128)(2,1)S(1)} async-done(((bf16[16,8,1408]{2,1,0:T(8,128)(2,1)}), bf16[16,8,1408]{2,1,0:T(8,128)(2,1)S(1)}, u32[]{:S(2)}, u32[]{:S(2)}) %all-to-all-start.3) | async-done | bytes 360480 | tf_op jit(solution)/shard_map/all_to_all | solution.py:75
  83.6 13.2 %all_to_all.31 = bf16[8,8,1408]{2,1,0:T(8,128)(2,1)S(1)} all-to-all(bf16[8,8,1408]{2,1,0:T(8,128)(2,1)S(1)} %broadcast_in_dim.18), channel_id=1, replica_groups=mesh['tile_0'=4,'tile_1'=4,'tile_2'=8,'rhs'=2] {'tile_2'}, dimensions={0} | all-to-all | bytes 360448 | tf_op jit(solution)/shard_map/all_to_all | solution.py:75
  97.4 16.0 %all_to_all.32 = bf16[16,8,1408]{2,1,0:T(8,128)(2,1)S(1)} all-to-all(bf16[16,8,1408]{2,1,0:T(8,128)(2,1)S(1)} %broadcast_in_dim.20), channel_id=1, replica_groups=mesh['tile_0'=4,'tile_1'=4,'tile_2'=8,'rhs'=2] {'tile_0','tile_1'}, dimensions={0} | all-to-all | bytes 720896 | tf_op jit(solution)/shard_map/all_to_all | solution.py:75
  114.3 4.9 %collective-permute-start.7 = (f32[64]{0:T(128)S(1)}, f32[64]{0:T(128)S(1)}, u32[]{:S(2)}, u32[]{:S(2)}) collective-permute-start(f32[64]{0:T(128)S(1)} %reshape.166), channel_id=1, source_target_pairs={{0,1},{1,0},{2,3},{3,2},{4,5},{5,4},{6,7},{7,6},{8,9},{9,8},{10,11... | collective-permute-start | bytes 776 | tf_op jit(solution)/shard_map/ppermute | solution.py:134
  119.5 4.2 %fusion.36 = f32[64,1024]{1,0:T(8,128)S(1)} fusion(bf16[64,2560]{1,0:T(8,128)(2,1)S(1)} %bitcast.64, bf16[1024,2560]{1,0:T(8,128)(2,1)} %param.4), kind=kOutput, calls=%fused_computation.114 | convolution fusion | flops 335544320 | bytes 5832704 | tf_op jit(solution)/shard_map/dot_general | solution.py:94
  124.0 1.3 %collective-permute-done.8 = f32[64,1024]{1,0:T(8,128)S(1)} collective-permute-done((f32[64,1024]{1,0:T(8,128)S(1)}, f32[64,1024]{1,0:T(8,128)S(1)}, u32[]{:S(2)}, u32[]{:S(2)}) %collective-permute-start.8) | collective-permute-done | bytes 262176 | tf_op jit(solution)/shard_map/ppermute | solution.py:146
  125.3 0.9 fusion.15
  (86 shorter events, 7.8 us)
Async XLA Ops:
  0.6 35.5 %copy-start.1 = (f32[8,128]{1,0:T(8,128)S(1)}, f32[8,128]{1,0:T(8,128)}, u32[]{:S(2)}) copy-start(f32[8,128]{1,0:T(8,128)} %param.6) | copy-start | bytes 12292
  0.6 40.2 %copy-start.2 = (f32[2560]{0:T(1024)S(1)}, f32[2560]{0:T(1024)}, u32[]{:S(2)}) copy-start(f32[2560]{0:T(1024)} %param.5) | copy-start | bytes 30724
  1.7 9.3 %collective-permute-start = (f32[64,2,128]{2,1,0:T(2,128)S(1)}, f32[64,2,128]{2,1,0:T(2,128)S(1)}, u32[]{:S(2)}, u32[]{:S(2)}) collective-permute-start(f32[64,2,128]{2,1,0:T(2,128)S(1)} %get-tuple-element.36), channel_id=1, source_target_pairs={{0,2},{2,4},{4,6},{6,8},{8,10},{10,12},{12,14},{14,16},{16,18},{18... | collective-permute-start | bytes 196616 | tf_op jit(solution)/shard_map/ppermute | solution.py:31
  6.1 5.2 %collective-permute-start.1 = (f32[64,2,128]{2,1,0:T(2,128)S(1)}, f32[64,2,128]{2,1,0:T(2,128)S(1)}, u32[]{:S(2)}, u32[]{:S(2)}) collective-permute-start(f32[64,2,128]{2,1,0:T(2,128)S(1)} %get-tuple-element.35), channel_id=1, source_target_pairs={{2,0},{4,2},{6,4},{8,6},{10,8},{12,10},{14,12},{16,14},{18,16},{20... | collective-permute-start | bytes 196616 | tf_op jit(solution)/shard_map/ppermute | solution.py:32
  31.0 13.5 %all-to-all-start.1 = ((bf16[8,8,1280]{2,1,0:T(8,128)(2,1)}), bf16[8,8,1280]{2,1,0:T(8,128)(2,1)S(1)}, u32[]{:S(2)}, u32[]{:S(2)}) async-start(bf16[8,8,1280]{2,1,0:T(8,128)(2,1)} %broadcast_in_dim.14), calls=%async_computation.1 | async-start | bytes 327680 | tf_op jit(solution)/shard_map/all_to_all | solution.py:75
  36.2 12.7 %collective-permute-start.3 = (f32[1,128]{1,0:T(1,128)S(1)}, f32[1,128]{1,0:T(1,128)S(1)}, u32[]{:S(2)}, u32[]{:S(2)}) collective-permute-start(f32[1,128]{1,0:T(1,128)S(1)} %get-tuple-element.49), channel_id=1, source_target_pairs={{0,2},{2,4},{4,6},{6,8},{8,10},{10,12},{12,14},{14,16},{16,18},{18... | collective-permute-start | bytes 1544 | tf_op jit(solution)/shard_map/ppermute | solution.py:31
  39.5 9.4 %collective-permute-start.4 = (f32[1,128]{1,0:T(1,128)S(1)}, f32[1,128]{1,0:T(1,128)S(1)}, u32[]{:S(2)}, u32[]{:S(2)}) collective-permute-start(f32[1,128]{1,0:T(1,128)S(1)} %get-tuple-element.50), channel_id=1, source_target_pairs={{2,0},{4,2},{6,4},{8,6},{10,8},{12,10},{14,12},{16,14},{18,16},{20... | collective-permute-start | bytes 1544 | tf_op jit(solution)/shard_map/ppermute | solution.py:32
  45.3 11.4 %all-to-all-start.2 = ((bf16[16,8,1280]{2,1,0:T(8,128)(2,1)}), bf16[16,8,1280]{2,1,0:T(8,128)(2,1)S(1)}, u32[]{:S(2)}, u32[]{:S(2)}) async-start(bf16[16,8,1280]{2,1,0:T(8,128)(2,1)} %broadcast_in_dim.15), calls=%async_computation.2 | async-start | bytes 655360 | tf_op jit(solution)/shard_map/all_to_all | solution.py:75
  48.9 18.5 %copy-start = (f32[64,1024]{1,0:T(8,128)S(1)}, f32[64,1024]{1,0:T(8,128)}, u32[]{:S(2)}) copy-start(f32[64,1024]{1,0:T(8,128)} %param.7) | copy-start | bytes 786436
  56.7 10.8 %slice-start = ((s8[5242880]{0:T(1024)(128)(4,1)}), s8[4194304]{0:T(1024)(128)(4,1)S(1)}, s32[]{:S(2)}) async-start(s8[5242880]{0:T(1024)(128)(4,1)} %bitcast.51), calls=%async_computation.6 | async-start | bytes 8388608
  56.7 10.8 %slice-start.1 = ((s8[5242880]{0:T(1024)(128)(4,1)}), s8[1048576]{0:T(1024)(128)(4,1)S(1)}, s32[]{:S(2)}) async-start(s8[5242880]{0:T(1024)(128)(4,1)} %bitcast.51), calls=%async_computation.7 | async-start | bytes 2097152
  61.0 6.3 %collective-permute-start.2 = (f32[64,1024]{1,0:T(8,128)S(1)}, f32[64,1024]{1,0:T(8,128)S(1)}, u32[]{:S(2)}, u32[]{:S(2)}) collective-permute-start(f32[64,1024]{1,0:T(8,128)S(1)} %fusion.35), channel_id=1, source_target_pairs={{0,1},{1,0},{2,3},{3,2},{4,5},{5,4},{6,7},{7,6},{8,9},{9,8},{10,11... | collective-permute-start | bytes 786440 | tf_op jit(solution)/shard_map/ppermute | solution.py:108
  69.5 12.7 %all-to-all-start.3 = ((bf16[16,8,1408]{2,1,0:T(8,128)(2,1)}), bf16[16,8,1408]{2,1,0:T(8,128)(2,1)S(1)}, u32[]{:S(2)}, u32[]{:S(2)}) async-start(bf16[16,8,1408]{2,1,0:T(8,128)(2,1)} %pad_maximum_fusion.2), calls=%async_computation.3 | async-start | bytes 720896 | tf_op jit(solution)/shard_map/all_to_all | solution.py:75
  73.2 9.1 %collective-permute-start.5 = (f32[64,2,128]{2,1,0:T(2,128)S(1)}, f32[64,2,128]{2,1,0:T(2,128)S(1)}, u32[]{:S(2)}, u32[]{:S(2)}) collective-permute-start(f32[64,2,128]{2,1,0:T(2,128)S(1)} %get-tuple-element.34), channel_id=1, source_target_pairs={{0,2},{2,4},{4,6},{6,8},{8,10},{10,12},{12,14},{14,16},{16,18},{18... | collective-permute-start | bytes 196616 | tf_op jit(solution)/shard_map/ppermute | solution.py:31
  75.4 6.9 %collective-permute-start.6 = (f32[64,2,128]{2,1,0:T(2,128)S(1)}, f32[64,2,128]{2,1,0:T(2,128)S(1)}, u32[]{:S(2)}, u32[]{:S(2)}) collective-permute-start(f32[64,2,128]{2,1,0:T(2,128)S(1)} %get-tuple-element.33), channel_id=1, source_target_pairs={{2,0},{4,2},{6,4},{8,6},{10,8},{12,10},{14,12},{16,14},{18,16},{20... | collective-permute-start | bytes 196616 | tf_op jit(solution)/shard_map/ppermute | solution.py:32
  114.3 9.6 %collective-permute-start.7 = (f32[64]{0:T(128)S(1)}, f32[64]{0:T(128)S(1)}, u32[]{:S(2)}, u32[]{:S(2)}) collective-permute-start(f32[64]{0:T(128)S(1)} %reshape.166), channel_id=1, source_target_pairs={{0,1},{1,0},{2,3},{3,2},{4,5},{5,4},{6,7},{7,6},{8,9},{9,8},{10,11... | collective-permute-start | bytes 776 | tf_op jit(solution)/shard_map/ppermute | solution.py:134
  123.7 1.6 %collective-permute-start.8 = (f32[64,1024]{1,0:T(8,128)S(1)}, f32[64,1024]{1,0:T(8,128)S(1)}, u32[]{:S(2)}, u32[]{:S(2)}) collective-permute-start(f32[64,1024]{1,0:T(8,128)S(1)} %fusion.36), channel_id=1, source_target_pairs={{0,1},{1,0},{2,3},{3,2},{4,5},{5,4},{6,7},{7,6},{8,9},{9,8},{10,11... | collective-permute-start | bytes 786440 | tf_op jit(solution)/shard_map/ppermute | solution.py:146

commit v3 on v2

v3 whole, which is shorter than its diff:
```python
import functools

import jax
import jax.numpy as jnp
from jax import lax
from jax.experimental import pallas as pl
from jax.experimental.pallas import tpu as pltpu
from jax.sharding import Mesh
from jax.sharding import PartitionSpec as P

TILE = ("tile_0", "tile_1", "tile_2")
PLANE = ("tile_0", "tile_1")
LINE = "tile_2"
SWAP = [(0, 1), (1, 0)]
F32, BF16 = jnp.float32, jnp.bfloat16
BLOCK = 8
LANES = 128
SLOTS = 16
DATA, BENT = 3, 4
PRIOR_CORE = 1


def from_neighbours(lower, upper):
    strips, cores = lax.axis_size(TILE), lax.axis_size("rhs")
    up = [(i * cores + PRIOR_CORE, (i + 1) * cores + PRIOR_CORE) for i in range(strips - 1)]
    down = [(target, source) for source, target in up]
    axes = (*TILE, "rhs")
    return lax.ppermute(upper, axes, up), lax.ppermute(lower, axes, down)


def moved(x, lanes):
    return pltpu.roll(x, lanes % LANES, 1)


def lane_of(x):
    return lax.broadcasted_iota(jnp.int32, x.shape, 1)


def packed(x):
    x = jnp.where(lane_of(x) < SLOTS, x, 0.0)
    hi = x.astype(BF16).astype(F32)
    mid = (x - hi).astype(BF16).astype(F32)
    return hi + moved(mid, SLOTS) + moved(x - hi - mid, 2 * SLOTS)


def unpacked(x):
    return x + moved(x, -SLOTS) + moved(x, -2 * SLOTS)


def forward_kernel(with_terms, *refs):
    if with_terms:
        field, load, sensitivity, tiles, total = refs
    else:
        field, sensitivity, tiles, total = refs
    rows, obs = total.shape
    groups = rows // BLOCK
    halves = tiles.shape[0] // groups
    piece = obs // halves
    total[...] = jnp.dot(field[...].astype(BF16), sensitivity[...], preferred_element_type=F32)
    for g in range(groups):
        block = slice(g * BLOCK, (g + 1) * BLOCK)
        if with_terms:
            x, y = load[block, :], field[block, :]
            sums = [jnp.sum(p, axis=1, keepdims=True) for p in (x * x, x * y, y * y)]
            lane = lax.broadcasted_iota(jnp.int32, (BLOCK, LANES), 1)
            line = jnp.zeros((BLOCK, LANES), F32)
            for i, value in enumerate(sums):
                line = jnp.where(lane == i, value, line)
            line = packed(line).astype(BF16)
        for h in range(halves):
            tiles[g * halves + h, :, :piece] = total[block, h * piece : (h + 1) * piece].astype(BF16)
            if with_terms:
                tiles[g * halves + h, :, piece:] = line


def added(tiles, part):
    count = tiles.shape[0]
    found = tiles[0, :, part].astype(F32)
    for i in range(1, count):
        found = found + tiles[i, :, part].astype(F32)
    return found


def sent(tile, part, copies):
    for i in range(copies.shape[0]):
        copies[i, :, part] = tile.astype(BF16)


def middle_kernel(piece, *refs):
    tiles, copies = refs[0], refs[-1]
    sent(added(tiles, slice(0, piece)), slice(0, piece), copies)
    if len(refs) == 3:
        terms = slice(piece, piece + LANES)
        line = unpacked(added(tiles, terms))
        line = jnp.where(lane_of(line) < BENT, line, refs[1][...])
        sent(packed(line), terms, copies)


def raised_kernel(piece, tiles, precision, copies):
    predicted = added(tiles, slice(0, piece))
    raised = precision[...] * predicted
    sent(raised, slice(0, piece), copies)
    if tiles.shape[2] > piece:
        terms = slice(piece, piece + LANES)
        line = unpacked(added(tiles, terms))
        data = jnp.sum(raised * predicted, axis=1, keepdims=True)
        line = jnp.where(lane_of(line) == DATA, data, line)
        sent(packed(line), terms, copies)


def back_kernel(piece, tiles, sensitivity, prior, back, wide, turned):
    params = sensitivity.shape[0]
    rows = back.shape[0]
    groups = rows // BLOCK
    halves = tiles.shape[0] // groups
    wide[rows:, :] = jnp.zeros((wide.shape[0] - rows, wide.shape[1]), F32)
    for g in range(groups):
        for h in range(halves):
            block = tiles[g * halves + h, :, :piece].astype(F32)
            wide[g * BLOCK : (g + 1) * BLOCK, h * piece : (h + 1) * piece] = block
    turned[...] = wide[...].T.astype(BF16)
    depth = 256
    for c in range(params // depth):
        part = slice(c * depth, (c + 1) * depth)
        product = jnp.dot(sensitivity[part, :], turned[...], preferred_element_type=F32)
        back[:, part] = product.T[:rows] + prior[:, part]
    if tiles.shape[2] > piece:
        found = [unpacked(tiles[q, :, piece:].astype(F32)) for q in range(tiles.shape[0])]
        spread = sum(found[1:], found[0])
        for g in range(groups):
            own = found[g * halves : (g + 1) * halves]
            lane = lane_of(spread)
            line = jnp.where(lane == DATA, sum(own[1:], own[0]), own[0])
            line = jnp.where(lane == BENT, moved(spread, -g), line)
            back[g * BLOCK : (g + 1) * BLOCK, params:] = line


def prior_kernel(field, low, high, sides, reaction, prior, bent):
    rows, params = field.shape
    strip_rows = params // LANES
    lane = lax.broadcasted_iota(jnp.int32, (BLOCK, LANES), 1)
    first, last = lane == 0, lane == LANES - 1
    bent_tile = jnp.zeros((BLOCK, LANES), F32)

    def wide(row):
        return jnp.broadcast_to(row, (BLOCK, LANES))

    def applied(above, here, below, weight):
        left = jnp.where(first, 0.0, moved(here, 1))
        right = jnp.where(last, 0.0, moved(here, -1))
        return weight * here - (above + below + left + right)

    weights = [wide(sides[0:1, :] + 4.0)]
    weights += [wide(reaction[i : i + 1, :] + 4.0) for i in range(strip_rows)]
    weights += [wide(sides[1:2, :] + 4.0)]
    has_low, has_high, active = (wide(sides[i : i + 1, :]) for i in (2, 3, 4))
    for g in range(rows // BLOCK):
        block = slice(g * BLOCK, (g + 1) * BLOCK)
        q = [low[block, i * LANES : (i + 1) * LANES] for i in range(2)]
        q += [field[block, i * LANES : (i + 1) * LANES] for i in range(strip_rows)]
        q += [high[block, i * LANES : (i + 1) * LANES] for i in range(2)]
        once = [applied(q[i], q[i + 1], q[i + 2], weights[i]) for i in range(strip_rows + 2)]
        once[0] = once[0] * has_low
        once[-1] = once[-1] * has_high
        squares = once[1] * once[1]
        for i in range(2, strip_rows + 1):
            squares = squares + once[i] * once[i]
        total = jnp.sum(squares, axis=1, keepdims=True)
        bent_tile = jnp.where(lane == BENT + g, total, bent_tile)
        for i in range(strip_rows):
            twice = applied(once[i], once[i + 1], once[i + 2], weights[i + 1])
            prior[block, i * LANES : (i + 1) * LANES] = twice * active
    bent[...] = bent_tile * active


def called(kernel, out_shape, operands, scratch=(), flops=10**6):
    vmem = pl.BlockSpec(memory_space=pltpu.VMEM)
    return pl.pallas_call(
        kernel,
        out_shape=out_shape,
        in_specs=[vmem] * len(operands),
        out_specs=jax.tree.map(lambda _: vmem, out_shape),
        scratch_shapes=list(scratch),
        compiler_params=pltpu.CompilerParams(vmem_limit_bytes=16 * 2**20),
        cost_estimate=pl.CostEstimate(flops=flops, bytes_accessed=10**6, transcendentals=0),
    )(*operands)


def per_device(sensitivity, precision, reaction, load):
    rows, params = load.shape
    _, columns = reaction.shape
    obs = sensitivity.shape[1]
    strip = lax.axis_index(TILE)
    strips = lax.axis_size(TILE)
    plane = lax.axis_size(PLANE)
    line = lax.axis_size(LINE)
    groups = rows // BLOCK
    halves = plane // groups
    piece = obs // halves
    flops = 2 * rows * params * obs
    own_precision = lax.dynamic_slice_in_dim(
        precision[None, :], (lax.axis_index(PLANE) % halves) * piece, piece, axis=1
    )

    active = lax.axis_index("rhs") == PRIOR_CORE
    present = jnp.stack([strip > 0, strip < strips - 1, active]).astype(F32)
    present = jnp.broadcast_to(present[:, None], (3, columns))

    def smoothed(field, low, high, sides):
        return called(
            prior_kernel,
            (jax.ShapeDtypeStruct((rows, params), F32), jax.ShapeDtypeStruct((BLOCK, LANES), F32)),
            (field, low, high, sides, reaction),
        )

    def exchanged(tiles, axis):
        return lax.all_to_all(tiles, axis, 0, 0, tiled=True)

    def observed(operands, width):
        return called(
            functools.partial(forward_kernel, width > piece),
            jax.ShapeDtypeStruct((plane, BLOCK, width), BF16),
            operands,
            [pltpu.VMEM((rows, obs), F32)],
            flops,
        )

    def middle(tiles, *more):
        shape = jax.ShapeDtypeStruct((line, BLOCK, tiles.shape[2]), BF16)
        return called(functools.partial(middle_kernel, piece), shape, (tiles, *more))

    def raised(tiles):
        shape = jax.ShapeDtypeStruct((plane, BLOCK, tiles.shape[2]), BF16)
        return called(functools.partial(raised_kernel, piece), shape, (tiles, own_precision))

    def projected(tiles, prior):
        return called(
            functools.partial(back_kernel, piece),
            jax.ShapeDtypeStruct((rows, params + tiles.shape[2] - piece), F32),
            (tiles, sensitivity, prior),
            [pltpu.VMEM((LANES, obs), F32), pltpu.VMEM((obs, LANES), BF16)],
            flops,
        )

    edge = 2 * columns
    above, below = (
        jnp.concatenate([part, jnp.pad(own, ((0, BLOCK - 1), (0, columns)))], axis=0)
        for part, own in ((load[:, :edge], reaction[:1]), (load[:, params - edge :], reaction[-1:]))
    )
    low, high = from_neighbours(above, below)
    tiles = jnp.dot(load.astype(BF16), sensitivity, preferred_element_type=F32).astype(BF16)
    tiles = tiles.reshape(groups, BLOCK, halves, piece).swapaxes(1, 2).reshape(plane, BLOCK, piece)
    sides = jnp.concatenate([low[rows : rows + 1, :columns], high[rows : rows + 1, :columns], present], axis=0)
    sides = jnp.pad(sides, ((0, BLOCK - sides.shape[0]), (0, 0)))
    prior, _ = smoothed(load, low, high, sides)
    tiles, own_precision, sides, prior = lax.optimization_barrier((tiles, own_precision, sides, prior))
    arrived = exchanged(middle(exchanged(tiles, PLANE)), LINE)
    received = exchanged(raised(arrived), PLANE)
    half = projected(received, prior)
    image = half + lax.ppermute(half, "rhs", SWAP)

    low, high = from_neighbours(image[:, :edge], image[:, params - edge :])
    tiles = observed((image, load, sensitivity), piece + LANES)
    tiles, low, high = lax.optimization_barrier((tiles, low, high))
    arrived = exchanged(tiles, PLANE)
    arrived, low, high = lax.optimization_barrier((arrived, low, high))
    prior, bent = smoothed(image, low, high, sides)
    tiles, prior = lax.optimization_barrier((middle(arrived, bent), prior))
    arrived = exchanged(tiles, LINE)
    received = exchanged(raised(arrived), PLANE)
    half = projected(received, prior)
    other = lax.ppermute(half, "rhs", SWAP)
    bb, bq, qq, data, bent = (half[:, params + i] for i in range(5))
    qw = data + other[:, params + DATA] + (bent + other[:, params + BENT])

    alpha = bb / bq
    fresh = bb - 2.0 * alpha * bq + alpha * alpha * qq
    beta = fresh / bb
    grown = 1.0 + beta
    curved = grown * grown * bq - 2.0 * alpha * grown * qq + alpha * alpha * qw
    second = fresh / curved
    near = (alpha + second * grown)[:, None]
    far = (alpha * second)[:, None]

    twice = half[:, :params] + other[:, :params]
    solution = near * load - far * image
    residual = load - near * image + far * twice
    return (solution, residual)


def solution(mesh):
    torus = Mesh(
        mesh.devices.reshape(4, 4, 8, mesh.shape["rhs"]), ("tile_0", "tile_1", "tile_2", "rhs")
    )
    placed = (P(TILE, "rhs"), P("rhs"), P(TILE, None), P(None, TILE))

    return jax.shard_map(
        per_device,
        mesh=torus,
        in_specs=placed,
        out_specs=(P(None, TILE), P(None, TILE)),
        check_vma=False,
    )
```

time: 127 us -> 112 us (0.88)
  blocking collectives: 48.1 us -> 81.1 us
  starting transfers between devices: 36.1 us -> 11.8 us
  waiting for transfers between devices: 19 us -> 3.36 us
  matrix products: 13.1 us -> 3.73 us
  Pallas kernels: 0 us -> 7 us
  other arithmetic: 4.41 us -> 1.39 us
  local copies, waits for them, and re-layouts: 4.4 us -> 2.6 us
    all_to_all x3 -> x6, blocking collectives: 48.1 us -> 81.1 us  [exchanged(): return lax.all_to_all(tiles, axis, 0, 0, tiled=True)]
    all_to_all x3 -> x0, waiting for transfers between devices: 16.8 us -> none  [exchanged(): return lax.all_to_all(tiles, axis, 0, 0, tiled=True)]
    all_to_all x3 -> x0, starting transfers between devices: 12.3 us -> none  [exchanged(): return lax.all_to_all(tiles, axis, 0, 0, tiled=True)]
    ppermute x9 -> x6, starting transfers between devices: 23.9 us -> 11.8 us  [the longest x4 11.6 us: from_neighbours(): return (lax.ppermute(upper, axes, up), lax.ppermute(lower, axes, down))]
    dot_general x4 -> x1, matrix products: 13.1 us -> 3.73 us  [per_device(): jnp.dot(load.astype(BF16), sensitivity, preferred_element_type=F32)]
    pallas_call x0 -> x9, Pallas kernels: none -> 7 us  [called(): pl.pallas_call(kernel, out_shape=out_shape, in_specs=[vmem] * len(operand...]
    broadcast_in_dim x6 -> x0, local copies, waits for them, and re-layouts: 1.55 us -> none  [the longest x4 1.46 us: to_all(): jnp.broadcast_to(tile.astype(BF16)[None], (lax.axis_size(axis), *tile.sha...]
    ppermute x9 -> x6, waiting for transfers between devices: 2.2 us -> 3.36 us  [the longest x1 1.57 us: per_device(): other = lax.ppermute(half, 'rhs', SWAP)]
  transfers between devices with their start and end apart: 12 -> 6, of which waited for: 6 -> 3; matrix products, arithmetic and copies ran while one was open for 8% -> 4% of each run, Pallas kernels for 0% -> 1%
where the time goes in v3:
time: 112 us
  blocking collectives  81.1 us (72%)
  starting transfers between devices  11.8 us (11%)
  Pallas kernels  7 us (6%)
  matrix products  3.73 us (3%)
  waiting for transfers between devices  3.36 us (3%)
  local copies, waits for them, and re-layouts  2.6 us (2%)
  other arithmetic  1.39 us (1%)
    all_to_all x6, blocking collectives, exchanged(): return lax.all_to_all(tiles, axis, 0, 0, tiled=True)  81.1 us
    ppermute x4, starting transfers between devices, from_neighbours(): return (lax.ppermute(upper, axes, up), lax.ppermute(lower, axes, down))  11.6 us
    pallas_call x9, Pallas kernels, called(): pl.pallas_call(kernel, out_shape=out_shape, in_specs=[vmem] * len(operand...  7 us
    dot_general x1, matrix products, per_device(): jnp.dot(load.astype(BF16), sensitivity, preferred_element_type=F32)  3.73 us
  transfers between devices with their start and end apart: 6, of which 3 were waited for; matrix products, arithmetic and copies ran while one was open for 4% of the time, Pallas kernels for 1%

profile of v3, /device:TPU:1, one launch (start us, length us, event | category | flops | bytes accessed | tf_op | source)
XLA Modules:
  0.0 111.8 jit_solution(4578447923001126980)
XLA Ops:
  0.7 0.8 fusion.9
  1.5 0.9 fusion.8
  2.4 1.3 %collective-permute-start.1 = (f32[72,256]{1,0:T(8,128)S(1)}, f32[72,256]{1,0:T(8,128)S(1)}, u32[]{:S(2)}, u32[]{:S(2)}) collective-permute-start(f32[72,256]{1,0:T(8,128)S(1)} %select_maximum_fusion), channel_id=1, source_target_pairs={{3,1},{5,3},{7,5},{9,7},{11,9},{13,11},{15,13},{17,15},{19,17},{21... | collective-permute-start | bytes 221192 | tf_op jit(solution)/shard_map/ppermute | solution.py:28
  3.7 5.0 %collective-permute-start = (f32[72,256]{1,0:T(8,128)S(1)}, f32[72,256]{1,0:T(8,128)S(1)}, u32[]{:S(2)}, u32[]{:S(2)}) collective-permute-start(f32[72,256]{1,0:T(8,128)S(1)} %select_maximum_fusion.1), channel_id=1, source_target_pairs={{1,3},{3,5},{5,7},{7,9},{9,11},{11,13},{13,15},{15,17},{17,19},{19... | collective-permute-start | bytes 221192 | tf_op jit(solution)/shard_map/ppermute | solution.py:28
  8.7 0.8 dynamic-slice.3
  9.5 3.7 %convolution_convert_fusion = bf16[64,2560]{1,0:T(8,128)(2,1)S(1)} fusion(bf16[1024,2560]{1,0:T(8,128)(2,1)} %sensitivity.3, f32[64,1024]{1,0:T(8,128)} %refs_1_.1), kind=kOutput, calls=%fused_computation | convolution fusion | flops 335773696 | bytes 5832704 | tf_op jit(solution)/shard_map/dot_general | solution.py:251
  13.5 1.3 %shard_map.59 = (f32[64,1024]{1,0:T(8,128)S(1)}, f32[8,128]{1,0:T(8,128)}) custom-call(f32[64,1024]{1,0:T(8,128)S(1)} %copy-done, f32[72,256]{1,0:T(8,128)S(1)} %collective-permute-done.low, f32[72,256]{1,0:T(8,128)S(1)} %collective-permute-done.1.high, f32[8,128]{1,0:T(8,128)S(1)} %pad.13.sides, f32[8,128]{1,0:T(8,128)S(1)} %copy-done.1), custom_call_target="tpu_custom_call" | custom-call | flops 1000000 | bytes 1000000 | tf_op jit(solution)/shard_map/pallas_call | solution.py:178
  14.9 21.2 %all_to_all.30.refs_0_ = bf16[16,8,1280]{2,1,0:T(8,128)(2,1)S(1)} all-to-all(bf16[16,8,1280]{2,1,0:T(8,128)(2,1)S(1)} %bitcast.11), channel_id=1, replica_groups=mesh['tile_0'=4,'tile_1'=4,'tile_2'=8,'rhs'=2] {'tile_0','tile_1'}, dimensions={0} | all-to-all | bytes 655360 | tf_op jit(solution)/shard_map/all_to_all | solution.py:217
  36.1 11.9 %all_to_all.31.tiles = bf16[8,8,1280]{2,1,0:T(8,128)(2,1)S(1)} all-to-all(bf16[8,8,1280]{2,1,0:T(8,128)(2,1)S(1)} %shard_map.60), channel_id=1, replica_groups=mesh['tile_0'=4,'tile_1'=4,'tile_2'=8,'rhs'=2] {'tile_2'}, dimensions={0} | all-to-all | bytes 327680 | tf_op jit(solution)/shard_map/all_to_all | solution.py:217
  48.1 10.5 %all_to_all.32.tiles = bf16[16,8,1280]{2,1,0:T(8,128)(2,1)S(1)} all-to-all(bf16[16,8,1280]{2,1,0:T(8,128)(2,1)S(1)} %shard_map.61), channel_id=1, replica_groups=mesh['tile_0'=4,'tile_1'=4,'tile_2'=8,'rhs'=2] {'tile_0','tile_1'}, dimensions={0} | all-to-all | bytes 655360 | tf_op jit(solution)/shard_map/all_to_all | solution.py:217
  58.6 1.7 %shard_map.62 = f32[64,1024]{1,0:T(8,128)S(1)} custom-call(bf16[16,8,1280]{2,1,0:T(8,128)(2,1)S(1)} %all_to_all.32.tiles, bf16[1024,2560]{1,0:T(8,128)(2,1)S(1)} %bitcast.10, f32[64,1024]{1,0:T(8,128)S(1)} %get-tuple-element.20.prior), custom_call_target="tpu_custom_call" | custom-call | flops 335544320 | bytes 1000000 | tf_op jit(solution)/shard_map/pallas_call | solution.py:178
  60.4 1.5 %collective-permute-done.2 = f32[64,1024]{1,0:T(8,128)S(1)} collective-permute-done((f32[64,1024]{1,0:T(8,128)S(1)}, f32[64,1024]{1,0:T(8,128)S(1)}, u32[]{:S(2)}, u32[]{:S(2)}) %collective-permute-start.2) | collective-permute-done | bytes 262176 | tf_op jit(solution)/shard_map/ppermute | solution.py:260
  62.0 1.3 %collective-permute-start.4 = (f32[64,256]{1,0:T(8,128)S(1)}, f32[64,256]{1,0:T(8,128)S(1)}, u32[]{:S(2)}, u32[]{:S(2)}) collective-permute-start(f32[64,256]{1,0:T(8,128)S(1)} %get-tuple-element.36), channel_id=1, source_target_pairs={{3,1},{5,3},{7,5},{9,7},{11,9},{13,11},{15,13},{17,15},{19,17},{21... | collective-permute-start | bytes 196616 | tf_op jit(solution)/shard_map/ppermute | solution.py:28
  63.3 4.0 %collective-permute-start.3 = (f32[64,256]{1,0:T(8,128)S(1)}, f32[64,256]{1,0:T(8,128)S(1)}, u32[]{:S(2)}, u32[]{:S(2)}) collective-permute-start(f32[64,256]{1,0:T(8,128)S(1)} %get-tuple-element.37), channel_id=1, source_target_pairs={{1,3},{3,5},{5,7},{7,9},{9,11},{11,13},{13,15},{15,17},{17,19},{19... | collective-permute-start | bytes 196616 | tf_op jit(solution)/shard_map/ppermute | solution.py:28
  67.3 1.0 shard_map.63
  68.3 0.3 collective-permute-done.3.low
  68.6 15.8 %all_to_all.33.refs_0_ = bf16[16,8,1408]{2,1,0:T(8,128)(2,1)S(1)} all-to-all(bf16[16,8,1408]{2,1,0:T(8,128)(2,1)S(1)} %shard_map.63), channel_id=1, replica_groups=mesh['tile_0'=4,'tile_1'=4,'tile_2'=8,'rhs'=2] {'tile_0','tile_1'}, dimensions={0} | all-to-all | bytes 720896 | tf_op jit(solution)/shard_map/all_to_all | solution.py:217
  84.4 0.8 shard_map.64
  85.3 10.8 %all_to_all.34.tiles = bf16[8,8,1408]{2,1,0:T(8,128)(2,1)S(1)} all-to-all(bf16[8,8,1408]{2,1,0:T(8,128)(2,1)S(1)} %shard_map.65), channel_id=1, replica_groups=mesh['tile_0'=4,'tile_1'=4,'tile_2'=8,'rhs'=2] {'tile_2'}, dimensions={0} | all-to-all | bytes 360448 | tf_op jit(solution)/shard_map/all_to_all | solution.py:217
  96.3 10.9 %all_to_all.35.tiles = bf16[16,8,1408]{2,1,0:T(8,128)(2,1)S(1)} all-to-all(bf16[16,8,1408]{2,1,0:T(8,128)(2,1)S(1)} %shard_map.66), channel_id=1, replica_groups=mesh['tile_0'=4,'tile_1'=4,'tile_2'=8,'rhs'=2] {'tile_0','tile_1'}, dimensions={0} | all-to-all | bytes 720896 | tf_op jit(solution)/shard_map/all_to_all | solution.py:217
  107.2 1.7 %shard_map.67 = f32[64,1152]{1,0:T(8,128)S(1)} custom-call(bf16[16,8,1408]{2,1,0:T(8,128)(2,1)S(1)} %all_to_all.35.tiles, bf16[1024,2560]{1,0:T(8,128)(2,1)S(1)} %bitcast.10, f32[64,1024]{1,0:T(8,128)S(1)} %get-tuple-element.31.prior), custom_call_target="tpu_custom_call" | custom-call | flops 335544320 | bytes 1000000 | tf_op jit(solution)/shard_map/pallas_call | solution.py:178
  109.0 1.6 %collective-permute-done.5 = f32[64,1152]{1,0:T(8,128)S(1)} collective-permute-done((f32[64,1152]{1,0:T(8,128)S(1)}, f32[64,1152]{1,0:T(8,128)S(1)}, u32[]{:S(2)}, u32[]{:S(2)}) %collective-permute-start.5) | collective-permute-done | bytes 294944 | tf_op jit(solution)/shard_map/ppermute | solution.py:272
  110.6 0.2 add_reduce_fusion
  110.8 1.0 fusion.1
  (29 shorter events, 1.0 us)
Async XLA Ops:
  0.6 12.9 %copy-start.1 = (f32[8,128]{1,0:T(8,128)S(1)}, f32[8,128]{1,0:T(8,128)}, u32[]{:S(2)}) copy-start(f32[8,128]{1,0:T(8,128)} %reaction.3) | copy-start | bytes 12292
  0.6 12.9 %copy-start = (f32[64,1024]{1,0:T(8,128)S(1)}, f32[64,1024]{1,0:T(8,128)}, u32[]{:S(2)}) copy-start(f32[64,1024]{1,0:T(8,128)} %refs_1_.1) | copy-start | bytes 786436
  0.7 57.9 %slice-start = ((s8[5242880]{0:T(1024)(128)(4,1)}), s8[1048576]{0:T(1024)(128)(4,1)S(1)}, s32[]{:S(2)}) async-start(s8[5242880]{0:T(1024)(128)(4,1)} %bitcast.9), calls=%async_computation.6 | async-start | bytes 2097152
  2.4 11.0 %collective-permute-start.1 = (f32[72,256]{1,0:T(8,128)S(1)}, f32[72,256]{1,0:T(8,128)S(1)}, u32[]{:S(2)}, u32[]{:S(2)}) collective-permute-start(f32[72,256]{1,0:T(8,128)S(1)} %select_maximum_fusion), channel_id=1, source_target_pairs={{3,1},{5,3},{7,5},{9,7},{11,9},{13,11},{15,13},{17,15},{19,17},{21... | collective-permute-start | bytes 221192 | tf_op jit(solution)/shard_map/ppermute | solution.py:28
  3.7 9.7 %collective-permute-start = (f32[72,256]{1,0:T(8,128)S(1)}, f32[72,256]{1,0:T(8,128)S(1)}, u32[]{:S(2)}, u32[]{:S(2)}) collective-permute-start(f32[72,256]{1,0:T(8,128)S(1)} %select_maximum_fusion.1), channel_id=1, source_target_pairs={{1,3},{3,5},{5,7},{7,9},{9,11},{11,13},{13,15},{15,17},{17,19},{19... | collective-permute-start | bytes 221192 | tf_op jit(solution)/shard_map/ppermute | solution.py:28
  9.5 49.1 %slice-start.1 = ((s8[5242880]{0:T(1024)(128)(4,1)}), s8[4194304]{0:T(1024)(128)(4,1)S(1)}, s32[]{:S(2)}) async-start(s8[5242880]{0:T(1024)(128)(4,1)} %bitcast.9), calls=%async_computation.7 | async-start | bytes 8388608
  60.3 1.6 %collective-permute-start.2 = (f32[64,1024]{1,0:T(8,128)S(1)}, f32[64,1024]{1,0:T(8,128)S(1)}, u32[]{:S(2)}, u32[]{:S(2)}) collective-permute-start(f32[64,1024]{1,0:T(8,128)S(1)} %shard_map.62), channel_id=1, source_target_pairs={{0,1},{1,0},{2,3},{3,2},{4,5},{5,4},{6,7},{7,6},{8,9},{9,8},{10,11... | collective-permute-start | bytes 786440 | tf_op jit(solution)/shard_map/ppermute | solution.py:260
  62.0 6.3 %collective-permute-start.4 = (f32[64,256]{1,0:T(8,128)S(1)}, f32[64,256]{1,0:T(8,128)S(1)}, u32[]{:S(2)}, u32[]{:S(2)}) collective-permute-start(f32[64,256]{1,0:T(8,128)S(1)} %get-tuple-element.36), channel_id=1, source_target_pairs={{3,1},{5,3},{7,5},{9,7},{11,9},{13,11},{15,13},{17,15},{19,17},{21... | collective-permute-start | bytes 196616 | tf_op jit(solution)/shard_map/ppermute | solution.py:28
  63.3 5.3 %collective-permute-start.3 = (f32[64,256]{1,0:T(8,128)S(1)}, f32[64,256]{1,0:T(8,128)S(1)}, u32[]{:S(2)}, u32[]{:S(2)}) collective-permute-start(f32[64,256]{1,0:T(8,128)S(1)} %get-tuple-element.37), channel_id=1, source_target_pairs={{1,3},{3,5},{5,7},{7,9},{9,11},{11,13},{13,15},{15,17},{17,19},{19... | collective-permute-start | bytes 196616 | tf_op jit(solution)/shard_map/ppermute | solution.py:28
  108.9 1.7 %collective-permute-start.5 = (f32[64,1152]{1,0:T(8,128)S(1)}, f32[64,1152]{1,0:T(8,128)S(1)}, u32[]{:S(2)}, u32[]{:S(2)}) collective-permute-start(f32[64,1152]{1,0:T(8,128)S(1)} %shard_map.67), channel_id=1, source_target_pairs={{0,1},{1,0},{2,3},{3,2},{4,5},{5,4},{6,7},{7,6},{8,9},{9,8},{10,11... | collective-permute-start | bytes 884744 | tf_op jit(solution)/shard_map/ppermute | solution.py:272

commit v4 on v3

--- a/solution.py
+++ b/solution.py
@@ -17,15 +17,16 @@
 LANES = 128
 SLOTS = 16
 DATA, BENT = 3, 4
-PRIOR_CORE = 1
-
-
-def from_neighbours(lower, upper):
+
+
+def links(core, step):
     strips, cores = lax.axis_size(TILE), lax.axis_size("rhs")
-    up = [(i * cores + PRIOR_CORE, (i + 1) * cores + PRIOR_CORE) for i in range(strips - 1)]
-    down = [(target, source) for source, target in up]
-    axes = (*TILE, "rhs")
-    return lax.ppermute(upper, axes, up), lax.ppermute(lower, axes, down)
+    pairs = [(i, i + step) for i in range(strips) if 0 <= i + step < strips]
+    return [(source * cores + core, target * cores + core) for source, target in pairs]
+
+
+def passed(rows, pairs):
+    return lax.ppermute(rows, (*TILE, "rhs"), pairs)
 
 
 def moved(x, lanes):
@@ -94,6 +95,10 @@
         line = unpacked(added(tiles, terms))
         line = jnp.where(lane_of(line) < BENT, line, refs[1][...])
         sent(packed(line), terms, copies)
+
+
+def gather_kernel(tiles, total):
+    total[0] = added(tiles, slice(None))
 
 
 def raised_kernel(piece, tiles, precision, copies):
@@ -135,7 +140,7 @@
             back[g * BLOCK : (g + 1) * BLOCK, params:] = line
 
 
-def prior_kernel(field, low, high, sides, reaction, prior, bent):
+def prior_kernel(field, low, high, low_line, high_line, reaction, prior, *bent):
     rows, params = field.shape
     strip_rows = params // LANES
     lane = lax.broadcasted_iota(jnp.int32, (BLOCK, LANES), 1)
@@ -150,27 +155,33 @@
         right = jnp.where(last, 0.0, moved(here, -1))
         return weight * here - (above + below + left + right)
 
-    weights = [wide(sides[0:1, :] + 4.0)]
-    weights += [wide(reaction[i : i + 1, :] + 4.0) for i in range(strip_rows)]
-    weights += [wide(sides[1:2, :] + 4.0)]
-    has_low, has_high, active = (wide(sides[i : i + 1, :]) for i in (2, 3, 4))
+    strip, upward = lax.axis_index(TILE), lax.axis_index("rhs") == 1
+    has_low = jnp.where(strip > 0, 1.0, 0.0)
+    has_high = jnp.where(strip < lax.axis_size(TILE) - 1, 1.0, 0.0)
+    own_factor = jnp.where(upward, 1.0, 0.0)
+    weights = [low_line[...]]
+    weights += [reaction[i : i + 1, :] for i in range(strip_rows)]
+    weights += [high_line[...]]
+    weights = [wide(row + 4.0) for row in weights]
     for g in range(rows // BLOCK):
         block = slice(g * BLOCK, (g + 1) * BLOCK)
-        q = [low[block, i * LANES : (i + 1) * LANES] for i in range(2)]
-        q += [field[block, i * LANES : (i + 1) * LANES] for i in range(strip_rows)]
-        q += [high[block, i * LANES : (i + 1) * LANES] for i in range(2)]
+        own = [field[block, i * LANES : (i + 1) * LANES] for i in range(strip_rows)]
+        lower, upper = ([e[block, i * LANES : (i + 1) * LANES] for i in range(2)] for e in (low, high))
+        q = [row * own_factor for row in (*lower, *own, *upper)]
         once = [applied(q[i], q[i + 1], q[i + 2], weights[i]) for i in range(strip_rows + 2)]
         once[0] = once[0] * has_low
         once[-1] = once[-1] * has_high
-        squares = once[1] * once[1]
-        for i in range(2, strip_rows + 1):
-            squares = squares + once[i] * once[i]
-        total = jnp.sum(squares, axis=1, keepdims=True)
-        bent_tile = jnp.where(lane == BENT + g, total, bent_tile)
+        if bent:
+            squares = once[1] * once[1]
+            for i in range(2, strip_rows + 1):
+                squares = squares + once[i] * once[i]
+            total = jnp.sum(squares, axis=1, keepdims=True)
+            bent_tile = jnp.where(lane == BENT + g, total, bent_tile)
         for i in range(strip_rows):
             twice = applied(once[i], once[i + 1], once[i + 2], weights[i + 1])
-            prior[block, i * LANES : (i + 1) * LANES] = twice * active
-    bent[...] = bent_tile * active
+            prior[block, i * LANES : (i + 1) * LANES] = twice
+    if bent:
+        bent[0][...] = bent_tile
 
 
 def called(kernel, out_shape, operands, scratch=(), flops=10**6):
@@ -190,8 +201,6 @@
     rows, params = load.shape
     _, columns = reaction.shape
     obs = sensitivity.shape[1]
-    strip = lax.axis_index(TILE)
-    strips = lax.axis_size(TILE)
     plane = lax.axis_size(PLANE)
     line = lax.axis_size(LINE)
     groups = rows // BLOCK
@@ -202,16 +211,11 @@
         precision[None, :], (lax.axis_index(PLANE) % halves) * piece, piece, axis=1
     )
 
-    active = lax.axis_index("rhs") == PRIOR_CORE
-    present = jnp.stack([strip > 0, strip < strips - 1, active]).astype(F32)
-    present = jnp.broadcast_to(present[:, None], (3, columns))
-
-    def smoothed(field, low, high, sides):
-        return called(
-            prior_kernel,
-            (jax.ShapeDtypeStruct((rows, params), F32), jax.ShapeDtypeStruct((BLOCK, LANES), F32)),
-            (field, low, high, sides, reaction),
-        )
+    def smoothed(field, low, high, with_bent):
+        prior = jax.ShapeDtypeStruct((rows, params), F32)
+        bent = jax.ShapeDtypeStruct((BLOCK, LANES), F32)
+        shape = (prior, bent) if with_bent else (prior,)
+        return called(prior_kernel, shape, (field, low, high, low_line, high_line, reaction))
 
     def exchanged(tiles, axis):
         return lax.all_to_all(tiles, axis, 0, 0, tiled=True)
@@ -229,7 +233,7 @@
         shape = jax.ShapeDtypeStruct((line, BLOCK, tiles.shape[2]), BF16)
         return called(functools.partial(middle_kernel, piece), shape, (tiles, *more))
 
-    def raised(tiles):
+    def raised(tiles, own_precision):
         shape = jax.ShapeDtypeStruct((plane, BLOCK, tiles.shape[2]), BF16)
         return called(functools.partial(raised_kernel, piece), shape, (tiles, own_precision))
 
@@ -243,31 +247,35 @@
         )
 
     edge = 2 * columns
-    above, below = (
-        jnp.concatenate([part, jnp.pad(own, ((0, BLOCK - 1), (0, columns)))], axis=0)
-        for part, own in ((load[:, :edge], reaction[:1]), (load[:, params - edge :], reaction[-1:]))
+
+    def with_reaction(part, own):
+        return jnp.concatenate([part, jnp.pad(own, ((0, BLOCK - 1), (0, columns)))], axis=0)
+
+    low = passed(with_reaction(load[:, params - edge :], reaction[-1:]), links(1, 1))
+    high = passed(with_reaction(load[:, :edge], reaction[:1]), links(1, -1))
+    tiles = observed((load, sensitivity), piece)
+    low_line, high_line = (e[rows : rows + 1, :columns] for e in (low, high))
+    (prior,) = smoothed(load, low, high, False)
+    tiles, own_precision, prior, low_line, high_line = lax.optimization_barrier(
+        (tiles, own_precision, prior, low_line, high_line)
     )
-    low, high = from_neighbours(above, below)
-    tiles = jnp.dot(load.astype(BF16), sensitivity, preferred_element_type=F32).astype(BF16)
-    tiles = tiles.reshape(groups, BLOCK, halves, piece).swapaxes(1, 2).reshape(plane, BLOCK, piece)
-    sides = jnp.concatenate([low[rows : rows + 1, :columns], high[rows : rows + 1, :columns], present], axis=0)
-    sides = jnp.pad(sides, ((0, BLOCK - sides.shape[0]), (0, 0)))
-    prior, _ = smoothed(load, low, high, sides)
-    tiles, own_precision, sides, prior = lax.optimization_barrier((tiles, own_precision, sides, prior))
-    arrived = exchanged(middle(exchanged(tiles, PLANE)), LINE)
-    received = exchanged(raised(arrived), PLANE)
+    tiles = middle(exchanged(tiles, PLANE))
+    arrived = exchanged(tiles, LINE)
+    received = exchanged(raised(arrived, own_precision), PLANE)
     half = projected(received, prior)
     image = half + lax.ppermute(half, "rhs", SWAP)
 
-    low, high = from_neighbours(image[:, :edge], image[:, params - edge :])
+    low = passed(image[:, params - edge :], links(1, 1))
+    high = passed(image[:, :edge], links(1, -1))
     tiles = observed((image, load, sensitivity), piece + LANES)
-    tiles, low, high = lax.optimization_barrier((tiles, low, high))
     arrived = exchanged(tiles, PLANE)
+    shape = jax.ShapeDtypeStruct((1, *arrived.shape[1:]), F32)
+    arrived = called(gather_kernel, shape, (arrived,))
     arrived, low, high = lax.optimization_barrier((arrived, low, high))
-    prior, bent = smoothed(image, low, high, sides)
+    prior, bent = smoothed(image, low, high, True)
     tiles, prior = lax.optimization_barrier((middle(arrived, bent), prior))
     arrived = exchanged(tiles, LINE)
-    received = exchanged(raised(arrived), PLANE)
+    received = exchanged(raised(arrived, own_precision), PLANE)
     half = projected(received, prior)
     other = lax.ppermute(half, "rhs", SWAP)
     bb, bq, qq, data, bent = (half[:, params + i] for i in range(5))

time: 112 us -> 112 us (level)
  blocking collectives: 81.1 us -> 71.3 us
  local copies, waits for them, and re-layouts: 2.6 us -> 8.42 us
  matrix products: 3.73 us -> 0 us
  waiting for transfers between devices: 3.36 us -> 7.01 us
  starting transfers between devices: 11.8 us -> 14.8 us
    all_to_all x6 -> x5, blocking collectives: 81.1 us -> 71.3 us  [exchanged(): return lax.all_to_all(tiles, axis, 0, 0, tiled=True)]
    unnamed x8 -> x12, local copies, waits for them, and re-layouts: 0.02 us -> 5.94 us
    all_to_all x0 -> x1, waiting for transfers between devices: none -> 4.05 us  [exchanged(): return lax.all_to_all(tiles, axis, 0, 0, tiled=True)]
    dot_general x1 -> x0, matrix products: 3.73 us -> none  [per_device(): jnp.dot(load.astype(BF16), sensitivity, preferred_element_type=F32)]
    all_to_all x0 -> x1, starting transfers between devices: none -> 3.55 us  [exchanged(): return lax.all_to_all(tiles, axis, 0, 0, tiled=True)]
    pallas_call x9 -> x11, Pallas kernels: 7 us -> 8.09 us  [called(): pl.pallas_call(kernel, out_shape=out_shape, in_specs=[vmem] * len(operand...]
  transfers between devices with their start and end apart: 6 -> 7, of which waited for: 3 -> 3; matrix products, arithmetic and copies ran while one was open for 4% -> 1% of each run, Pallas kernels for 1% -> 1%
where the time goes in v4:
time: 112 us
  blocking collectives  71.3 us (64%)
  starting transfers between devices  14.8 us (13%)
  local copies, waits for them, and re-layouts  8.42 us (8%)
  Pallas kernels  8.09 us (7%)
  waiting for transfers between devices  7.01 us (6%)
  other arithmetic  1.22 us (1%)
    all_to_all x5, blocking collectives, exchanged(): return lax.all_to_all(tiles, axis, 0, 0, tiled=True)  71.3 us
    ppermute x4, starting transfers between devices, passed(): return lax.ppermute(rows, (*TILE, 'rhs'), pairs)  10.9 us
    pallas_call x11, Pallas kernels, called(): pl.pallas_call(kernel, out_shape=out_shape, in_specs=[vmem] * len(operand...  8.09 us
    unnamed x12, local copies, waits for them, and re-layouts  5.94 us
    all_to_all x1, waiting for transfers between devices, exchanged(): return lax.all_to_all(tiles, axis, 0, 0, tiled=True)  4.05 us
    all_to_all x1, starting transfers between devices, exchanged(): return lax.all_to_all(tiles, axis, 0, 0, tiled=True)  3.55 us
  transfers between devices with their start and end apart: 7, of which 3 were waited for; matrix products, arithmetic and copies ran while one was open for 1% of the time, Pallas kernels for 1%

profile of v4, /device:TPU:1, one launch (start us, length us, event | category | flops | bytes accessed | tf_op | source)
XLA Modules:
  0.0 111.7 jit_solution(4377553963660747166)
XLA Ops:
  0.6 0.8 fusion.8
  1.4 0.9 fusion.7
  2.3 4.4 %collective-permute-start = (f32[72,256]{1,0:T(8,128)S(1)}, f32[72,256]{1,0:T(8,128)S(1)}, u32[]{:S(2)}, u32[]{:S(2)}) collective-permute-start(f32[72,256]{1,0:T(8,128)S(1)} %select_maximum_fusion.1), channel_id=1, source_target_pairs={{1,3},{3,5},{5,7},{7,9},{9,11},{11,13},{13,15},{15,17},{17,19},{19... | collective-permute-start | bytes 221192 | tf_op jit(solution)/shard_map/ppermute | solution.py:29
  6.7 1.3 %collective-permute-start.1 = (f32[72,256]{1,0:T(8,128)S(1)}, f32[72,256]{1,0:T(8,128)S(1)}, u32[]{:S(2)}, u32[]{:S(2)}) collective-permute-start(f32[72,256]{1,0:T(8,128)S(1)} %select_maximum_fusion), channel_id=1, source_target_pairs={{3,1},{5,3},{7,5},{9,7},{11,9},{13,11},{15,13},{17,15},{19,17},{21... | collective-permute-start | bytes 221192 | tf_op jit(solution)/shard_map/ppermute | solution.py:29
  8.8 2.5 %copy-done = bf16[1024,2560]{1,0:T(8,128)(2,1)S(1)} copy-done((bf16[1024,2560]{1,0:T(8,128)(2,1)S(1)}, bf16[1024,2560]{1,0:T(8,128)(2,1)}, u32[]{:S(2)}) %copy-start) | copy-done | bytes 5242904
  11.3 0.9 copy-done.3
  12.3 1.0 shard_map.59
  14.0 19.0 %all_to_all.30.refs_0_ = bf16[16,8,1280]{2,1,0:T(8,128)(2,1)S(1)} all-to-all(bf16[16,8,1280]{2,1,0:T(8,128)(2,1)S(1)} %shard_map.59), channel_id=1, replica_groups=mesh['tile_0'=4,'tile_1'=4,'tile_2'=8,'rhs'=2] {'tile_0','tile_1'}, dimensions={0} | all-to-all | bytes 655360 | tf_op jit(solution)/shard_map/all_to_all | solution.py:221
  33.1 13.4 %all_to_all.31.tiles = bf16[8,8,1280]{2,1,0:T(8,128)(2,1)S(1)} all-to-all(bf16[8,8,1280]{2,1,0:T(8,128)(2,1)S(1)} %shard_map.61), channel_id=1, replica_groups=mesh['tile_0'=4,'tile_1'=4,'tile_2'=8,'rhs'=2] {'tile_2'}, dimensions={0} | all-to-all | bytes 327680 | tf_op jit(solution)/shard_map/all_to_all | solution.py:221
  46.5 11.4 %all_to_all.32.tiles = bf16[16,8,1280]{2,1,0:T(8,128)(2,1)S(1)} all-to-all(bf16[16,8,1280]{2,1,0:T(8,128)(2,1)S(1)} %shard_map.62), channel_id=1, replica_groups=mesh['tile_0'=4,'tile_1'=4,'tile_2'=8,'rhs'=2] {'tile_0','tile_1'}, dimensions={0} | all-to-all | bytes 655360 | tf_op jit(solution)/shard_map/all_to_all | solution.py:221
  57.9 1.7 %shard_map.63 = f32[64,1024]{1,0:T(8,128)S(1)} custom-call(bf16[16,8,1280]{2,1,0:T(8,128)(2,1)S(1)} %all_to_all.32.tiles, bf16[1024,2560]{1,0:T(8,128)(2,1)S(1)} %copy-done.1, f32[64,1024]{1,0:T(8,128)S(1)} %shard_map.60.prior), custom_call_target="tpu_custom_call" | custom-call | flops 335544320 | bytes 1000000 | tf_op jit(solution)/shard_map/pallas_call | solution.py:189
  59.7 1.5 %collective-permute-done.2 = f32[64,1024]{1,0:T(8,128)S(1)} collective-permute-done((f32[64,1024]{1,0:T(8,128)S(1)}, f32[64,1024]{1,0:T(8,128)S(1)}, u32[]{:S(2)}, u32[]{:S(2)}) %collective-permute-start.2) | collective-permute-done | bytes 262176 | tf_op jit(solution)/shard_map/ppermute | solution.py:266
  61.2 1.8 %shard_map.64 = bf16[16,8,1408]{2,1,0:T(8,128)(2,1)} custom-call(f32[64,1024]{1,0:T(8,128)S(1)} %add.63.refs_0_.field, f32[64,1024]{1,0:T(8,128)S(1)} %copy-done.4, bf16[1024,2560]{1,0:T(8,128)(2,1)S(1)} %copy-done.1), custom_call_target="tpu_custom_call" | custom-call | flops 335544320 | bytes 1000000 | tf_op jit(solution)/shard_map/pallas_call | solution.py:189
  63.0 3.5 %all-to-all-start.3 = ((bf16[16,8,1408]{2,1,0:T(8,128)(2,1)}), bf16[16,8,1408]{2,1,0:T(8,128)(2,1)S(1)}, u32[]{:S(2)}, u32[]{:S(2)}) async-start(bf16[16,8,1408]{2,1,0:T(8,128)(2,1)} %shard_map.64), calls=%async_computation.3 | async-start | bytes 720896 | tf_op jit(solution)/shard_map/all_to_all | solution.py:221
  66.6 1.3 %collective-permute-start.4 = (f32[64,256]{1,0:T(8,128)S(1)}, f32[64,256]{1,0:T(8,128)S(1)}, u32[]{:S(2)}, u32[]{:S(2)}) collective-permute-start(f32[64,256]{1,0:T(8,128)S(1)} %get-tuple-element.30), channel_id=1, source_target_pairs={{3,1},{5,3},{7,5},{9,7},{11,9},{13,11},{15,13},{17,15},{19,17},{21... | collective-permute-start | bytes 196616 | tf_op jit(solution)/shard_map/ppermute | solution.py:29
  67.9 4.0 %collective-permute-start.3 = (f32[64,256]{1,0:T(8,128)S(1)}, f32[64,256]{1,0:T(8,128)S(1)}, u32[]{:S(2)}, u32[]{:S(2)}) collective-permute-start(f32[64,256]{1,0:T(8,128)S(1)} %get-tuple-element.31), channel_id=1, source_target_pairs={{1,3},{3,5},{5,7},{7,9},{9,11},{11,13},{13,15},{15,17},{17,19},{19... | collective-permute-start | bytes 196616 | tf_op jit(solution)/shard_map/ppermute | solution.py:29
  71.9 4.0 %all-to-all-done.3.tiles = bf16[16,8,1408]{2,1,0:T(8,128)(2,1)S(1)} async-done(((bf16[16,8,1408]{2,1,0:T(8,128)(2,1)}), bf16[16,8,1408]{2,1,0:T(8,128)(2,1)S(1)}, u32[]{:S(2)}, u32[]{:S(2)}) %all-to-all-start.3) | async-done | bytes 360480 | tf_op jit(solution)/shard_map/all_to_all | solution.py:221
  76.0 0.8 shard_map.66
  76.9 10.6 %all_to_all.33.tiles = bf16[8,8,1408]{2,1,0:T(8,128)(2,1)S(1)} all-to-all(bf16[8,8,1408]{2,1,0:T(8,128)(2,1)S(1)} %shard_map.67), channel_id=1, replica_groups=mesh['tile_0'=4,'tile_1'=4,'tile_2'=8,'rhs'=2] {'tile_2'}, dimensions={0} | all-to-all | bytes 360448 | tf_op jit(solution)/shard_map/all_to_all | solution.py:221
  87.7 16.9 %all_to_all.34.tiles = bf16[16,8,1408]{2,1,0:T(8,128)(2,1)S(1)} all-to-all(bf16[16,8,1408]{2,1,0:T(8,128)(2,1)S(1)} %shard_map.68), channel_id=1, replica_groups=mesh['tile_0'=4,'tile_1'=4,'tile_2'=8,'rhs'=2] {'tile_0','tile_1'}, dimensions={0} | all-to-all | bytes 720896 | tf_op jit(solution)/shard_map/all_to_all | solution.py:221
  104.7 2.5 %copy-done.2 = bf16[1024,2560]{1,0:T(8,128)(2,1)S(1)} copy-done((bf16[1024,2560]{1,0:T(8,128)(2,1)S(1)}, bf16[1024,2560]{1,0:T(8,128)(2,1)}, u32[]{:S(2)}) %copy-start.2) | copy-done | bytes 5242904
  107.1 1.7 %shard_map.69 = f32[64,1152]{1,0:T(8,128)S(1)} custom-call(bf16[16,8,1408]{2,1,0:T(8,128)(2,1)S(1)} %all_to_all.34.tiles, bf16[1024,2560]{1,0:T(8,128)(2,1)S(1)} %copy-done.2, f32[64,1024]{1,0:T(8,128)S(1)} %get-tuple-element.25.prior), custom_call_target="tpu_custom_call" | custom-call | flops 335544320 | bytes 1000000 | tf_op jit(solution)/shard_map/pallas_call | solution.py:189
  109.1 1.4 %collective-permute-done.5 = f32[64,1152]{1,0:T(8,128)S(1)} collective-permute-done((f32[64,1152]{1,0:T(8,128)S(1)}, f32[64,1152]{1,0:T(8,128)S(1)}, u32[]{:S(2)}, u32[]{:S(2)}) %collective-permute-start.5) | collective-permute-done | bytes 294944 | tf_op jit(solution)/shard_map/ppermute | solution.py:280
  110.7 1.0 fusion.1
  (30 shorter events, 2.6 us)
Async XLA Ops:
  0.6 12.7 %copy-start.5 = (f32[8,128]{1,0:T(8,128)S(1)}, f32[8,128]{1,0:T(8,128)}, u32[]{:S(2)}) copy-start(f32[8,128]{1,0:T(8,128)} %reaction.3) | copy-start | bytes 12292
  2.3 11.0 %collective-permute-start = (f32[72,256]{1,0:T(8,128)S(1)}, f32[72,256]{1,0:T(8,128)S(1)}, u32[]{:S(2)}, u32[]{:S(2)}) collective-permute-start(f32[72,256]{1,0:T(8,128)S(1)} %select_maximum_fusion.1), channel_id=1, source_target_pairs={{1,3},{3,5},{5,7},{7,9},{9,11},{11,13},{13,15},{15,17},{17,19},{19... | collective-permute-start | bytes 221192 | tf_op jit(solution)/shard_map/ppermute | solution.py:29
  6.7 6.6 %collective-permute-start.1 = (f32[72,256]{1,0:T(8,128)S(1)}, f32[72,256]{1,0:T(8,128)S(1)}, u32[]{:S(2)}, u32[]{:S(2)}) collective-permute-start(f32[72,256]{1,0:T(8,128)S(1)} %select_maximum_fusion), channel_id=1, source_target_pairs={{3,1},{5,3},{7,5},{9,7},{11,9},{13,11},{15,13},{17,15},{19,17},{21... | collective-permute-start | bytes 221192 | tf_op jit(solution)/shard_map/ppermute | solution.py:29
  8.8 2.5 %copy-start = (bf16[1024,2560]{1,0:T(8,128)(2,1)S(1)}, bf16[1024,2560]{1,0:T(8,128)(2,1)}, u32[]{:S(2)}) copy-start(bf16[1024,2560]{1,0:T(8,128)(2,1)} %sensitivity.3) | copy-start | bytes 15728644
  11.3 0.9 copy-start.3
  12.3 45.6 %copy-start.1 = (bf16[1024,2560]{1,0:T(8,128)(2,1)S(1)}, bf16[1024,2560]{1,0:T(8,128)(2,1)}, u32[]{:S(2)}) copy-start(bf16[1024,2560]{1,0:T(8,128)(2,1)} %sensitivity.3) | copy-start | bytes 15728644
  13.3 47.9 %copy-start.4 = (f32[64,1024]{1,0:T(8,128)S(1)}, f32[64,1024]{1,0:T(8,128)}, u32[]{:S(2)}) copy-start(f32[64,1024]{1,0:T(8,128)} %refs_1_.3) | copy-start | bytes 786436
  59.6 1.6 %collective-permute-start.2 = (f32[64,1024]{1,0:T(8,128)S(1)}, f32[64,1024]{1,0:T(8,128)S(1)}, u32[]{:S(2)}, u32[]{:S(2)}) collective-permute-start(f32[64,1024]{1,0:T(8,128)S(1)} %shard_map.63), channel_id=1, source_target_pairs={{0,1},{1,0},{2,3},{3,2},{4,5},{5,4},{6,7},{7,6},{8,9},{9,8},{10,11... | collective-permute-start | bytes 786440 | tf_op jit(solution)/shard_map/ppermute | solution.py:266
  63.0 12.9 %all-to-all-start.3 = ((bf16[16,8,1408]{2,1,0:T(8,128)(2,1)}), bf16[16,8,1408]{2,1,0:T(8,128)(2,1)S(1)}, u32[]{:S(2)}, u32[]{:S(2)}) async-start(bf16[16,8,1408]{2,1,0:T(8,128)(2,1)} %shard_map.64), calls=%async_computation.3 | async-start | bytes 720896 | tf_op jit(solution)/shard_map/all_to_all | solution.py:221
  66.6 9.4 %collective-permute-start.4 = (f32[64,256]{1,0:T(8,128)S(1)}, f32[64,256]{1,0:T(8,128)S(1)}, u32[]{:S(2)}, u32[]{:S(2)}) collective-permute-start(f32[64,256]{1,0:T(8,128)S(1)} %get-tuple-element.30), channel_id=1, source_target_pairs={{3,1},{5,3},{7,5},{9,7},{11,9},{13,11},{15,13},{17,15},{19,17},{21... | collective-permute-start | bytes 196616 | tf_op jit(solution)/shard_map/ppermute | solution.py:29
  67.9 8.1 %collective-permute-start.3 = (f32[64,256]{1,0:T(8,128)S(1)}, f32[64,256]{1,0:T(8,128)S(1)}, u32[]{:S(2)}, u32[]{:S(2)}) collective-permute-start(f32[64,256]{1,0:T(8,128)S(1)} %get-tuple-element.31), channel_id=1, source_target_pairs={{1,3},{3,5},{5,7},{7,9},{9,11},{11,13},{13,15},{15,17},{17,19},{19... | collective-permute-start | bytes 196616 | tf_op jit(solution)/shard_map/ppermute | solution.py:29
  104.7 2.5 %copy-start.2 = (bf16[1024,2560]{1,0:T(8,128)(2,1)S(1)}, bf16[1024,2560]{1,0:T(8,128)(2,1)}, u32[]{:S(2)}) copy-start(bf16[1024,2560]{1,0:T(8,128)(2,1)} %sensitivity.3) | copy-start | bytes 15728644
  108.8 1.7 %collective-permute-start.5 = (f32[64,1152]{1,0:T(8,128)S(1)}, f32[64,1152]{1,0:T(8,128)S(1)}, u32[]{:S(2)}, u32[]{:S(2)}) collective-permute-start(f32[64,1152]{1,0:T(8,128)S(1)} %shard_map.69), channel_id=1, source_target_pairs={{0,1},{1,0},{2,3},{3,2},{4,5},{5,4},{6,7},{7,6},{8,9},{9,8},{10,11... | collective-permute-start | bytes 884744 | tf_op jit(solution)/shard_map/ppermute | solution.py:280

commit v5 on v4

--- a/solution.py
+++ b/solution.py
@@ -97,13 +97,21 @@
         sent(packed(line), terms, copies)
 
 
+def relay_kernel(tiles, out):
+    out[...] = tiles[...]
+
+
 def gather_kernel(tiles, total):
     total[0] = added(tiles, slice(None))
 
 
 def raised_kernel(piece, tiles, precision, copies):
     predicted = added(tiles, slice(0, piece))
-    raised = precision[...] * predicted
+    half = lax.axis_index(PLANE) % (precision.shape[0] // piece)
+    own = precision[:piece]
+    for i in range(1, precision.shape[0] // piece):
+        own = jnp.where(half == i, precision[i * piece : (i + 1) * piece], own)
+    raised = own.reshape(1, piece) * predicted
     sent(raised, slice(0, piece), copies)
     if tiles.shape[2] > piece:
         terms = slice(piece, piece + LANES)
@@ -207,9 +215,6 @@
     halves = plane // groups
     piece = obs // halves
     flops = 2 * rows * params * obs
-    own_precision = lax.dynamic_slice_in_dim(
-        precision[None, :], (lax.axis_index(PLANE) % halves) * piece, piece, axis=1
-    )
 
     def smoothed(field, low, high, with_bent):
         prior = jax.ShapeDtypeStruct((rows, params), F32)
@@ -233,9 +238,9 @@
         shape = jax.ShapeDtypeStruct((line, BLOCK, tiles.shape[2]), BF16)
         return called(functools.partial(middle_kernel, piece), shape, (tiles, *more))
 
-    def raised(tiles, own_precision):
+    def raised(tiles):
         shape = jax.ShapeDtypeStruct((plane, BLOCK, tiles.shape[2]), BF16)
-        return called(functools.partial(raised_kernel, piece), shape, (tiles, own_precision))
+        return called(functools.partial(raised_kernel, piece), shape, (tiles, precision))
 
     def projected(tiles, prior):
         return called(
@@ -251,17 +256,19 @@
     def with_reaction(part, own):
         return jnp.concatenate([part, jnp.pad(own, ((0, BLOCK - 1), (0, columns)))], axis=0)
 
+    tiles = observed((load, sensitivity), piece)
+    tiles, load, reaction = lax.optimization_barrier((tiles, load, reaction))
     low = passed(with_reaction(load[:, params - edge :], reaction[-1:]), links(1, 1))
     high = passed(with_reaction(load[:, :edge], reaction[:1]), links(1, -1))
-    tiles = observed((load, sensitivity), piece)
+    tiles = called(relay_kernel, jax.ShapeDtypeStruct(tiles.shape, BF16), (tiles,))
+    tiles = exchanged(tiles, PLANE)
+    tiles = middle(tiles)
+    tiles, low, high = lax.optimization_barrier((tiles, low, high))
     low_line, high_line = (e[rows : rows + 1, :columns] for e in (low, high))
     (prior,) = smoothed(load, low, high, False)
-    tiles, own_precision, prior, low_line, high_line = lax.optimization_barrier(
-        (tiles, own_precision, prior, low_line, high_line)
-    )
-    tiles = middle(exchanged(tiles, PLANE))
+    tiles, prior, low_line, high_line = lax.optimization_barrier((tiles, prior, low_line, high_line))
     arrived = exchanged(tiles, LINE)
-    received = exchanged(raised(arrived, own_precision), PLANE)
+    received = exchanged(raised(arrived), PLANE)
     half = projected(received, prior)
     image = half + lax.ppermute(half, "rhs", SWAP)
 
@@ -275,7 +282,7 @@
     prior, bent = smoothed(image, low, high, True)
     tiles, prior = lax.optimization_barrier((middle(arrived, bent), prior))
     arrived = exchanged(tiles, LINE)
-    received = exchanged(raised(arrived, own_precision), PLANE)
+    received = exchanged(raised(arrived), PLANE)
     half = projected(received, prior)
     other = lax.ppermute(half, "rhs", SWAP)
     bb, bq, qq, data, bent = (half[:, params + i] for i in range(5))

time: 112 us -> 113 us (level)
  blocking collectives: 71.3 us -> 60.5 us
  starting transfers between devices: 14.8 us -> 22.2 us
  waiting for transfers between devices: 7.01 us -> 10.4 us
    all_to_all x5 -> x4, blocking collectives: 71.3 us -> 60.5 us  [exchanged(): return lax.all_to_all(tiles, axis, 0, 0, tiled=True)]
    all_to_all x1 -> x2, starting transfers between devices: 3.55 us -> 11.1 us  [exchanged(): return lax.all_to_all(tiles, axis, 0, 0, tiled=True)]
    all_to_all x1 -> x2, waiting for transfers between devices: 4.05 us -> 7.44 us  [exchanged(): return lax.all_to_all(tiles, axis, 0, 0, tiled=True)]
    unnamed x12 -> x16, local copies, waits for them, and re-layouts: 5.94 us -> 8.42 us
    slice x2, local copies, waits for them, and re-layouts: 1.67 us -> 0.02 us  [per_device(): high = passed(with_reaction(load[:, :edge], reaction[:1]), links(1, -1))]
    pallas_call x11 -> x12, Pallas kernels: 8.09 us -> 8.86 us  [called(): pl.pallas_call(kernel, out_shape=out_shape, in_specs=[vmem] * len(operand...]
  transfers between devices with their start and end apart: 7 -> 8, of which waited for: 3 -> 5; matrix products, arithmetic and copies ran while one was open for 1% -> 0% of each run, Pallas kernels for 1% -> 0%
where the time goes in v5:
time: 113 us
  blocking collectives  60.5 us (54%)
  starting transfers between devices  22.2 us (20%)
  waiting for transfers between devices  10.4 us (9%)
  Pallas kernels  8.86 us (8%)
  local copies, waits for them, and re-layouts  8.45 us (7%)
  other arithmetic  1.22 us (1%)
    all_to_all x4, blocking collectives, exchanged(): return lax.all_to_all(tiles, axis, 0, 0, tiled=True)  60.5 us
    all_to_all x2, starting transfers between devices, exchanged(): return lax.all_to_all(tiles, axis, 0, 0, tiled=True)  11.1 us
    ppermute x4, starting transfers between devices, passed(): return lax.ppermute(rows, (*TILE, 'rhs'), pairs)  10.1 us
    pallas_call x12, Pallas kernels, called(): pl.pallas_call(kernel, out_shape=out_shape, in_specs=[vmem] * len(operand...  8.86 us
    unnamed x16, local copies, waits for them, and re-layouts  8.42 us
    all_to_all x2, waiting for transfers between devices, exchanged(): return lax.all_to_all(tiles, axis, 0, 0, tiled=True)  7.44 us
  transfers between devices with their start and end apart: 8, of which 5 were waited for; matrix products, arithmetic and copies ran while one was open for 0% of the time, Pallas kernels for 0%

profile of v5, /device:TPU:1, one launch (start us, length us, event | category | flops | bytes accessed | tf_op | source)
XLA Modules:
  0.0 112.6 jit_solution(1897234079809428843)
XLA Ops:
  0.6 2.5 %copy-done = bf16[1024,2560]{1,0:T(8,128)(2,1)S(1)} copy-done((bf16[1024,2560]{1,0:T(8,128)(2,1)S(1)}, bf16[1024,2560]{1,0:T(8,128)(2,1)}, u32[]{:S(2)}) %copy-start) | copy-done | bytes 5242904
  3.1 0.9 copy-done.4
  4.1 1.0 shard_map.59.tiles
  5.8 7.6 %all-to-all-start = ((bf16[16,8,1280]{2,1,0:T(8,128)(2,1)}), bf16[16,8,1280]{2,1,0:T(8,128)(2,1)S(1)}, u32[]{:S(2)}, u32[]{:S(2)}) async-start(bf16[16,8,1280]{2,1,0:T(8,128)(2,1)} %shard_map.60), calls=%async_computation | async-start | bytes 655360 | tf_op jit(solution)/shard_map/all_to_all | solution.py:226
  13.5 3.5 %collective-permute-start = (f32[72,256]{1,0:T(8,128)S(1)}, f32[72,256]{1,0:T(8,128)S(1)}, u32[]{:S(2)}, u32[]{:S(2)}) collective-permute-start(f32[72,256]{1,0:T(8,128)S(1)} %select_maximum_fusion.1), channel_id=1, source_target_pairs={{1,3},{3,5},{5,7},{7,9},{9,11},{11,13},{13,15},{15,17},{17,19},{19... | collective-permute-start | bytes 221192 | tf_op jit(solution)/shard_map/ppermute | solution.py:29
  17.1 1.3 %collective-permute-start.1 = (f32[72,256]{1,0:T(8,128)S(1)}, f32[72,256]{1,0:T(8,128)S(1)}, u32[]{:S(2)}, u32[]{:S(2)}) collective-permute-start(f32[72,256]{1,0:T(8,128)S(1)} %select_maximum_fusion), channel_id=1, source_target_pairs={{3,1},{5,3},{7,5},{9,7},{11,9},{13,11},{15,13},{17,15},{19,17},{21... | collective-permute-start | bytes 221192 | tf_op jit(solution)/shard_map/ppermute | solution.py:29
  18.4 3.6 %all-to-all-done.refs_0_ = bf16[16,8,1280]{2,1,0:T(8,128)(2,1)S(1)} async-done(((bf16[16,8,1280]{2,1,0:T(8,128)(2,1)}), bf16[16,8,1280]{2,1,0:T(8,128)(2,1)S(1)}, u32[]{:S(2)}, u32[]{:S(2)}) %all-to-all-start) | async-done | bytes 327712 | tf_op jit(solution)/shard_map/all_to_all | solution.py:226
  23.3 15.8 %all_to_all.30.tiles = bf16[8,8,1280]{2,1,0:T(8,128)(2,1)S(1)} all-to-all(bf16[8,8,1280]{2,1,0:T(8,128)(2,1)S(1)} %shard_map.61), channel_id=1, replica_groups=mesh['tile_0'=4,'tile_1'=4,'tile_2'=8,'rhs'=2] {'tile_2'}, dimensions={0} | all-to-all | bytes 327680 | tf_op jit(solution)/shard_map/all_to_all | solution.py:226
  39.1 16.9 %all_to_all.31.tiles = bf16[16,8,1280]{2,1,0:T(8,128)(2,1)S(1)} all-to-all(bf16[16,8,1280]{2,1,0:T(8,128)(2,1)S(1)} %shard_map.63), channel_id=1, replica_groups=mesh['tile_0'=4,'tile_1'=4,'tile_2'=8,'rhs'=2] {'tile_0','tile_1'}, dimensions={0} | all-to-all | bytes 655360 | tf_op jit(solution)/shard_map/all_to_all | solution.py:226
  56.0 2.5 %copy-done.1 = bf16[1024,2560]{1,0:T(8,128)(2,1)S(1)} copy-done((bf16[1024,2560]{1,0:T(8,128)(2,1)S(1)}, bf16[1024,2560]{1,0:T(8,128)(2,1)}, u32[]{:S(2)}) %copy-start.1) | copy-done | bytes 5242904
  58.5 1.7 %shard_map.64 = f32[64,1024]{1,0:T(8,128)S(1)} custom-call(bf16[16,8,1280]{2,1,0:T(8,128)(2,1)S(1)} %all_to_all.31.tiles, bf16[1024,2560]{1,0:T(8,128)(2,1)S(1)} %copy-done.1, f32[64,1024]{1,0:T(8,128)S(1)} %shard_map.62.prior), custom_call_target="tpu_custom_call" | custom-call | flops 335544320 | bytes 1000000 | tf_op jit(solution)/shard_map/pallas_call | solution.py:197
  60.7 1.2 %collective-permute-done.2 = f32[64,1024]{1,0:T(8,128)S(1)} collective-permute-done((f32[64,1024]{1,0:T(8,128)S(1)}, f32[64,1024]{1,0:T(8,128)S(1)}, u32[]{:S(2)}, u32[]{:S(2)}) %collective-permute-start.2) | collective-permute-done | bytes 262176 | tf_op jit(solution)/shard_map/ppermute | solution.py:273
  61.9 1.8 %shard_map.65 = bf16[16,8,1408]{2,1,0:T(8,128)(2,1)} custom-call(f32[64,1024]{1,0:T(8,128)S(1)} %add.50.refs_0_.field, f32[64,1024]{1,0:T(8,128)S(1)} %copy-done.5, bf16[1024,2560]{1,0:T(8,128)(2,1)S(1)} %copy-done.2), custom_call_target="tpu_custom_call" | custom-call | flops 335544320 | bytes 1000000 | tf_op jit(solution)/shard_map/pallas_call | solution.py:197
  63.7 3.5 %all-to-all-start.3 = ((bf16[16,8,1408]{2,1,0:T(8,128)(2,1)}), bf16[16,8,1408]{2,1,0:T(8,128)(2,1)S(1)}, u32[]{:S(2)}, u32[]{:S(2)}) async-start(bf16[16,8,1408]{2,1,0:T(8,128)(2,1)} %shard_map.65), calls=%async_computation.3 | async-start | bytes 720896 | tf_op jit(solution)/shard_map/all_to_all | solution.py:226
  67.3 1.3 %collective-permute-start.4 = (f32[64,256]{1,0:T(8,128)S(1)}, f32[64,256]{1,0:T(8,128)S(1)}, u32[]{:S(2)}, u32[]{:S(2)}) collective-permute-start(f32[64,256]{1,0:T(8,128)S(1)} %get-tuple-element.40), channel_id=1, source_target_pairs={{3,1},{5,3},{7,5},{9,7},{11,9},{13,11},{15,13},{17,15},{19,17},{21... | collective-permute-start | bytes 196616 | tf_op jit(solution)/shard_map/ppermute | solution.py:29
  68.6 4.0 %collective-permute-start.3 = (f32[64,256]{1,0:T(8,128)S(1)}, f32[64,256]{1,0:T(8,128)S(1)}, u32[]{:S(2)}, u32[]{:S(2)}) collective-permute-start(f32[64,256]{1,0:T(8,128)S(1)} %get-tuple-element.41), channel_id=1, source_target_pairs={{1,3},{3,5},{5,7},{7,9},{9,11},{11,13},{13,15},{15,17},{17,19},{19... | collective-permute-start | bytes 196616 | tf_op jit(solution)/shard_map/ppermute | solution.py:29
  72.6 3.9 %all-to-all-done.3.tiles = bf16[16,8,1408]{2,1,0:T(8,128)(2,1)S(1)} async-done(((bf16[16,8,1408]{2,1,0:T(8,128)(2,1)}), bf16[16,8,1408]{2,1,0:T(8,128)(2,1)S(1)}, u32[]{:S(2)}, u32[]{:S(2)}) %all-to-all-start.3) | async-done | bytes 360480 | tf_op jit(solution)/shard_map/all_to_all | solution.py:226
  76.5 0.8 shard_map.67
  77.5 10.8 %all_to_all.32.tiles = bf16[8,8,1408]{2,1,0:T(8,128)(2,1)S(1)} all-to-all(bf16[8,8,1408]{2,1,0:T(8,128)(2,1)S(1)} %shard_map.68), channel_id=1, replica_groups=mesh['tile_0'=4,'tile_1'=4,'tile_2'=8,'rhs'=2] {'tile_2'}, dimensions={0} | all-to-all | bytes 360448 | tf_op jit(solution)/shard_map/all_to_all | solution.py:226
  88.5 17.0 %all_to_all.33.tiles = bf16[16,8,1408]{2,1,0:T(8,128)(2,1)S(1)} all-to-all(bf16[16,8,1408]{2,1,0:T(8,128)(2,1)S(1)} %shard_map.69), channel_id=1, replica_groups=mesh['tile_0'=4,'tile_1'=4,'tile_2'=8,'rhs'=2] {'tile_0','tile_1'}, dimensions={0} | all-to-all | bytes 720896 | tf_op jit(solution)/shard_map/all_to_all | solution.py:226
  105.5 2.5 %copy-done.3 = bf16[1024,2560]{1,0:T(8,128)(2,1)S(1)} copy-done((bf16[1024,2560]{1,0:T(8,128)(2,1)S(1)}, bf16[1024,2560]{1,0:T(8,128)(2,1)}, u32[]{:S(2)}) %copy-start.3) | copy-done | bytes 5242904
  108.0 1.7 %shard_map.70 = f32[64,1152]{1,0:T(8,128)S(1)} custom-call(bf16[16,8,1408]{2,1,0:T(8,128)(2,1)S(1)} %all_to_all.33.tiles, bf16[1024,2560]{1,0:T(8,128)(2,1)S(1)} %copy-done.3, f32[64,1024]{1,0:T(8,128)S(1)} %get-tuple-element.35.prior), custom_call_target="tpu_custom_call" | custom-call | flops 335544320 | bytes 1000000 | tf_op jit(solution)/shard_map/pallas_call | solution.py:197
  110.2 1.2 %collective-permute-done.5 = f32[64,1152]{1,0:T(8,128)S(1)} collective-permute-done((f32[64,1152]{1,0:T(8,128)S(1)}, f32[64,1152]{1,0:T(8,128)S(1)}, u32[]{:S(2)}, u32[]{:S(2)}) %collective-permute-start.5) | collective-permute-done | bytes 294944 | tf_op jit(solution)/shard_map/ppermute | solution.py:287
  111.6 1.0 fusion.1
  (34 shorter events, 3.8 us)
Async XLA Ops:
  0.6 2.5 %copy-start = (bf16[1024,2560]{1,0:T(8,128)(2,1)S(1)}, bf16[1024,2560]{1,0:T(8,128)(2,1)}, u32[]{:S(2)}) copy-start(bf16[1024,2560]{1,0:T(8,128)(2,1)} %sensitivity.3) | copy-start | bytes 15728644
  3.1 0.9 copy-start.4
  4.1 9.4 %copy-start.5 = (f32[64,1024]{1,0:T(8,128)S(1)}, f32[64,1024]{1,0:T(8,128)}, u32[]{:S(2)}) copy-start(f32[64,1024]{1,0:T(8,128)} %refs_1_.2) | copy-start | bytes 786436
  4.1 9.4 %copy-start.7 = (f32[8,128]{1,0:T(8,128)S(1)}, f32[8,128]{1,0:T(8,128)}, u32[]{:S(2)}) copy-start(f32[8,128]{1,0:T(8,128)} %reaction.1) | copy-start | bytes 12292
  4.1 35.0 %copy-start.6 = (f32[2560]{0:T(1024)S(1)}, f32[2560]{0:T(1024)}, u32[]{:S(2)}) copy-start(f32[2560]{0:T(1024)} %precision.3) | copy-start | bytes 30724
  5.8 16.1 %all-to-all-start = ((bf16[16,8,1280]{2,1,0:T(8,128)(2,1)}), bf16[16,8,1280]{2,1,0:T(8,128)(2,1)S(1)}, u32[]{:S(2)}, u32[]{:S(2)}) async-start(bf16[16,8,1280]{2,1,0:T(8,128)(2,1)} %shard_map.60), calls=%async_computation | async-start | bytes 655360 | tf_op jit(solution)/shard_map/all_to_all | solution.py:226
  13.5 8.5 %collective-permute-start = (f32[72,256]{1,0:T(8,128)S(1)}, f32[72,256]{1,0:T(8,128)S(1)}, u32[]{:S(2)}, u32[]{:S(2)}) collective-permute-start(f32[72,256]{1,0:T(8,128)S(1)} %select_maximum_fusion.1), channel_id=1, source_target_pairs={{1,3},{3,5},{5,7},{7,9},{9,11},{11,13},{13,15},{15,17},{17,19},{19... | collective-permute-start | bytes 221192 | tf_op jit(solution)/shard_map/ppermute | solution.py:29
  17.1 5.6 %collective-permute-start.1 = (f32[72,256]{1,0:T(8,128)S(1)}, f32[72,256]{1,0:T(8,128)S(1)}, u32[]{:S(2)}, u32[]{:S(2)}) collective-permute-start(f32[72,256]{1,0:T(8,128)S(1)} %select_maximum_fusion), channel_id=1, source_target_pairs={{3,1},{5,3},{7,5},{9,7},{11,9},{13,11},{15,13},{17,15},{19,17},{21... | collective-permute-start | bytes 221192 | tf_op jit(solution)/shard_map/ppermute | solution.py:29
  56.0 2.5 %copy-start.1 = (bf16[1024,2560]{1,0:T(8,128)(2,1)S(1)}, bf16[1024,2560]{1,0:T(8,128)(2,1)}, u32[]{:S(2)}) copy-start(bf16[1024,2560]{1,0:T(8,128)(2,1)} %sensitivity.3) | copy-start | bytes 15728644
  58.5 3.4 %copy-start.2 = (bf16[1024,2560]{1,0:T(8,128)(2,1)S(1)}, bf16[1024,2560]{1,0:T(8,128)(2,1)}, u32[]{:S(2)}) copy-start(bf16[1024,2560]{1,0:T(8,128)(2,1)} %sensitivity.3) | copy-start | bytes 15728644
  60.2 1.6 %collective-permute-start.2 = (f32[64,1024]{1,0:T(8,128)S(1)}, f32[64,1024]{1,0:T(8,128)S(1)}, u32[]{:S(2)}, u32[]{:S(2)}) collective-permute-start(f32[64,1024]{1,0:T(8,128)S(1)} %shard_map.64), channel_id=1, source_target_pairs={{0,1},{1,0},{2,3},{3,2},{4,5},{5,4},{6,7},{7,6},{8,9},{9,8},{10,11... | collective-permute-start | bytes 786440 | tf_op jit(solution)/shard_map/ppermute | solution.py:273
  63.7 12.7 %all-to-all-start.3 = ((bf16[16,8,1408]{2,1,0:T(8,128)(2,1)}), bf16[16,8,1408]{2,1,0:T(8,128)(2,1)S(1)}, u32[]{:S(2)}, u32[]{:S(2)}) async-start(bf16[16,8,1408]{2,1,0:T(8,128)(2,1)} %shard_map.65), calls=%async_computation.3 | async-start | bytes 720896 | tf_op jit(solution)/shard_map/all_to_all | solution.py:226
  67.3 9.2 %collective-permute-start.4 = (f32[64,256]{1,0:T(8,128)S(1)}, f32[64,256]{1,0:T(8,128)S(1)}, u32[]{:S(2)}, u32[]{:S(2)}) collective-permute-start(f32[64,256]{1,0:T(8,128)S(1)} %get-tuple-element.40), channel_id=1, source_target_pairs={{3,1},{5,3},{7,5},{9,7},{11,9},{13,11},{15,13},{17,15},{19,17},{21... | collective-permute-start | bytes 196616 | tf_op jit(solution)/shard_map/ppermute | solution.py:29
  68.6 7.9 %collective-permute-start.3 = (f32[64,256]{1,0:T(8,128)S(1)}, f32[64,256]{1,0:T(8,128)S(1)}, u32[]{:S(2)}, u32[]{:S(2)}) collective-permute-start(f32[64,256]{1,0:T(8,128)S(1)} %get-tuple-element.41), channel_id=1, source_target_pairs={{1,3},{3,5},{5,7},{7,9},{9,11},{11,13},{13,15},{15,17},{17,19},{19... | collective-permute-start | bytes 196616 | tf_op jit(solution)/shard_map/ppermute | solution.py:29
  105.5 2.5 %copy-start.3 = (bf16[1024,2560]{1,0:T(8,128)(2,1)S(1)}, bf16[1024,2560]{1,0:T(8,128)(2,1)}, u32[]{:S(2)}) copy-start(bf16[1024,2560]{1,0:T(8,128)(2,1)} %sensitivity.3) | copy-start | bytes 15728644
  109.7 1.7 %collective-permute-start.5 = (f32[64,1152]{1,0:T(8,128)S(1)}, f32[64,1152]{1,0:T(8,128)S(1)}, u32[]{:S(2)}, u32[]{:S(2)}) collective-permute-start(f32[64,1152]{1,0:T(8,128)S(1)} %shard_map.70), channel_id=1, source_target_pairs={{0,1},{1,0},{2,3},{3,2},{4,5},{5,4},{6,7},{7,6},{8,9},{9,8},{10,11... | collective-permute-start | bytes 884744 | tf_op jit(solution)/shard_map/ppermute | solution.py:287

commit v6 on v5

--- a/solution.py
+++ b/solution.py
@@ -201,7 +201,7 @@
         out_specs=jax.tree.map(lambda _: vmem, out_shape),
         scratch_shapes=list(scratch),
         compiler_params=pltpu.CompilerParams(vmem_limit_bytes=16 * 2**20),
-        cost_estimate=pl.CostEstimate(flops=flops, bytes_accessed=10**6, transcendentals=0),
+        cost_estimate=pl.CostEstimate(flops=flops, bytes_accessed=10**7, transcendentals=0),
     )(*operands)
 
 
@@ -256,7 +256,8 @@
     def with_reaction(part, own):
         return jnp.concatenate([part, jnp.pad(own, ((0, BLOCK - 1), (0, columns)))], axis=0)
 
-    tiles = observed((load, sensitivity), piece)
+    tiles = jnp.dot(load.astype(BF16), sensitivity, preferred_element_type=F32).astype(BF16)
+    tiles = tiles.reshape(groups, BLOCK, halves, piece).swapaxes(1, 2).reshape(plane, BLOCK, piece)
     tiles, load, reaction = lax.optimization_barrier((tiles, load, reaction))
     low = passed(with_reaction(load[:, params - edge :], reaction[-1:]), links(1, 1))
     high = passed(with_reaction(load[:, :edge], reaction[:1]), links(1, -1))

time: 113 us -> 112 us (level)
  matrix products: 0 us -> 3.63 us
  local copies, waits for them, and re-layouts: 8.45 us -> 5.02 us
    dot_general x0 -> x1, matrix products: none -> 3.63 us  [per_device(): jnp.dot(load.astype(BF16), sensitivity, preferred_element_type=F32)]
    unnamed x16 -> x12, local copies, waits for them, and re-layouts: 8.42 us -> 4.99 us
    pallas_call x12 -> x11, Pallas kernels: 8.86 us -> 7.83 us  [called(): pl.pallas_call(kernel, out_shape=out_shape, in_specs=[vmem] * len(operand...]
where the time goes in v6:
time: 112 us
  blocking collectives  60.5 us (54%)
  starting transfers between devices  22.2 us (20%)
  waiting for transfers between devices  10.4 us (9%)
  Pallas kernels  7.83 us (7%)
  local copies, waits for them, and re-layouts  5.02 us (4%)
  matrix products  3.63 us (3%)
  other arithmetic  1.22 us (1%)
    all_to_all x4, blocking collectives, exchanged(): return lax.all_to_all(tiles, axis, 0, 0, tiled=True)  60.5 us
    all_to_all x2, starting transfers between devices, exchanged(): return lax.all_to_all(tiles, axis, 0, 0, tiled=True)  11.1 us
    ppermute x4, starting transfers between devices, passed(): return lax.ppermute(rows, (*TILE, 'rhs'), pairs)  10.1 us
    pallas_call x11, Pallas kernels, called(): pl.pallas_call(kernel, out_shape=out_shape, in_specs=[vmem] * len(operand...  7.83 us
    all_to_all x2, waiting for transfers between devices, exchanged(): return lax.all_to_all(tiles, axis, 0, 0, tiled=True)  7.45 us
    unnamed x12, local copies, waits for them, and re-layouts  4.99 us
    dot_general x1, matrix products, per_device(): jnp.dot(load.astype(BF16), sensitivity, preferred_element_type=F32)  3.63 us
  transfers between devices with their start and end apart: 8, of which 5 were waited for; matrix products, arithmetic and copies ran while one was open for 0% of the time, Pallas kernels for 0%

profile of v6, /device:TPU:1, one launch (start us, length us, event | category | flops | bytes accessed | tf_op | source)
XLA Modules:
  0.0 111.7 jit_solution(2798776007343363405)
XLA Ops:
  0.7 3.6 %convolution_convert_fusion = bf16[64,2560]{1,0:T(8,128)(2,1)S(1)} fusion(bf16[1024,2560]{1,0:T(8,128)(2,1)} %sensitivity.3, f32[64,1024]{1,0:T(8,128)} %refs_1_), kind=kOutput, calls=%fused_computation | convolution fusion | flops 335773696 | bytes 5832704 | tf_op jit(solution)/shard_map/dot_general | solution.py:259
  4.3 0.7 shard_map.59
  5.0 7.6 %all-to-all-start = ((bf16[16,8,1280]{2,1,0:T(8,128)(2,1)}), bf16[16,8,1280]{2,1,0:T(8,128)(2,1)S(1)}, u32[]{:S(2)}, u32[]{:S(2)}) async-start(bf16[16,8,1280]{2,1,0:T(8,128)(2,1)} %shard_map.59), calls=%async_computation | async-start | bytes 655360 | tf_op jit(solution)/shard_map/all_to_all | solution.py:226
  12.7 3.5 %collective-permute-start = (f32[72,256]{1,0:T(8,128)S(1)}, f32[72,256]{1,0:T(8,128)S(1)}, u32[]{:S(2)}, u32[]{:S(2)}) collective-permute-start(f32[72,256]{1,0:T(8,128)S(1)} %select_maximum_fusion.1), channel_id=1, source_target_pairs={{1,3},{3,5},{5,7},{7,9},{9,11},{11,13},{13,15},{15,17},{17,19},{19... | collective-permute-start | bytes 221192 | tf_op jit(solution)/shard_map/ppermute | solution.py:29
  16.3 1.3 %collective-permute-start.1 = (f32[72,256]{1,0:T(8,128)S(1)}, f32[72,256]{1,0:T(8,128)S(1)}, u32[]{:S(2)}, u32[]{:S(2)}) collective-permute-start(f32[72,256]{1,0:T(8,128)S(1)} %select_maximum_fusion), channel_id=1, source_target_pairs={{3,1},{5,3},{7,5},{9,7},{11,9},{13,11},{15,13},{17,15},{19,17},{21... | collective-permute-start | bytes 221192 | tf_op jit(solution)/shard_map/ppermute | solution.py:29
  17.6 3.6 %all-to-all-done.refs_0_ = bf16[16,8,1280]{2,1,0:T(8,128)(2,1)S(1)} async-done(((bf16[16,8,1280]{2,1,0:T(8,128)(2,1)}), bf16[16,8,1280]{2,1,0:T(8,128)(2,1)S(1)}, u32[]{:S(2)}, u32[]{:S(2)}) %all-to-all-start) | async-done | bytes 327712 | tf_op jit(solution)/shard_map/all_to_all | solution.py:226
  21.8 0.7 shard_map.61.prior
  22.5 15.8 %all_to_all.30.tiles = bf16[8,8,1280]{2,1,0:T(8,128)(2,1)S(1)} all-to-all(bf16[8,8,1280]{2,1,0:T(8,128)(2,1)S(1)} %shard_map.60), channel_id=1, replica_groups=mesh['tile_0'=4,'tile_1'=4,'tile_2'=8,'rhs'=2] {'tile_2'}, dimensions={0} | all-to-all | bytes 327680 | tf_op jit(solution)/shard_map/all_to_all | solution.py:226
  38.3 16.9 %all_to_all.31.tiles = bf16[16,8,1280]{2,1,0:T(8,128)(2,1)S(1)} all-to-all(bf16[16,8,1280]{2,1,0:T(8,128)(2,1)S(1)} %shard_map.62), channel_id=1, replica_groups=mesh['tile_0'=4,'tile_1'=4,'tile_2'=8,'rhs'=2] {'tile_0','tile_1'}, dimensions={0} | all-to-all | bytes 655360 | tf_op jit(solution)/shard_map/all_to_all | solution.py:226
  55.2 2.5 %copy-done = bf16[1024,2560]{1,0:T(8,128)(2,1)S(1)} copy-done((bf16[1024,2560]{1,0:T(8,128)(2,1)S(1)}, bf16[1024,2560]{1,0:T(8,128)(2,1)}, u32[]{:S(2)}) %copy-start) | copy-done | bytes 5242904
  57.7 1.7 %shard_map.63 = f32[64,1024]{1,0:T(8,128)S(1)} custom-call(bf16[16,8,1280]{2,1,0:T(8,128)(2,1)S(1)} %all_to_all.31.tiles, bf16[1024,2560]{1,0:T(8,128)(2,1)S(1)} %copy-done, f32[64,1024]{1,0:T(8,128)S(1)} %shard_map.61.prior), custom_call_target="tpu_custom_call" | custom-call | flops 335544320 | bytes 10000000 | tf_op jit(solution)/shard_map/pallas_call | solution.py:197
  59.9 1.2 %collective-permute-done.2 = f32[64,1024]{1,0:T(8,128)S(1)} collective-permute-done((f32[64,1024]{1,0:T(8,128)S(1)}, f32[64,1024]{1,0:T(8,128)S(1)}, u32[]{:S(2)}, u32[]{:S(2)}) %collective-permute-start.2) | collective-permute-done | bytes 262176 | tf_op jit(solution)/shard_map/ppermute | solution.py:274
  61.1 1.8 %shard_map.64 = bf16[16,8,1408]{2,1,0:T(8,128)(2,1)} custom-call(f32[64,1024]{1,0:T(8,128)S(1)} %add.50.refs_0_.field, f32[64,1024]{1,0:T(8,128)S(1)} %copy-done.3, bf16[1024,2560]{1,0:T(8,128)(2,1)S(1)} %copy-done.1), custom_call_target="tpu_custom_call" | custom-call | flops 335544320 | bytes 10000000 | tf_op jit(solution)/shard_map/pallas_call | solution.py:197
  62.9 3.5 %all-to-all-start.3 = ((bf16[16,8,1408]{2,1,0:T(8,128)(2,1)}), bf16[16,8,1408]{2,1,0:T(8,128)(2,1)S(1)}, u32[]{:S(2)}, u32[]{:S(2)}) async-start(bf16[16,8,1408]{2,1,0:T(8,128)(2,1)} %shard_map.64), calls=%async_computation.3 | async-start | bytes 720896 | tf_op jit(solution)/shard_map/all_to_all | solution.py:226
  66.5 1.3 %collective-permute-start.4 = (f32[64,256]{1,0:T(8,128)S(1)}, f32[64,256]{1,0:T(8,128)S(1)}, u32[]{:S(2)}, u32[]{:S(2)}) collective-permute-start(f32[64,256]{1,0:T(8,128)S(1)} %get-tuple-element.40), channel_id=1, source_target_pairs={{3,1},{5,3},{7,5},{9,7},{11,9},{13,11},{15,13},{17,15},{19,17},{21... | collective-permute-start | bytes 196616 | tf_op jit(solution)/shard_map/ppermute | solution.py:29
  67.8 4.0 %collective-permute-start.3 = (f32[64,256]{1,0:T(8,128)S(1)}, f32[64,256]{1,0:T(8,128)S(1)}, u32[]{:S(2)}, u32[]{:S(2)}) collective-permute-start(f32[64,256]{1,0:T(8,128)S(1)} %get-tuple-element.41), channel_id=1, source_target_pairs={{1,3},{3,5},{5,7},{7,9},{9,11},{11,13},{13,15},{15,17},{17,19},{19... | collective-permute-start | bytes 196616 | tf_op jit(solution)/shard_map/ppermute | solution.py:29
  71.8 3.9 %all-to-all-done.3.tiles = bf16[16,8,1408]{2,1,0:T(8,128)(2,1)S(1)} async-done(((bf16[16,8,1408]{2,1,0:T(8,128)(2,1)}), bf16[16,8,1408]{2,1,0:T(8,128)(2,1)S(1)}, u32[]{:S(2)}, u32[]{:S(2)}) %all-to-all-start.3) | async-done | bytes 360480 | tf_op jit(solution)/shard_map/all_to_all | solution.py:226
  75.7 0.8 shard_map.66
  76.6 10.8 %all_to_all.32.tiles = bf16[8,8,1408]{2,1,0:T(8,128)(2,1)S(1)} all-to-all(bf16[8,8,1408]{2,1,0:T(8,128)(2,1)S(1)} %shard_map.67), channel_id=1, replica_groups=mesh['tile_0'=4,'tile_1'=4,'tile_2'=8,'rhs'=2] {'tile_2'}, dimensions={0} | all-to-all | bytes 360448 | tf_op jit(solution)/shard_map/all_to_all | solution.py:226
  87.6 17.0 %all_to_all.33.tiles = bf16[16,8,1408]{2,1,0:T(8,128)(2,1)S(1)} all-to-all(bf16[16,8,1408]{2,1,0:T(8,128)(2,1)S(1)} %shard_map.68), channel_id=1, replica_groups=mesh['tile_0'=4,'tile_1'=4,'tile_2'=8,'rhs'=2] {'tile_0','tile_1'}, dimensions={0} | all-to-all | bytes 720896 | tf_op jit(solution)/shard_map/all_to_all | solution.py:226
  104.7 2.5 %copy-done.2 = bf16[1024,2560]{1,0:T(8,128)(2,1)S(1)} copy-done((bf16[1024,2560]{1,0:T(8,128)(2,1)S(1)}, bf16[1024,2560]{1,0:T(8,128)(2,1)}, u32[]{:S(2)}) %copy-start.2) | copy-done | bytes 5242904
  107.2 1.7 %shard_map.69 = f32[64,1152]{1,0:T(8,128)S(1)} custom-call(bf16[16,8,1408]{2,1,0:T(8,128)(2,1)S(1)} %all_to_all.33.tiles, bf16[1024,2560]{1,0:T(8,128)(2,1)S(1)} %copy-done.2, f32[64,1024]{1,0:T(8,128)S(1)} %get-tuple-element.35.prior), custom_call_target="tpu_custom_call" | custom-call | flops 335544320 | bytes 10000000 | tf_op jit(solution)/shard_map/pallas_call | solution.py:197
  109.3 1.2 %collective-permute-done.5 = f32[64,1152]{1,0:T(8,128)S(1)} collective-permute-done((f32[64,1152]{1,0:T(8,128)S(1)}, f32[64,1152]{1,0:T(8,128)S(1)}, u32[]{:S(2)}, u32[]{:S(2)}) %collective-permute-start.5) | collective-permute-done | bytes 294944 | tf_op jit(solution)/shard_map/ppermute | solution.py:288
  110.8 1.0 fusion.1
  (30 shorter events, 2.4 us)
Async XLA Ops:
  0.6 12.0 %copy-start.3 = (f32[64,1024]{1,0:T(8,128)S(1)}, f32[64,1024]{1,0:T(8,128)}, u32[]{:S(2)}) copy-start(f32[64,1024]{1,0:T(8,128)} %refs_1_) | copy-start | bytes 786436
  0.6 12.0 %copy-start.5 = (f32[8,128]{1,0:T(8,128)S(1)}, f32[8,128]{1,0:T(8,128)}, u32[]{:S(2)}) copy-start(f32[8,128]{1,0:T(8,128)} %reaction.1) | copy-start | bytes 12292
  0.7 37.6 %copy-start.4 = (f32[2560]{0:T(1024)S(1)}, f32[2560]{0:T(1024)}, u32[]{:S(2)}) copy-start(f32[2560]{0:T(1024)} %precision.3) | copy-start | bytes 30724
  5.0 16.1 %all-to-all-start = ((bf16[16,8,1280]{2,1,0:T(8,128)(2,1)}), bf16[16,8,1280]{2,1,0:T(8,128)(2,1)S(1)}, u32[]{:S(2)}, u32[]{:S(2)}) async-start(bf16[16,8,1280]{2,1,0:T(8,128)(2,1)} %shard_map.59), calls=%async_computation | async-start | bytes 655360 | tf_op jit(solution)/shard_map/all_to_all | solution.py:226
  12.7 8.5 %collective-permute-start = (f32[72,256]{1,0:T(8,128)S(1)}, f32[72,256]{1,0:T(8,128)S(1)}, u32[]{:S(2)}, u32[]{:S(2)}) collective-permute-start(f32[72,256]{1,0:T(8,128)S(1)} %select_maximum_fusion.1), channel_id=1, source_target_pairs={{1,3},{3,5},{5,7},{7,9},{9,11},{11,13},{13,15},{15,17},{17,19},{19... | collective-permute-start | bytes 221192 | tf_op jit(solution)/shard_map/ppermute | solution.py:29
  16.3 5.6 %collective-permute-start.1 = (f32[72,256]{1,0:T(8,128)S(1)}, f32[72,256]{1,0:T(8,128)S(1)}, u32[]{:S(2)}, u32[]{:S(2)}) collective-permute-start(f32[72,256]{1,0:T(8,128)S(1)} %select_maximum_fusion), channel_id=1, source_target_pairs={{3,1},{5,3},{7,5},{9,7},{11,9},{13,11},{15,13},{17,15},{19,17},{21... | collective-permute-start | bytes 221192 | tf_op jit(solution)/shard_map/ppermute | solution.py:29
  55.2 2.5 %copy-start = (bf16[1024,2560]{1,0:T(8,128)(2,1)S(1)}, bf16[1024,2560]{1,0:T(8,128)(2,1)}, u32[]{:S(2)}) copy-start(bf16[1024,2560]{1,0:T(8,128)(2,1)} %sensitivity.3) | copy-start | bytes 15728644
  57.7 3.4 %copy-start.1 = (bf16[1024,2560]{1,0:T(8,128)(2,1)S(1)}, bf16[1024,2560]{1,0:T(8,128)(2,1)}, u32[]{:S(2)}) copy-start(bf16[1024,2560]{1,0:T(8,128)(2,1)} %sensitivity.3) | copy-start | bytes 15728644
  59.4 1.6 %collective-permute-start.2 = (f32[64,1024]{1,0:T(8,128)S(1)}, f32[64,1024]{1,0:T(8,128)S(1)}, u32[]{:S(2)}, u32[]{:S(2)}) collective-permute-start(f32[64,1024]{1,0:T(8,128)S(1)} %shard_map.63), channel_id=1, source_target_pairs={{0,1},{1,0},{2,3},{3,2},{4,5},{5,4},{6,7},{7,6},{8,9},{9,8},{10,11... | collective-permute-start | bytes 786440 | tf_op jit(solution)/shard_map/ppermute | solution.py:274
  62.9 12.7 %all-to-all-start.3 = ((bf16[16,8,1408]{2,1,0:T(8,128)(2,1)}), bf16[16,8,1408]{2,1,0:T(8,128)(2,1)S(1)}, u32[]{:S(2)}, u32[]{:S(2)}) async-start(bf16[16,8,1408]{2,1,0:T(8,128)(2,1)} %shard_map.64), calls=%async_computation.3 | async-start | bytes 720896 | tf_op jit(solution)/shard_map/all_to_all | solution.py:226
  66.5 9.2 %collective-permute-start.4 = (f32[64,256]{1,0:T(8,128)S(1)}, f32[64,256]{1,0:T(8,128)S(1)}, u32[]{:S(2)}, u32[]{:S(2)}) collective-permute-start(f32[64,256]{1,0:T(8,128)S(1)} %get-tuple-element.40), channel_id=1, source_target_pairs={{3,1},{5,3},{7,5},{9,7},{11,9},{13,11},{15,13},{17,15},{19,17},{21... | collective-permute-start | bytes 196616 | tf_op jit(solution)/shard_map/ppermute | solution.py:29
  67.8 7.9 %collective-permute-start.3 = (f32[64,256]{1,0:T(8,128)S(1)}, f32[64,256]{1,0:T(8,128)S(1)}, u32[]{:S(2)}, u32[]{:S(2)}) collective-permute-start(f32[64,256]{1,0:T(8,128)S(1)} %get-tuple-element.41), channel_id=1, source_target_pairs={{1,3},{3,5},{5,7},{7,9},{9,11},{11,13},{13,15},{15,17},{17,19},{19... | collective-permute-start | bytes 196616 | tf_op jit(solution)/shard_map/ppermute | solution.py:29
  104.7 2.5 %copy-start.2 = (bf16[1024,2560]{1,0:T(8,128)(2,1)S(1)}, bf16[1024,2560]{1,0:T(8,128)(2,1)}, u32[]{:S(2)}) copy-start(bf16[1024,2560]{1,0:T(8,128)(2,1)} %sensitivity.3) | copy-start | bytes 15728644
  108.9 1.7 %collective-permute-start.5 = (f32[64,1152]{1,0:T(8,128)S(1)}, f32[64,1152]{1,0:T(8,128)S(1)}, u32[]{:S(2)}, u32[]{:S(2)}) collective-permute-start(f32[64,1152]{1,0:T(8,128)S(1)} %shard_map.69), channel_id=1, source_target_pairs={{0,1},{1,0},{2,3},{3,2},{4,5},{5,4},{6,7},{7,6},{8,9},{9,8},{10,11... | collective-permute-start | bytes 884744 | tf_op jit(solution)/shard_map/ppermute | solution.py:288

commit v7 on v6

--- a/solution.py
+++ b/solution.py
@@ -175,7 +175,7 @@
         block = slice(g * BLOCK, (g + 1) * BLOCK)
         own = [field[block, i * LANES : (i + 1) * LANES] for i in range(strip_rows)]
         lower, upper = ([e[block, i * LANES : (i + 1) * LANES] for i in range(2)] for e in (low, high))
-        q = [row * own_factor for row in (*lower, *own, *upper)]
+        q = [*lower, *own, *upper]
         once = [applied(q[i], q[i + 1], q[i + 2], weights[i]) for i in range(strip_rows + 2)]
         once[0] = once[0] * has_low
         once[-1] = once[-1] * has_high
@@ -187,9 +187,9 @@
             bent_tile = jnp.where(lane == BENT + g, total, bent_tile)
         for i in range(strip_rows):
             twice = applied(once[i], once[i + 1], once[i + 2], weights[i + 1])
-            prior[block, i * LANES : (i + 1) * LANES] = twice
+            prior[block, i * LANES : (i + 1) * LANES] = twice * own_factor
     if bent:
-        bent[0][...] = bent_tile
+        bent[0][...] = bent_tile * own_factor
 
 
 def called(kernel, out_shape, operands, scratch=(), flops=10**6):

time: 112 us -> 112 us (level)
  no operation moved by 1% of the time
where the time goes in v7:
time: 112 us; the launch traced here: 111 us
  blocking collectives  60.3 us (54%)
  starting transfers between devices  22 us (20%)
  waiting for transfers between devices  10.6 us (9%)
  Pallas kernels  7.83 us (7%)
  local copies, waits for them, and re-layouts  5.02 us (4%)
  matrix products  3.63 us (3%)
  other arithmetic  1.22 us (1%)
    all_to_all x4, blocking collectives, exchanged(): return lax.all_to_all(tiles, axis, 0, 0, tiled=True)  60.3 us
    all_to_all x2, starting transfers between devices, exchanged(): return lax.all_to_all(tiles, axis, 0, 0, tiled=True)  11.1 us
    ppermute x4, starting transfers between devices, passed(): return lax.ppermute(rows, (*TILE, 'rhs'), pairs)  10.1 us
    pallas_call x11, Pallas kernels, called(): pl.pallas_call(kernel, out_shape=out_shape, in_specs=[vmem] * len(operand...  7.83 us
    all_to_all x2, waiting for transfers between devices, exchanged(): return lax.all_to_all(tiles, axis, 0, 0, tiled=True)  7.45 us
    unnamed x12, local copies, waits for them, and re-layouts  4.99 us
    dot_general x1, matrix products, per_device(): jnp.dot(load.astype(BF16), sensitivity, preferred_element_type=F32)  3.63 us
  transfers between devices with their start and end apart: 8, of which 5 were waited for; matrix products, arithmetic and copies ran while one was open for 0% of the time, Pallas kernels for 0%

profile of v7, /device:TPU:1, one launch (start us, length us, event | category | flops | bytes accessed | tf_op | source)
XLA Modules:
  0.0 111.4 jit_solution(9641346974007238047)
XLA Ops:
  0.7 3.6 %convolution_convert_fusion = bf16[64,2560]{1,0:T(8,128)(2,1)S(1)} fusion(bf16[1024,2560]{1,0:T(8,128)(2,1)} %sensitivity.3, f32[64,1024]{1,0:T(8,128)} %refs_1_), kind=kOutput, calls=%fused_computation | convolution fusion | flops 335773696 | bytes 5832704 | tf_op jit(solution)/shard_map/dot_general | solution.py:259
  4.3 0.7 shard_map.59
  5.0 7.6 %all-to-all-start = ((bf16[16,8,1280]{2,1,0:T(8,128)(2,1)}), bf16[16,8,1280]{2,1,0:T(8,128)(2,1)S(1)}, u32[]{:S(2)}, u32[]{:S(2)}) async-start(bf16[16,8,1280]{2,1,0:T(8,128)(2,1)} %shard_map.59), calls=%async_computation | async-start | bytes 655360 | tf_op jit(solution)/shard_map/all_to_all | solution.py:226
  12.7 3.5 %collective-permute-start = (f32[72,256]{1,0:T(8,128)S(1)}, f32[72,256]{1,0:T(8,128)S(1)}, u32[]{:S(2)}, u32[]{:S(2)}) collective-permute-start(f32[72,256]{1,0:T(8,128)S(1)} %select_maximum_fusion.1), channel_id=1, source_target_pairs={{1,3},{3,5},{5,7},{7,9},{9,11},{11,13},{13,15},{15,17},{17,19},{19... | collective-permute-start | bytes 221192 | tf_op jit(solution)/shard_map/ppermute | solution.py:29
  16.3 1.3 %collective-permute-start.1 = (f32[72,256]{1,0:T(8,128)S(1)}, f32[72,256]{1,0:T(8,128)S(1)}, u32[]{:S(2)}, u32[]{:S(2)}) collective-permute-start(f32[72,256]{1,0:T(8,128)S(1)} %select_maximum_fusion), channel_id=1, source_target_pairs={{3,1},{5,3},{7,5},{9,7},{11,9},{13,11},{15,13},{17,15},{19,17},{21... | collective-permute-start | bytes 221192 | tf_op jit(solution)/shard_map/ppermute | solution.py:29
  17.6 3.6 %all-to-all-done.refs_0_ = bf16[16,8,1280]{2,1,0:T(8,128)(2,1)S(1)} async-done(((bf16[16,8,1280]{2,1,0:T(8,128)(2,1)}), bf16[16,8,1280]{2,1,0:T(8,128)(2,1)S(1)}, u32[]{:S(2)}, u32[]{:S(2)}) %all-to-all-start) | async-done | bytes 327712 | tf_op jit(solution)/shard_map/all_to_all | solution.py:226
  21.8 0.7 shard_map.61.prior
  22.5 15.8 %all_to_all.30.tiles = bf16[8,8,1280]{2,1,0:T(8,128)(2,1)S(1)} all-to-all(bf16[8,8,1280]{2,1,0:T(8,128)(2,1)S(1)} %shard_map.60), channel_id=1, replica_groups=mesh['tile_0'=4,'tile_1'=4,'tile_2'=8,'rhs'=2] {'tile_2'}, dimensions={0} | all-to-all | bytes 327680 | tf_op jit(solution)/shard_map/all_to_all | solution.py:226
  38.3 16.8 %all_to_all.31.tiles = bf16[16,8,1280]{2,1,0:T(8,128)(2,1)S(1)} all-to-all(bf16[16,8,1280]{2,1,0:T(8,128)(2,1)S(1)} %shard_map.62), channel_id=1, replica_groups=mesh['tile_0'=4,'tile_1'=4,'tile_2'=8,'rhs'=2] {'tile_0','tile_1'}, dimensions={0} | all-to-all | bytes 655360 | tf_op jit(solution)/shard_map/all_to_all | solution.py:226
  55.1 2.5 %copy-done = bf16[1024,2560]{1,0:T(8,128)(2,1)S(1)} copy-done((bf16[1024,2560]{1,0:T(8,128)(2,1)S(1)}, bf16[1024,2560]{1,0:T(8,128)(2,1)}, u32[]{:S(2)}) %copy-start) | copy-done | bytes 5242904
  57.6 1.7 %shard_map.63 = f32[64,1024]{1,0:T(8,128)S(1)} custom-call(bf16[16,8,1280]{2,1,0:T(8,128)(2,1)S(1)} %all_to_all.31.tiles, bf16[1024,2560]{1,0:T(8,128)(2,1)S(1)} %copy-done, f32[64,1024]{1,0:T(8,128)S(1)} %shard_map.61.prior), custom_call_target="tpu_custom_call" | custom-call | flops 335544320 | bytes 10000000 | tf_op jit(solution)/shard_map/pallas_call | solution.py:197
  59.8 1.2 %collective-permute-done.2 = f32[64,1024]{1,0:T(8,128)S(1)} collective-permute-done((f32[64,1024]{1,0:T(8,128)S(1)}, f32[64,1024]{1,0:T(8,128)S(1)}, u32[]{:S(2)}, u32[]{:S(2)}) %collective-permute-start.2) | collective-permute-done | bytes 262176 | tf_op jit(solution)/shard_map/ppermute | solution.py:274
  61.0 1.8 %shard_map.64 = bf16[16,8,1408]{2,1,0:T(8,128)(2,1)} custom-call(f32[64,1024]{1,0:T(8,128)S(1)} %add.50.refs_0_.field, f32[64,1024]{1,0:T(8,128)S(1)} %copy-done.3, bf16[1024,2560]{1,0:T(8,128)(2,1)S(1)} %copy-done.1), custom_call_target="tpu_custom_call" | custom-call | flops 335544320 | bytes 10000000 | tf_op jit(solution)/shard_map/pallas_call | solution.py:197
  62.7 3.5 %all-to-all-start.3 = ((bf16[16,8,1408]{2,1,0:T(8,128)(2,1)}), bf16[16,8,1408]{2,1,0:T(8,128)(2,1)S(1)}, u32[]{:S(2)}, u32[]{:S(2)}) async-start(bf16[16,8,1408]{2,1,0:T(8,128)(2,1)} %shard_map.64), calls=%async_computation.3 | async-start | bytes 720896 | tf_op jit(solution)/shard_map/all_to_all | solution.py:226
  66.3 1.3 %collective-permute-start.4 = (f32[64,256]{1,0:T(8,128)S(1)}, f32[64,256]{1,0:T(8,128)S(1)}, u32[]{:S(2)}, u32[]{:S(2)}) collective-permute-start(f32[64,256]{1,0:T(8,128)S(1)} %get-tuple-element.40), channel_id=1, source_target_pairs={{3,1},{5,3},{7,5},{9,7},{11,9},{13,11},{15,13},{17,15},{19,17},{21... | collective-permute-start | bytes 196616 | tf_op jit(solution)/shard_map/ppermute | solution.py:29
  67.6 4.0 %collective-permute-start.3 = (f32[64,256]{1,0:T(8,128)S(1)}, f32[64,256]{1,0:T(8,128)S(1)}, u32[]{:S(2)}, u32[]{:S(2)}) collective-permute-start(f32[64,256]{1,0:T(8,128)S(1)} %get-tuple-element.41), channel_id=1, source_target_pairs={{1,3},{3,5},{5,7},{7,9},{9,11},{11,13},{13,15},{15,17},{17,19},{19... | collective-permute-start | bytes 196616 | tf_op jit(solution)/shard_map/ppermute | solution.py:29
  71.6 3.9 %all-to-all-done.3.tiles = bf16[16,8,1408]{2,1,0:T(8,128)(2,1)S(1)} async-done(((bf16[16,8,1408]{2,1,0:T(8,128)(2,1)}), bf16[16,8,1408]{2,1,0:T(8,128)(2,1)S(1)}, u32[]{:S(2)}, u32[]{:S(2)}) %all-to-all-start.3) | async-done | bytes 360480 | tf_op jit(solution)/shard_map/all_to_all | solution.py:226
  75.5 0.8 shard_map.66
  76.5 11.1 %all_to_all.32.tiles = bf16[8,8,1408]{2,1,0:T(8,128)(2,1)S(1)} all-to-all(bf16[8,8,1408]{2,1,0:T(8,128)(2,1)S(1)} %shard_map.67), channel_id=1, replica_groups=mesh['tile_0'=4,'tile_1'=4,'tile_2'=8,'rhs'=2] {'tile_2'}, dimensions={0} | all-to-all | bytes 360448 | tf_op jit(solution)/shard_map/all_to_all | solution.py:226
  87.8 16.6 %all_to_all.33.tiles = bf16[16,8,1408]{2,1,0:T(8,128)(2,1)S(1)} all-to-all(bf16[16,8,1408]{2,1,0:T(8,128)(2,1)S(1)} %shard_map.68), channel_id=1, replica_groups=mesh['tile_0'=4,'tile_1'=4,'tile_2'=8,'rhs'=2] {'tile_0','tile_1'}, dimensions={0} | all-to-all | bytes 720896 | tf_op jit(solution)/shard_map/all_to_all | solution.py:226
  104.4 2.5 %copy-done.2 = bf16[1024,2560]{1,0:T(8,128)(2,1)S(1)} copy-done((bf16[1024,2560]{1,0:T(8,128)(2,1)S(1)}, bf16[1024,2560]{1,0:T(8,128)(2,1)}, u32[]{:S(2)}) %copy-start.2) | copy-done | bytes 5242904
  106.9 1.7 %shard_map.69 = f32[64,1152]{1,0:T(8,128)S(1)} custom-call(bf16[16,8,1408]{2,1,0:T(8,128)(2,1)S(1)} %all_to_all.33.tiles, bf16[1024,2560]{1,0:T(8,128)(2,1)S(1)} %copy-done.2, f32[64,1024]{1,0:T(8,128)S(1)} %get-tuple-element.35.prior), custom_call_target="tpu_custom_call" | custom-call | flops 335544320 | bytes 10000000 | tf_op jit(solution)/shard_map/pallas_call | solution.py:197
  108.9 1.3 %collective-permute-done.5 = f32[64,1152]{1,0:T(8,128)S(1)} collective-permute-done((f32[64,1152]{1,0:T(8,128)S(1)}, f32[64,1152]{1,0:T(8,128)S(1)}, u32[]{:S(2)}, u32[]{:S(2)}) %collective-permute-start.5) | collective-permute-done | bytes 294944 | tf_op jit(solution)/shard_map/ppermute | solution.py:288
  110.5 1.0 fusion.1
  (30 shorter events, 2.2 us)
Async XLA Ops:
  0.6 12.0 %copy-start.3 = (f32[64,1024]{1,0:T(8,128)S(1)}, f32[64,1024]{1,0:T(8,128)}, u32[]{:S(2)}) copy-start(f32[64,1024]{1,0:T(8,128)} %refs_1_) | copy-start | bytes 786436
  0.6 12.0 %copy-start.5 = (f32[8,128]{1,0:T(8,128)S(1)}, f32[8,128]{1,0:T(8,128)}, u32[]{:S(2)}) copy-start(f32[8,128]{1,0:T(8,128)} %reaction.1) | copy-start | bytes 12292
  0.7 37.6 %copy-start.4 = (f32[2560]{0:T(1024)S(1)}, f32[2560]{0:T(1024)}, u32[]{:S(2)}) copy-start(f32[2560]{0:T(1024)} %precision.3) | copy-start | bytes 30724
  5.0 16.1 %all-to-all-start = ((bf16[16,8,1280]{2,1,0:T(8,128)(2,1)}), bf16[16,8,1280]{2,1,0:T(8,128)(2,1)S(1)}, u32[]{:S(2)}, u32[]{:S(2)}) async-start(bf16[16,8,1280]{2,1,0:T(8,128)(2,1)} %shard_map.59), calls=%async_computation | async-start | bytes 655360 | tf_op jit(solution)/shard_map/all_to_all | solution.py:226
  12.7 8.5 %collective-permute-start = (f32[72,256]{1,0:T(8,128)S(1)}, f32[72,256]{1,0:T(8,128)S(1)}, u32[]{:S(2)}, u32[]{:S(2)}) collective-permute-start(f32[72,256]{1,0:T(8,128)S(1)} %select_maximum_fusion.1), channel_id=1, source_target_pairs={{1,3},{3,5},{5,7},{7,9},{9,11},{11,13},{13,15},{15,17},{17,19},{19... | collective-permute-start | bytes 221192 | tf_op jit(solution)/shard_map/ppermute | solution.py:29
  16.3 5.6 %collective-permute-start.1 = (f32[72,256]{1,0:T(8,128)S(1)}, f32[72,256]{1,0:T(8,128)S(1)}, u32[]{:S(2)}, u32[]{:S(2)}) collective-permute-start(f32[72,256]{1,0:T(8,128)S(1)} %select_maximum_fusion), channel_id=1, source_target_pairs={{3,1},{5,3},{7,5},{9,7},{11,9},{13,11},{15,13},{17,15},{19,17},{21... | collective-permute-start | bytes 221192 | tf_op jit(solution)/shard_map/ppermute | solution.py:29
  55.1 2.5 %copy-start = (bf16[1024,2560]{1,0:T(8,128)(2,1)S(1)}, bf16[1024,2560]{1,0:T(8,128)(2,1)}, u32[]{:S(2)}) copy-start(bf16[1024,2560]{1,0:T(8,128)(2,1)} %sensitivity.3) | copy-start | bytes 15728644
  57.6 3.4 %copy-start.1 = (bf16[1024,2560]{1,0:T(8,128)(2,1)S(1)}, bf16[1024,2560]{1,0:T(8,128)(2,1)}, u32[]{:S(2)}) copy-start(bf16[1024,2560]{1,0:T(8,128)(2,1)} %sensitivity.3) | copy-start | bytes 15728644
  59.3 1.6 %collective-permute-start.2 = (f32[64,1024]{1,0:T(8,128)S(1)}, f32[64,1024]{1,0:T(8,128)S(1)}, u32[]{:S(2)}, u32[]{:S(2)}) collective-permute-start(f32[64,1024]{1,0:T(8,128)S(1)} %shard_map.63), channel_id=1, source_target_pairs={{0,1},{1,0},{2,3},{3,2},{4,5},{5,4},{6,7},{7,6},{8,9},{9,8},{10,11... | collective-permute-start | bytes 786440 | tf_op jit(solution)/shard_map/ppermute | solution.py:274
  62.7 12.7 %all-to-all-start.3 = ((bf16[16,8,1408]{2,1,0:T(8,128)(2,1)}), bf16[16,8,1408]{2,1,0:T(8,128)(2,1)S(1)}, u32[]{:S(2)}, u32[]{:S(2)}) async-start(bf16[16,8,1408]{2,1,0:T(8,128)(2,1)} %shard_map.64), calls=%async_computation.3 | async-start | bytes 720896 | tf_op jit(solution)/shard_map/all_to_all | solution.py:226
  66.3 9.2 %collective-permute-start.4 = (f32[64,256]{1,0:T(8,128)S(1)}, f32[64,256]{1,0:T(8,128)S(1)}, u32[]{:S(2)}, u32[]{:S(2)}) collective-permute-start(f32[64,256]{1,0:T(8,128)S(1)} %get-tuple-element.40), channel_id=1, source_target_pairs={{3,1},{5,3},{7,5},{9,7},{11,9},{13,11},{15,13},{17,15},{19,17},{21... | collective-permute-start | bytes 196616 | tf_op jit(solution)/shard_map/ppermute | solution.py:29
  67.6 7.9 %collective-permute-start.3 = (f32[64,256]{1,0:T(8,128)S(1)}, f32[64,256]{1,0:T(8,128)S(1)}, u32[]{:S(2)}, u32[]{:S(2)}) collective-permute-start(f32[64,256]{1,0:T(8,128)S(1)} %get-tuple-element.41), channel_id=1, source_target_pairs={{1,3},{3,5},{5,7},{7,9},{9,11},{11,13},{13,15},{15,17},{17,19},{19... | collective-permute-start | bytes 196616 | tf_op jit(solution)/shard_map/ppermute | solution.py:29
  104.4 2.5 %copy-start.2 = (bf16[1024,2560]{1,0:T(8,128)(2,1)S(1)}, bf16[1024,2560]{1,0:T(8,128)(2,1)}, u32[]{:S(2)}) copy-start(bf16[1024,2560]{1,0:T(8,128)(2,1)} %sensitivity.3) | copy-start | bytes 15728644
  108.6 1.7 %collective-permute-start.5 = (f32[64,1152]{1,0:T(8,128)S(1)}, f32[64,1152]{1,0:T(8,128)S(1)}, u32[]{:S(2)}, u32[]{:S(2)}) collective-permute-start(f32[64,1152]{1,0:T(8,128)S(1)} %shard_map.69), channel_id=1, source_target_pairs={{0,1},{1,0},{2,3},{3,2},{4,5},{5,4},{6,7},{7,6},{8,9},{9,8},{10,11... | collective-permute-start | bytes 884744 | tf_op jit(solution)/shard_map/ppermute | solution.py:288
